TPU v7x, 32 devices: a whole 2x2x4 slice. The times are simulated.
32 devices in a mesh: rep: 16 (over z, y, core), shard: 2 (over x).
Axes of the slice: x: 2, y: 2, z: 4, core: 2. Of those that a mesh axis runs over, the one named last changes fastest.
Arguments:
- tokens: bfloat16 [32768, 768], P(('rep', 'shard')), may hold values from -6 to 6
- routes: int32 [32768, 2], P(('rep', 'shard')), may hold values from 0 to 3, all different within a row; in each aligned block of 1024 rows (0 to 1023, 1024 to 2047, ...) at most 640 rows name the same one
- pic_block: int32 [32], P(('rep', 'shard')), may hold values from 0 to 3
- norm1_gain: bfloat16 [768], P('shard'), may hold values from 0.099609375 to 1.8984375
- w_query: bfloat16 [768, 768], P('shard'), may hold values from -0.21875 to 0.21875
- w_key: bfloat16 [768, 768], P('shard'), may hold values from -0.21875 to 0.21875
- w_value: bfloat16 [768, 768], P('shard'), may hold values from -0.21875 to 0.21875
- w_out: bfloat16 [768, 768], P('shard'), may hold values from -0.875 to 0.875
- norm2_gain: bfloat16 [768], P('shard'), may hold values from 0.099609375 to 1.8984375
- router: bfloat16 [768, 4], P('shard'), may hold values from -0.21875 to 0.21875
- expert_gate: bfloat16 [4, 768, 2048], P(None, 'shard'), may hold values from -0.21875 to 0.21875
- expert_up: bfloat16 [4, 768, 2048], P(None, 'shard'), may hold values from -0.21875 to 0.21875
- expert_down: bfloat16 [4, 2048, 768], P(None, 'shard'), may hold values from -0.125 to 0.125
- shared_gate: bfloat16 [768, 2048], P('shard'), may hold values from -0.21875 to 0.21875
- shared_up: bfloat16 [768, 2048], P('shard'), may hold values from -0.21875 to 0.21875
- shared_down: bfloat16 [2048, 768], P('shard'), may hold values from -0.125 to 0.125
- cotangent: bfloat16 [32768, 768], P(('rep', 'shard')), may hold values from -6 to 6
Outputs:
- output: bfloat16 [32768, 768], P(('rep', 'shard'))
- input_grad: float32 [32768, 768], P(('rep', 'shard'))
- grad_norm1_gain: float32 [768], P('shard')
- grad_w_query: float32 [768, 768], P('shard')
- grad_w_key: float32 [768, 768], P('shard')
- grad_w_value: float32 [768, 768], P('shard')
- grad_w_out: float32 [768, 768], P('shard')
- grad_norm2_gain: float32 [768], P('shard')
- grad_router: float32 [768, 4], P('shard')
- grad_expert_gate: float32 [4, 768, 2048], P(None, 'shard')
- grad_expert_up: float32 [4, 768, 2048], P(None, 'shard')
- grad_expert_down: float32 [4, 2048, 768], P(None, 'shard')
- grad_shared_gate: float32 [768, 2048], P('shard')
- grad_shared_up: float32 [768, 2048], P('shard')
- grad_shared_down: float32 [2048, 768], P('shard')
Inputs may be any that keep to these rules, and one draw needn't show every extreme that they name: `routes`: each row names two different experts; among the 1024 rows of one device no expert is named by more than 640 rows, and in every draw some expert is named by exactly 640 rows of some device.
All inputs are finite; a program needn't handle non-finite values.
Results may differ from a plain program's by a relative error of at most 0.015.
Values may be sent and summed in bfloat16 or wider, within the bound.
No kernel may reach another device: no remote copies, remote signals or barrier semaphores. Data moves between devices by JAX's collectives and lax.ppermute only.
A program may use at most 768 MiB of HBM per device.

v0:
```python
import jax
import jax.numpy as jnp
from jax import lax
from jax.sharding import PartitionSpec as P

D = 768
HEADS = 12
HEAD_DIM = 64
PIC = 256
CAP = 640


def rotary_tables(length, head_dim):
    halfway = head_dim // 2
    freqs_base = 10000.0 ** (-jnp.arange(halfway, dtype=jnp.float32) / halfway)
    angles = jnp.arange(length, dtype=jnp.float32)[:, None] * freqs_base[None, :]
    cosine_table = jnp.concatenate([jnp.cos(angles), jnp.cos(angles)], axis=1)
    sine_table = jnp.concatenate([jnp.sin(angles), jnp.sin(angles)], axis=1)
    return (cosine_table, sine_table)


def turn_half(values):
    halfway = values.shape[-1] // 2
    return jnp.concatenate([-values[..., halfway:], values[..., :halfway]], axis=-1)


def rotate(values, cosine_table, sine_table):
    return values * cosine_table[:, None, :] + turn_half(values) * sine_table[:, None, :]


def rotate_back(upstream, cosine_table, sine_table):
    return upstream * cosine_table[:, None, :] - turn_half(upstream) * sine_table[:, None, :]


def allowed_mask(row_start, block_rows, length, picture_block):
    position = jnp.arange(length)
    row_ids = row_start + jnp.arange(block_rows)
    in_picture = position // PIC == picture_block
    row_picture = row_ids // PIC == picture_block
    return (position[None, :] <= row_ids[:, None]) | row_picture[:, None] & in_picture[None, :]


def block_scores(query_rows, keys, row_start, length, picture_block):
    block_rows = query_rows.shape[0]
    scores = (
        jnp.einsum("qhd,khd->hqk", query_rows, keys, preferred_element_type=jnp.float32) * 0.125
    )
    allowed = allowed_mask(row_start, block_rows, length, picture_block)
    return jnp.where(allowed[None], scores, -1e30)


def attend_forward(scan_item):
    query, keys, values, picture_block = scan_item
    length = query.shape[0]
    block_rows = min(512, length)
    out_blocks = []
    lse_blocks = []
    for row_start in range(0, length, block_rows):
        scores = block_scores(
            query[row_start : row_start + block_rows], keys, row_start, length, picture_block
        )
        top_score = jnp.max(scores, axis=-1, keepdims=True)
        weights = jnp.exp(scores - top_score)
        totals = jnp.sum(weights, axis=-1, keepdims=True)
        probs = (weights / totals).astype(jnp.bfloat16)
        out_blocks.append(
            jnp.einsum("hqk,khd->qhd", probs, values, preferred_element_type=jnp.float32)
        )
        lse_blocks.append((top_score + jnp.log(totals))[..., 0])
    return (jnp.concatenate(out_blocks, axis=0), jnp.concatenate(lse_blocks, axis=1))


def attend_backward(scan_item):
    query, keys, values, picture_block, log_sums, d_mixed = scan_item
    length = query.shape[0]
    block_rows = min(512, length)
    query_blocks = []
    d_keys = jnp.zeros(keys.shape, jnp.float32)
    d_values = jnp.zeros(values.shape, jnp.float32)
    for row_start in range(0, length, block_rows):
        rows_query = query[row_start : row_start + block_rows]
        rows_grad = d_mixed[row_start : row_start + block_rows]
        scores = block_scores(rows_query, keys, row_start, length, picture_block)
        probs = jnp.exp(scores - log_sums[:, row_start : row_start + block_rows, None])
        d_probs = jnp.einsum("qhd,khd->hqk", rows_grad, values, preferred_element_type=jnp.float32)
        centre = jnp.sum(probs * d_probs, axis=-1, keepdims=True)
        d_scores = (probs * (d_probs - centre) * 0.125).astype(jnp.bfloat16)
        query_blocks.append(
            jnp.einsum("hqk,khd->qhd", d_scores, keys, preferred_element_type=jnp.float32)
        )
        d_keys = d_keys + jnp.einsum(
            "hqk,qhd->khd", d_scores, rows_query, preferred_element_type=jnp.float32
        )
        d_values = d_values + jnp.einsum(
            "hqk,qhd->khd",
            probs.astype(jnp.bfloat16),
            rows_grad,
            preferred_element_type=jnp.float32,
        )
    return (jnp.concatenate(query_blocks, axis=0), d_keys, d_values)


def normalize(values, gain_vec):
    inverse = lax.rsqrt(jnp.mean(values * values, axis=-1, keepdims=True) + 1e-05)
    return (values * inverse * gain_vec, inverse)


def normalize_back(upstream, values, inverse, gain_vec):
    scaled = values * inverse
    gain_grad = jnp.sum(upstream * scaled, axis=0)
    inner_term = upstream * gain_vec
    back_grad = inverse * (
        inner_term - scaled * jnp.mean(inner_term * scaled, axis=-1, keepdims=True)
    )
    return (back_grad, gain_grad)


def swiglu_back(upstream, gate_pre, up_pre):
    squashed = jax.nn.sigmoid(gate_pre)
    activated = gate_pre * squashed
    d_up = (upstream * activated).astype(jnp.bfloat16)
    d_gate = (upstream * up_pre * squashed * (1.0 + gate_pre * (1.0 - squashed))).astype(
        jnp.bfloat16
    )
    return (d_gate, d_up)


def weight_grad(left, right):
    return jnp.einsum("tk,tn->kn", left, right, preferred_element_type=jnp.float32)


def on_device(
    tokens,
    routes,
    pic_block,
    norm1_gain,
    w_query,
    w_key,
    w_value,
    w_out,
    norm2_gain,
    router,
    expert_gate,
    expert_up,
    expert_down,
    shared_gate,
    shared_up,
    shared_down,
    cotangent,
):
    shard_dims = (0, 0, 0, 0, 0, 0, 0, 1, 1, 1, 0, 0, 0)
    local_shapes = [
        weight.shape
        for weight in (
            norm1_gain,
            w_query,
            w_key,
            w_value,
            w_out,
            norm2_gain,
            router,
            expert_gate,
            expert_up,
            expert_down,
            shared_gate,
            shared_up,
            shared_down,
        )
    ]
    gathered = (
        lax.all_gather(norm1_gain, "shard", axis=0, tiled=True),
        lax.all_gather(w_query, "shard", axis=0, tiled=True),
        lax.all_gather(w_key, "shard", axis=0, tiled=True),
        lax.all_gather(w_value, "shard", axis=0, tiled=True),
        lax.all_gather(w_out, "shard", axis=0, tiled=True),
        lax.all_gather(norm2_gain, "shard", axis=0, tiled=True),
        lax.all_gather(router, "shard", axis=0, tiled=True),
        lax.all_gather(expert_gate, "shard", axis=1, tiled=True),
        lax.all_gather(expert_up, "shard", axis=1, tiled=True),
        lax.all_gather(expert_down, "shard", axis=1, tiled=True),
        lax.all_gather(shared_gate, "shard", axis=0, tiled=True),
        lax.all_gather(shared_up, "shard", axis=0, tiled=True),
        lax.all_gather(shared_down, "shard", axis=0, tiled=True),
    )
    (
        gain_first,
        query_full,
        key_full,
        value_full,
        out_full,
        gain_second,
        router_full,
        gate_full,
        up_full,
        down_full,
        common_gate,
        common_up,
        common_down,
    ) = gathered
    seqs_here = pic_block.shape[0]
    tok_rows = tokens.shape[0]
    length = tok_rows // seqs_here
    expert_count = router_full.shape[1]
    capacity = CAP

    def to_heads(matrix):
        return matrix.reshape(seqs_here, length, HEADS, HEAD_DIM)

    inputs = tokens.astype(jnp.float32)
    normed_one, inv_one = normalize(inputs, gain_first.astype(jnp.float32))
    normed_one_b = normed_one.astype(jnp.bfloat16)
    cosine_table, sine_table = rotary_tables(length, HEAD_DIM)
    query_pre = jnp.dot(normed_one_b, query_full, preferred_element_type=jnp.float32)
    key_pre = jnp.dot(normed_one_b, key_full, preferred_element_type=jnp.float32)
    query_rot = rotate(to_heads(query_pre), cosine_table, sine_table).astype(jnp.bfloat16)
    keys_rot = rotate(to_heads(key_pre), cosine_table, sine_table).astype(jnp.bfloat16)
    values_heads = to_heads(
        jnp.dot(normed_one_b, value_full, preferred_element_type=jnp.float32).astype(jnp.bfloat16)
    )
    mixed_full, log_sums = lax.map(attend_forward, (query_rot, keys_rot, values_heads, pic_block))
    mixed_b = mixed_full.astype(jnp.bfloat16).reshape(tok_rows, D)
    resid = inputs + jnp.dot(mixed_b, out_full, preferred_element_type=jnp.float32)
    gain_two_f = gain_second.astype(jnp.float32)
    normed_two, inv_two = normalize(resid, gain_two_f)
    normed_two_b = normed_two.astype(jnp.bfloat16)
    logits = jnp.dot(normed_two_b, router_full, preferred_element_type=jnp.float32)
    picked = routes[:, :, None] == jnp.arange(expert_count)[None, None, :]
    chosen = jnp.sum(jnp.where(picked, logits[:, None, :], 0.0), axis=-1)
    gates = jax.nn.softmax(chosen, axis=-1)
    flat_pick = picked.reshape(tok_rows * 2, expert_count).astype(jnp.int32)
    running = jnp.cumsum(flat_pick, axis=0) - 1
    slot_within = jnp.sum(running * flat_pick, axis=1)
    flat_slot = routes.reshape(-1) * capacity + slot_within
    owner = (
        jnp.zeros((expert_count * capacity,), jnp.int32)
        .at[flat_slot]
        .set(jnp.arange(tok_rows * 2, dtype=jnp.int32) // 2)
    )
    filled = jnp.zeros((expert_count * capacity,), jnp.bool_).at[flat_slot].set(True)
    slot_gate = (
        jnp.zeros((expert_count * capacity,), jnp.float32).at[flat_slot].set(gates.reshape(-1))
    )
    expert_in = jnp.where(filled[:, None], normed_two_b[owner], jnp.zeros((), jnp.bfloat16))
    expert_in = expert_in.reshape(expert_count, capacity, D)
    gate_pre = jnp.einsum("ecd,edf->ecf", expert_in, gate_full, preferred_element_type=jnp.float32)
    up_pre = jnp.einsum("ecd,edf->ecf", expert_in, up_full, preferred_element_type=jnp.float32)
    hidden_b = (jax.nn.silu(gate_pre) * up_pre).astype(jnp.bfloat16)
    expert_out = jnp.einsum("ecf,efd->ecd", hidden_b, down_full, preferred_element_type=jnp.float32)
    expert_flat = expert_out.reshape(expert_count * capacity, D)
    pair_out = expert_flat[flat_slot].reshape(tok_rows, 2, D)
    moe_out = jnp.sum(gates[:, :, None] * pair_out, axis=1)
    common_gate_pre = jnp.dot(normed_two_b, common_gate, preferred_element_type=jnp.float32)
    common_up_pre = jnp.dot(normed_two_b, common_up, preferred_element_type=jnp.float32)
    common_hid = (jax.nn.silu(common_gate_pre) * common_up_pre).astype(jnp.bfloat16)
    common_out = jnp.dot(common_hid, common_down, preferred_element_type=jnp.float32)
    output = (resid + moe_out + common_out).astype(jnp.bfloat16)
    again = (
        lax.all_gather(norm1_gain, "shard", axis=0, tiled=True),
        lax.all_gather(w_query, "shard", axis=0, tiled=True),
        lax.all_gather(w_key, "shard", axis=0, tiled=True),
        lax.all_gather(w_value, "shard", axis=0, tiled=True),
        lax.all_gather(w_out, "shard", axis=0, tiled=True),
        lax.all_gather(norm2_gain, "shard", axis=0, tiled=True),
        lax.all_gather(router, "shard", axis=0, tiled=True),
        lax.all_gather(expert_gate, "shard", axis=1, tiled=True),
        lax.all_gather(expert_up, "shard", axis=1, tiled=True),
        lax.all_gather(expert_down, "shard", axis=1, tiled=True),
        lax.all_gather(shared_gate, "shard", axis=0, tiled=True),
        lax.all_gather(shared_up, "shard", axis=0, tiled=True),
        lax.all_gather(shared_down, "shard", axis=0, tiled=True),
    )
    (
        gain_first,
        query_full,
        key_full,
        value_full,
        out_full,
        gain_second,
        router_full,
        gate_full,
        up_full,
        down_full,
        common_gate,
        common_up,
        common_down,
    ) = again
    d_output = cotangent.astype(jnp.float32)
    grad_common_down = weight_grad(common_hid, cotangent)
    d_common = jnp.dot(cotangent, common_down.T, preferred_element_type=jnp.float32)
    d_cgate, d_cup = swiglu_back(d_common, common_gate_pre, common_up_pre)
    grad_common_gate = weight_grad(normed_two_b, d_cgate)
    grad_common_up = weight_grad(normed_two_b, d_cup)
    d_normed = jnp.dot(d_cgate, common_gate.T, preferred_element_type=jnp.float32)
    d_normed = d_normed + jnp.dot(d_cup, common_up.T, preferred_element_type=jnp.float32)
    d_expert_out = (
        (d_output[owner] * slot_gate[:, None])
        .astype(jnp.bfloat16)
        .reshape(expert_count, capacity, D)
    )
    grad_down = jnp.einsum(
        "ecf,ecd->efd", hidden_b, d_expert_out, preferred_element_type=jnp.float32
    )
    d_hidden = jnp.einsum(
        "ecd,efd->ecf", d_expert_out, down_full, preferred_element_type=jnp.float32
    )
    d_gate_pre, d_up_pre = swiglu_back(d_hidden, gate_pre, up_pre)
    grad_gate = jnp.einsum(
        "ecd,ecf->edf", expert_in, d_gate_pre, preferred_element_type=jnp.float32
    )
    grad_up = jnp.einsum("ecd,ecf->edf", expert_in, d_up_pre, preferred_element_type=jnp.float32)
    d_expert_in = jnp.einsum(
        "ecf,edf->ecd", d_gate_pre, gate_full, preferred_element_type=jnp.float32
    )
    d_expert_in = d_expert_in + jnp.einsum(
        "ecf,edf->ecd", d_up_pre, up_full, preferred_element_type=jnp.float32
    )
    d_expert_flat = d_expert_in.reshape(expert_count * capacity, D)
    d_normed = d_normed + jnp.sum(d_expert_flat[flat_slot].reshape(tok_rows, 2, D), axis=1)
    d_gates = jnp.sum(d_output[:, None, :] * pair_out, axis=-1)
    d_chosen = gates * (d_gates - jnp.sum(gates * d_gates, axis=-1, keepdims=True))
    d_logits = jnp.sum(jnp.where(picked, d_chosen[:, :, None], 0.0), axis=1).astype(jnp.bfloat16)
    grad_router_full = weight_grad(normed_two_b, d_logits)
    d_normed = d_normed + jnp.dot(d_logits, router_full.T, preferred_element_type=jnp.float32)
    d_resid_norm, grad_gain_two = normalize_back(
        d_normed, resid, inv_two, gain_second.astype(jnp.float32)
    )
    d_resid = d_output + d_resid_norm
    d_resid_b = d_resid.astype(jnp.bfloat16)
    grad_out_full = weight_grad(mixed_b, d_resid_b)
    d_mixed = jnp.dot(d_resid_b, out_full.T, preferred_element_type=jnp.float32).astype(
        jnp.bfloat16
    )
    d_query, d_keys, d_values = lax.map(
        attend_backward, (query_rot, keys_rot, values_heads, pic_block, log_sums, to_heads(d_mixed))
    )
    d_query_pre = (
        rotate_back(d_query, cosine_table, sine_table).astype(jnp.bfloat16).reshape(tok_rows, D)
    )
    d_key_pre = (
        rotate_back(d_keys, cosine_table, sine_table).astype(jnp.bfloat16).reshape(tok_rows, D)
    )
    d_value_pre = d_values.astype(jnp.bfloat16).reshape(tok_rows, D)
    grad_query_full = weight_grad(normed_one_b, d_query_pre)
    grad_key_full = weight_grad(normed_one_b, d_key_pre)
    grad_value_full = weight_grad(normed_one_b, d_value_pre)
    d_normed_one = jnp.dot(d_query_pre, query_full.T, preferred_element_type=jnp.float32)
    d_normed_one = d_normed_one + jnp.dot(d_key_pre, key_full.T, preferred_element_type=jnp.float32)
    d_normed_one = d_normed_one + jnp.dot(
        d_value_pre, value_full.T, preferred_element_type=jnp.float32
    )
    d_input_norm, grad_gain_one = normalize_back(
        d_normed_one, inputs, inv_one, gain_first.astype(jnp.float32)
    )
    input_grad = d_resid + d_input_norm
    full_grads = (
        grad_gain_one,
        grad_query_full,
        grad_key_full,
        grad_value_full,
        grad_out_full,
        grad_gain_two,
        grad_router_full,
        grad_gate,
        grad_up,
        grad_down,
        grad_common_gate,
        grad_common_up,
        grad_common_down,
    )
    shard_count = lax.axis_size("shard")
    rep_count = lax.axis_size("rep")
    halves = []
    for shard_pos in range(shard_count):
        parts_here = []
        for whole_grad, axis_pos, shape_here in zip(full_grads, shard_dims, local_shapes):
            width_here = shape_here[axis_pos]
            piece = lax.slice_in_dim(
                whole_grad, shard_pos * width_here, (shard_pos + 1) * width_here, axis=axis_pos
            )
            parts_here.append(piece.reshape(-1))
        halves.append(jnp.concatenate(parts_here))
    half_size = halves[0].shape[0]
    ordered = jnp.stack(halves).reshape(shard_count, rep_count, half_size // rep_count)
    ordered = jnp.transpose(ordered, (1, 0, 2)).reshape(-1)
    reduced = lax.psum_scatter(ordered, ("rep", "shard"), scatter_dimension=0, tiled=True)
    spread = lax.all_gather(reduced, "rep", axis=0, tiled=True)
    pieces = []
    offset = 0
    for shape_here in local_shapes:
        entries = 1
        for extent in shape_here:
            entries = entries * extent
        pieces.append(spread[offset : offset + entries].reshape(shape_here))
        offset = offset + entries
    return (
        output,
        input_grad,
        pieces[0],
        pieces[1],
        pieces[2],
        pieces[3],
        pieces[4],
        pieces[5],
        pieces[6],
        pieces[7],
        pieces[8],
        pieces[9],
        pieces[10],
        pieces[11],
        pieces[12],
    )


def solution(mesh):
    return jax.shard_map(
        on_device,
        mesh=mesh,
        in_specs=(
            P(("rep", "shard"), None),
            P(("rep", "shard"), None),
            P(("rep", "shard")),
            P("shard"),
            P("shard", None),
            P("shard", None),
            P("shard", None),
            P("shard", None),
            P("shard"),
            P("shard", None),
            P(None, "shard", None),
            P(None, "shard", None),
            P(None, "shard", None),
            P("shard", None),
            P("shard", None),
            P("shard", None),
            P(("rep", "shard"), None),
        ),
        out_specs=(
            P(("rep", "shard"), None),
            P(("rep", "shard"), None),
            P("shard"),
            P("shard", None),
            P("shard", None),
            P("shard", None),
            P("shard", None),
            P("shard"),
            P("shard", None),
            P(None, "shard", None),
            P(None, "shard", None),
            P(None, "shard", None),
            P("shard", None),
            P("shard", None),
            P("shard", None),
        ),
        check_vma=False,
    )
```

profile of v0, /device:TPU:0, one launch (start us, length us, event | category | flops | bytes accessed | tf_op | source)
XLA Modules:
  0.0 5645.7 jit_solution(18397870925945727596)
XLA Ops:
  210.9 36.6 all-gather.31.cloned.1.call-done
  308.6 92.0 %all-gather.23.cloned.1.call-done = bf16[4,768,2048]{2,1,0:T(8,128)(2,1)} async-done(((bf16[4,384,2048]{2,1,0:T(8,128)(2,1)}), bf16[4,768,2048]{2,1,0:T(8,128)(2,1)}) %all-gather.23.cloned.1.call-update) | async-done | bytes 12582928 | tf_op jit(solution)/shard_map/all_gather | solution.py:179
  400.6 19.2 fusion.53
  419.8 133.9 %all-gather.21.cloned.1.call-done = bf16[4,768,2048]{2,1,0:T(8,128)(2,1)} async-done(((bf16[4,384,2048]{2,1,0:T(8,128)(2,1)}), bf16[4,768,2048]{2,1,0:T(8,128)(2,1)}) %all-gather.21.cloned.1.call-update) | async-done | bytes 12582928 | tf_op jit(solution)/shard_map/all_gather | solution.py:178
  553.7 19.6 fusion.54
  573.3 133.4 %all-gather.25.cloned.1.call-done = bf16[4,2048,768]{2,1,0:T(8,128)(2,1)} async-done(((bf16[4,1024,768]{2,1,0:T(8,128)(2,1)}), bf16[4,2048,768]{2,1,0:T(8,128)(2,1)}) %all-gather.25.cloned.1.call-update) | async-done | bytes 12582928 | tf_op jit(solution)/shard_map/all_gather | solution.py:180
  706.7 32.3 multiply_convert_fusion.2
  738.9 16.6 fusion.173
  755.5 17.5 convolution_add_fusion
  807.7 16.5 fusion.168
  846.9 17.2 multiply_reduce_fusion.2
  887.1 54.3 fusion.20
  941.4 52.0 fusion.23
  999.3 17.5 fusion.52
  1016.8 17.4 fusion.51
  1034.1 19.7 fusion.68
  1078.7 52.0 fusion.29
  1130.7 54.0 fusion.61
  1242.1 18.5 fusion.159
  1272.7 19.0 fusion.158
  1303.9 18.3 fusion.157
  1437.1 106.9 %dynamic-update-slice.21 = f32[12978432]{0:T(1024)} dynamic-update-slice(f32[12978432]{0:T(1024)} %constant_dynamic-update-slice_fusion, f32[3145728]{0:T(1024)} %bitcast.175, s32[]{} %constant.178) | dynamic-update-slice | bytes 25165828
  1544.0 106.8 %dynamic-update-slice.22 = f32[12978432]{0:T(1024)} dynamic-update-slice(f32[12978432]{0:T(1024)} %dynamic-update-slice.21, f32[3145728]{0:T(1024)} %bitcast.176, s32[]{} %constant.179) | dynamic-update-slice | bytes 25165828
  1650.8 106.9 %dynamic-update-slice.23 = f32[12978432]{0:T(1024)} dynamic-update-slice(f32[12978432]{0:T(1024)} %dynamic-update-slice.22, f32[3145728]{0:T(1024)} %reshape.674, s32[]{} %constant.180) | dynamic-update-slice | bytes 25165828
  1757.8 26.4 dynamic-update-slice.24
  1784.2 28.0 dynamic-update-slice.25
  1812.2 26.3 dynamic-update-slice.26
  1838.5 301.3 %while.3 = (u32[]{:T(128)}, f32[12978432]{0:T(1024)}, f32[16,1,811152]{2,1,0:T(1,128)}, u32[]{}, u32[]{}) while((u32[]{:T(128)}, f32[12978432]{0:T(1024)}, f32[16,1,811152]{2,1,0:T(1,128)}, u32[]{}, u32[]{}) %tuple.83), condition=%wide.cond.1, body=%wide.body.1.sunk | while | flops 9 | bytes 12979037
  1841.5 16.0 reshape_dynamic-update-slice_fusion.5
  1992.1 16.0 reshape_dynamic-update-slice_fusion.5
  2179.5 106.9 %dynamic-update-slice.8 = f32[12978432]{0:T(1024)} dynamic-update-slice(f32[12978432]{0:T(1024)} %constant_dynamic-update-slice_fusion.1, f32[3145728]{0:T(1024)} %bitcast.178, s32[]{} %constant.178) | dynamic-update-slice | bytes 25165828
  2286.4 106.9 %dynamic-update-slice.9 = f32[12978432]{0:T(1024)} dynamic-update-slice(f32[12978432]{0:T(1024)} %dynamic-update-slice.8, f32[3145728]{0:T(1024)} %bitcast.177, s32[]{} %constant.179) | dynamic-update-slice | bytes 25165828
  2393.3 107.1 %dynamic-update-slice.10 = f32[12978432]{0:T(1024)} dynamic-update-slice(f32[12978432]{0:T(1024)} %dynamic-update-slice.9, f32[3145728]{0:T(1024)} %reshape.685, s32[]{} %constant.180) | dynamic-update-slice | bytes 25165828
  2500.4 26.5 dynamic-update-slice.11
  2526.9 28.0 dynamic-update-slice.12
  2554.9 26.3 dynamic-update-slice.13
  2581.2 301.2 %while.2 = (u32[]{:T(128)}, f32[12978432]{0:T(1024)}, f32[16,1,811152]{2,1,0:T(1,128)}, u32[]{}, u32[]{}) while((u32[]{:T(128)}, f32[12978432]{0:T(1024)}, f32[16,1,811152]{2,1,0:T(1,128)}, u32[]{}, u32[]{}) %tuple.80), condition=%wide.cond, body=%wide.body.sunk | while | flops 9 | bytes 12979037
  2602.8 16.0 reshape_dynamic-update-slice_fusion.4
  2621.6 16.0 reshape_dynamic-update-slice_fusion.4
  2809.9 16.0 reshape_dynamic-update-slice_fusion.4
  2828.7 16.0 reshape_dynamic-update-slice_fusion.4
  2882.4 124.3 %maximum_bitcast_fusion = f32[16,2,811152]{2,1,0:T(2,128)} fusion(f32[1,16,811152]{2,0,1:T(1,128)} %bitcast.171, f32[1,16,811152]{2,0,1:T(1,128)} %bitcast.172), kind=kLoop, calls=%fused_computation.9 | loop fusion | flops 25956864 | bytes 207654912 | tf_op jit(solution)/shard_map/transpose | solution.py:384
  3006.7 194.2 %reshape.689 = f32[25956864]{0:T(1024)} reshape(f32[16,2,811152]{2,1,0:T(2,128)} %maximum_bitcast_fusion) | data formatting | bytes 207654912 | tf_op jit(solution)/shard_map/reshape | solution.py:384
  3202.8 1437.9 %all-reduce.7.cloned.1.call-done = f32[25956864]{0:T(1024)} async-done(((f32[25956864]{0:T(1024)}), f32[25956864]{0:T(1024)}) %all-reduce.7.cloned.1.call-update) | async-done | bytes 103827472
  4643.5 16.5 broadcast.424
  4659.9 26.8 dynamic-update-slice
  4712.9 828.2 %all-reduce.5.cloned.1.call-done = f32[12978432]{0:T(1024)} async-done(((f32[12978432]{0:T(1024)}), f32[12978432]{0:T(1024)}) %all-reduce.5.cloned.1.call-update) | async-done | bytes 51913744
  5541.2 25.5 fusion.154
  (490 shorter events, 1218.6 us)
Async XLA Ops:
  7.2 65.5 %all-gather.15.cloned.1.call-start = ((), (), s32[]{:S(2)}) async-start(), calls=%async_computation.1 | async-start | bytes 1769472 | tf_op jit(solution)/shard_map/all_gather | solution.py:172
  7.9 71.1 %all-gather.17.cloned.1.call-start = ((), (), s32[]{:S(2)}) async-start(), calls=%async_computation.2 | async-start | bytes 1769472 | tf_op jit(solution)/shard_map/all_gather | solution.py:173
  8.7 101.5 %all-gather.13.cloned.1.call-start = ((), (), s32[]{:S(2)}) async-start(), calls=%async_computation | async-start | bytes 1769472 | tf_op jit(solution)/shard_map/all_gather | solution.py:174
  9.4 153.7 %all-gather.19.cloned.1.call-start = ((), (), s32[]{:S(2)}) async-start(), calls=%async_computation.3 | async-start | bytes 1769472 | tf_op jit(solution)/shard_map/all_gather | solution.py:175
  10.0 185.6 %all-gather.27.cloned.1.call-start = ((), (), s32[]{:S(2)}) async-start(), calls=%async_computation.7 | async-start | bytes 4718592 | tf_op jit(solution)/shard_map/all_gather | solution.py:181
  10.6 192.6 %all-gather.29.cloned.1.call-start = ((), (), s32[]{:S(2)}) async-start(), calls=%async_computation.8 | async-start | bytes 4718592 | tf_op jit(solution)/shard_map/all_gather | solution.py:182
  11.1 236.3 %all-gather.31.cloned.1.call-start = ((), (), s32[]{:S(2)}) async-start(), calls=%async_computation.9 | async-start | bytes 4718592 | tf_op jit(solution)/shard_map/all_gather | solution.py:183
  11.9 388.7 %all-gather.23.cloned.1.call-start = ((), (), s32[]{:S(2)}) async-start(), calls=%async_computation.5 | async-start | bytes 18874368 | tf_op jit(solution)/shard_map/all_gather | solution.py:179
  12.6 541.1 %all-gather.21.cloned.1.call-start = ((), (), s32[]{:S(2)}) async-start(), calls=%async_computation.4 | async-start | bytes 18874368 | tf_op jit(solution)/shard_map/all_gather | solution.py:178
  13.4 693.3 %all-gather.25.cloned.1.call-start = ((), (), s32[]{:S(2)}) async-start(), calls=%async_computation.6 | async-start | bytes 18874368 | tf_op jit(solution)/shard_map/all_gather | solution.py:180
  14.0 4626.6 %all-reduce.7.cloned.1.call-start = ((), (), s32[]{:S(2)}) async-start(), calls=%async_computation.11 | async-start | bytes 207659008
  14.6 15.9 copy-start.91
  16.2 39.6 copy-start.8
  22.6 87.6 %copy-start.77 = (f32[768]{0:T(1024)}, f32[768]{0:T(1024)S(1)}, u32[]{:S(2)}) copy-start(f32[768]{0:T(1024)S(1)} %reshape.765) | copy-start | bytes 9220
  37.2 18.6 copy-start.85
  45.9 16.3 copy-start.64
  62.2 23.0 copy-start.28
  86.1 41.4 copy-start.15
  113.1 38.5 copy-start.12
  138.1 15.9 copy-start.44
  168.5 99.1 %copy-start.6 = (bf16[1024,768]{0,1:T(8,128)(2,1)}, bf16[1024,768]{0,1:T(8,128)(2,1)S(1)}, u32[]{:S(2)}) copy-start(bf16[1024,768]{0,1:T(8,128)(2,1)S(1)} %multiply_convert_fusion.9) | copy-start | bytes 4718596
  170.1 19.2 copy-start.59
  170.1 19.2 copy-start.66
  170.1 19.1 copy-start.73
  180.7 525.9 %copy-start.88 = (f32[4,640]{1,0:T(4,128)}, f32[4,640]{1,0:T(4,128)S(1)}, u32[]{:S(2)}) copy-start(f32[4,640]{1,0:T(4,128)S(1)} %mul.399) | copy-start | bytes 30724
  203.2 44.3 copy-start.56
  303.5 97.1 %copy-start.92 = (pred[4,640]{1,0:T(4,128)(4,1)S(1)}, pred[4,640]{1,0:T(4,128)(4,1)}, u32[]{:S(2)}) copy-start(pred[4,640]{1,0:T(4,128)(4,1)} %broadcast_in_dim.191) | copy-start | bytes 7684
  755.5 17.5 copy-start.68
  846.8 18.5 copy-start.60
  846.8 18.5 copy-start.67
  846.8 18.5 copy-start.74
  846.9 18.5 copy-start.63
  846.9 18.6 copy-start.70
  846.9 18.6 copy-start.72
  846.9 18.6 copy-start.76
  887.1 54.3 copy-start.16
  1016.8 17.4 copy-start.89
  1344.6 23.8 copy-start.47
  1356.9 22.4 copy-start.50
  1356.9 33.4 copy-start.48
  1379.3 33.3 copy-start.46
  1390.3 33.2 copy-start.49
  1401.3 33.2 copy-start.87
  1650.8 106.9 %copy-start.19 = (f32[48,16,8,128]{3,1,2,0:T(8,128)S(1)}, f32[48,16,8,128]{3,1,2,0:T(8,128)}, u32[]{:S(2)}) copy-start(f32[48,16,8,128]{3,1,2,0:T(8,128)} %copy.177) | copy-start | bytes 9437188
  1784.2 28.0 copy-start.20
  2393.3 107.1 %copy-start.18 = (f32[48,16,8,128]{3,1,2,0:T(8,128)S(1)}, f32[48,16,8,128]{3,1,2,0:T(8,128)}, u32[]{:S(2)}) copy-start(f32[48,16,8,128]{3,1,2,0:T(8,128)} %copy.181) | copy-start | bytes 9437188
  2526.9 28.0 copy-start.17
  3200.9 2340.3 %all-reduce.5.cloned.1.call-start = ((), (), s32[]{:S(2)}) async-start(), calls=%async_computation.10 | async-start | bytes 103833600
  (72 other events, 338.7 us)
Sparse Core Ops, SparseCore 0:
  9.6 25.5 all-gather.14
  36.7 22.7 all-gather.16
  61.1 22.7 all-gather.12
  85.3 22.7 all-gather.18
  109.5 44.9 all-gather.26
  155.9 45.0 all-gather.28
  202.5 44.9 all-gather.30
  249.0 151.5 all-gather.22
  402.1 151.5 all-gather.20
  555.1 151.5 all-gather.24
  3201.0 1439.5 all-reduce.6
  4686.9 854.1 all-reduce.4
where the time goes:
time: 5720 us; the launch traced here: 5650 us
  waiting for transfers between devices  2670 us (47%)
  local copies, waits for them, and re-layouts  2160 us (38%)
  matrix products  584 us (10%)
  other arithmetic  206 us (4%)
    unnamed x14, waiting for transfers between devices  2270 us
    unnamed x324, local copies, waits for them, and re-layouts  1590 us
    reshape x1, local copies, waits for them, and re-layouts, on_device(): ordered = jnp.transpose(ordered, (1, 0, 2)).reshape(-1)  194 us
    all_gather x1, waiting for transfers between devices, on_device(): lax.all_gather(expert_gate, 'shard', axis=1, tiled=True)  134 us
    all_gather x1, waiting for transfers between devices, on_device(): lax.all_gather(expert_down, 'shard', axis=1, tiled=True)  133 us
    transpose x1, other arithmetic, on_device(): ordered = jnp.transpose(ordered, (1, 0, 2)).reshape(-1)  124 us
  transfers between devices with their start and end apart: 12, of which 6 were waited for; matrix products, arithmetic and copies ran while one was open for 5% of the time, Pallas kernels for 0%

commit v1 on v0

v1 whole, which is shorter than its diff:
```python
import functools

import jax
import jax.numpy as jnp
from jax import lax
from jax.experimental import pallas as pl
from jax.experimental.pallas import tpu as pltpu
from jax.sharding import PartitionSpec as P

D = 768
HEADS = 12
HEAD_DIM = 64
PIC = 256
CAP = 640
PAIR = 2 * HEAD_DIM
PAIRS = HEADS // 2
QB = 256
EPS = 1e-05
BF = jnp.bfloat16
F32 = jnp.float32
ALL = ("rep", "shard")
MIB = 1 << 20


def nn(a, b):
    return lax.dot_general(a, b, (((1,), (0,)), ((), ())), preferred_element_type=F32)


def nt(a, b):
    return lax.dot_general(a, b, (((1,), (1,)), ((), ())), preferred_element_type=F32)


def resident(shape):
    zeros = (0,) * len(shape)
    return pl.BlockSpec(shape, lambda *_: zeros, pipeline_mode=pl.Buffered(1))


def rotary_tables(length):
    halfway = HEAD_DIM // 2
    freqs_base = 10000.0 ** (-jnp.arange(halfway, dtype=F32) / halfway)
    angles = jnp.arange(length, dtype=F32)[:, None] * freqs_base[None, :]
    cosine = jnp.cos(angles)
    sine = jnp.sin(angles)
    zero = jnp.zeros_like(sine)
    cos_t = jnp.concatenate([cosine] * 4, axis=1)
    left = jnp.concatenate([-sine, zero, -sine, zero], axis=1)
    right = jnp.concatenate([zero, sine, zero, sine], axis=1)
    return cos_t, left, right


def turned(v, left, right):
    return pltpu.roll(v, 96, 1) * left + pltpu.roll(v, 32, 1) * right


def head_masks(rows):
    lane = lax.broadcasted_iota(jnp.int32, (rows, PAIR), 1)
    return lane < HEAD_DIM, lane >= HEAD_DIM


def attend_forward_body(pic, tok, gain, wqkv, cos_t, left, right, q_o, k_o, v_o, mix_o, lse_o, xn):
    length = tok.shape[0]

    @pl.when(pl.program_id(0) == 0)
    def _():
        for lo in range(0, length, QB):
            x = tok[lo : lo + QB, :].astype(F32)
            inv = lax.rsqrt(jnp.mean(x * x, axis=1, keepdims=True) + EPS)
            xn[lo : lo + QB, :] = (x * inv * gain[...]).astype(BF)

    for lo in range(0, length, QB):
        rows = slice(lo, lo + QB)
        qkv = nn(xn[rows, :], wqkv[...])
        q, k = qkv[:, :PAIR], qkv[:, PAIR : 2 * PAIR]
        c_, l_, r_ = cos_t[rows, :], left[rows, :], right[rows, :]
        q_o[rows, :] = (q * c_ + turned(q, l_, r_)).astype(BF) * jnp.asarray(0.125, BF)
        k_o[rows, :] = (k * c_ + turned(k, l_, r_)).astype(BF)
        v_o[rows, :] = qkv[:, 2 * PAIR :].astype(BF)
    masks = head_masks(QB)
    row = lax.broadcasted_iota(jnp.int32, (QB, QB), 0)
    col = lax.broadcasted_iota(jnp.int32, (QB, QB), 1)
    causal = col <= row
    for block in range(length // QB):
        rows = slice(block * QB, (block + 1) * QB)
        allowed = causal | (pic[0] == block)
        q = q_o[rows, :]
        outs = []
        for head in range(2):
            qm = jnp.where(masks[head], q, jnp.zeros_like(q))
            s_d = jnp.where(allowed, nt(qm, k_o[rows, :]), -1e30)
            top = jnp.max(s_d, axis=1, keepdims=True)
            if block:
                s_o = nt(qm, k_o[: block * QB, :])
                top = jnp.maximum(top, jnp.max(s_o, axis=1, keepdims=True))
            p_d = jnp.exp(s_d - top)
            total = jnp.sum(p_d, axis=1, keepdims=True)
            acc = nn(p_d.astype(BF), v_o[rows, :])
            if block:
                p_o = jnp.exp(s_o - top)
                total = total + jnp.sum(p_o, axis=1, keepdims=True)
                acc = acc + nn(p_o.astype(BF), v_o[: block * QB, :])
            outs.append(acc / total)
            lse = jnp.broadcast_to(top + jnp.log(total), (QB, PAIR))
            lse_o[0, head : head + 1, rows] = jnp.transpose(lse)[0:1, :]
        mix_o[rows, :] = jnp.where(masks[0], outs[0], outs[1]).astype(BF)


def attend_forward(pic_block, tokens, gain, wqkv, tables):
    length = tokens.shape[0]
    pair = pl.BlockSpec((length, PAIR), lambda p: (0, p))
    wide = jax.ShapeDtypeStruct((length, D), BF)
    return pl.pallas_call(
        attend_forward_body,
        grid=(PAIRS,),
        in_specs=[
            pl.BlockSpec(memory_space=pltpu.SMEM),
            resident((length, D)),
            resident((1, D)),
            pl.BlockSpec((D, 3 * PAIR), lambda p: (0, p)),
            resident((length, PAIR)),
            resident((length, PAIR)),
            resident((length, PAIR)),
        ],
        out_specs=[pair, pair, pair, pair, pl.BlockSpec((1, 8, length), lambda p: (p, 0, 0))],
        out_shape=[wide, wide, wide, wide, jax.ShapeDtypeStruct((PAIRS, 8, length), F32)],
        scratch_shapes=[pltpu.VMEM((length, D), BF)],
        compiler_params=pltpu.CompilerParams(vmem_limit_bytes=48 * MIB),
        name="attend_forward",
    )(pic_block, tokens, gain, wqkv, *tables)


def attend_backward_body(
    pic, tok, gain, wqkv, wout, cos_t, left, right, q_i, k_i, v_i, mix_i, lse_i, dres, dres_f,
    gqkv_o, gout_o, igrad_o, ggain_o,
    xn_t, dxn, dmix, dqkv, dk_s, dv_s, k_t,
):
    length = tok.shape[0]
    step = pl.program_id(0)

    @pl.when(step == 0)
    def _():
        for lo in range(0, length, QB):
            x = tok[lo : lo + QB, :].astype(F32)
            inv = lax.rsqrt(jnp.mean(x * x, axis=1, keepdims=True) + EPS)
            xn_t[:, lo : lo + QB] = jnp.transpose((x * inv * gain[...]).astype(BF))

    dm = nt(dres[...], wout[...]).astype(BF)
    dmix[...] = dm
    mixed = mix_i[...]
    gout_o[...] = nn(jnp.transpose(mixed), dres[...]).astype(BF)
    prod = jnp.transpose(dm.astype(F32) * mixed.astype(F32))
    delta = (
        jnp.sum(prod[:HEAD_DIM, :], axis=0, keepdims=True),
        jnp.sum(prod[HEAD_DIM:, :], axis=0, keepdims=True),
    )
    k_t[...] = jnp.transpose(k_i[...])
    masks = head_masks(QB)
    key_row = lax.broadcasted_iota(jnp.int32, (QB, QB), 0)
    query_col = lax.broadcasted_iota(jnp.int32, (QB, QB), 1)
    causal = key_row <= query_col
    for block in reversed(range(length // QB)):
        rows = slice(block * QB, (block + 1) * QB)
        first = block == length // QB - 1
        allowed = causal | (pic[0] == block)
        q = q_i[rows, :]
        dm = dmix[rows, :]
        dq_t = []
        parts = {"d": [], "o": []}
        for head in range(2):
            qm = jnp.where(masks[head], q, jnp.zeros_like(q))
            dmm = jnp.where(masks[head], dm, jnp.zeros_like(dm))
            lse = lse_i[0, head : head + 1, rows]
            cent = delta[head][:, rows]
            half = slice(head * HEAD_DIM, (head + 1) * HEAD_DIM)
            dq = None
            for part, keys in (("d", rows), ("o", slice(0, block * QB))):
                if part == "o" and block == 0:
                    continue
                st = nt(k_i[keys, :], qm)
                pt = jnp.exp(st - lse)
                if part == "d":
                    pt = jnp.where(allowed, pt, 0.0)
                dpt = nt(v_i[keys, :], dmm)
                dst = (pt * (dpt - cent)).astype(BF)
                parts[part].append((nn(dst, qm), nn(pt.astype(BF), dmm)))
                add = nn(k_t[half, keys], dst)
                dq = add if dq is None else dq + add
            dq_t.append(dq)
        for part, keys in (("d", rows), ("o", slice(0, block * QB))):
            if not parts[part]:
                continue
            dk = parts[part][0][0] + parts[part][1][0]
            dv = parts[part][0][1] + parts[part][1][1]
            if first:
                dk_s[keys, :] = dk
                dv_s[keys, :] = dv
            else:
                dk_s[keys, :] = dk_s[keys, :] + dk
                dv_s[keys, :] = dv_s[keys, :] + dv
        dq = jnp.transpose(jnp.concatenate(dq_t, axis=0)) * 0.125
        c_, l_, r_ = cos_t[rows, :], left[rows, :], right[rows, :]
        dqkv[rows, :PAIR] = (dq * c_ - turned(dq, l_, r_)).astype(BF)
        dk = dk_s[rows, :]
        dqkv[rows, PAIR : 2 * PAIR] = (dk * c_ - turned(dk, l_, r_)).astype(BF)
        dqkv[rows, 2 * PAIR :] = dv_s[rows, :].astype(BF)
    gqkv_o[...] = nn(xn_t[...], dqkv[...]).astype(BF)
    add = nt(dqkv[...], wqkv[...])

    @pl.when(step == 0)
    def _():
        dxn[...] = add

    @pl.when(step > 0)
    def _():
        dxn[...] = dxn[...] + add

    @pl.when(step == PAIRS - 1)
    def _():
        total = jnp.zeros((1, D), F32)
        for lo in range(0, length, QB):
            rows = slice(lo, lo + QB)
            x = tok[rows, :].astype(F32)
            inv = lax.rsqrt(jnp.mean(x * x, axis=1, keepdims=True) + EPS)
            n = x * inv
            up = dxn[rows, :]
            total = total + jnp.sum(up * n, axis=0, keepdims=True)
            u = up * gain[...]
            igrad_o[rows, :] = dres_f[rows, :] + inv * (u - n * jnp.mean(u * n, axis=1, keepdims=True))
        ggain_o[...] = total


def attend_backward(pic_block, tokens, gain, wqkv, wout, tables, q, k, v, mixed, lse, dres, dres_f):
    length = tokens.shape[0]
    pair = pl.BlockSpec((length, PAIR), lambda p: (0, p))
    return pl.pallas_call(
        attend_backward_body,
        grid=(PAIRS,),
        in_specs=[
            pl.BlockSpec(memory_space=pltpu.SMEM),
            resident((length, D)),
            resident((1, D)),
            pl.BlockSpec((D, 3 * PAIR), lambda p: (0, p)),
            pl.BlockSpec((PAIR, D), lambda p: (p, 0)),
            resident((length, PAIR)),
            resident((length, PAIR)),
            resident((length, PAIR)),
            pair, pair, pair, pair,
            pl.BlockSpec((1, 8, length), lambda p: (p, 0, 0)),
            resident((length, D)),
            resident((length, D)),
        ],
        out_specs=[
            pl.BlockSpec((D, 3 * PAIR), lambda p: (0, p)),
            pl.BlockSpec((PAIR, D), lambda p: (p, 0)),
            resident((length, D)),
            resident((1, D)),
        ],
        out_shape=[
            jax.ShapeDtypeStruct((D, 3 * D), BF),
            jax.ShapeDtypeStruct((D, D), BF),
            jax.ShapeDtypeStruct((length, D), F32),
            jax.ShapeDtypeStruct((1, D), F32),
        ],
        scratch_shapes=[
            pltpu.VMEM((D, length), BF),
            pltpu.VMEM((length, D), F32),
            pltpu.VMEM((length, PAIR), BF),
            pltpu.VMEM((length, 3 * PAIR), BF),
            pltpu.VMEM((length, PAIR), F32),
            pltpu.VMEM((length, PAIR), F32),
            pltpu.VMEM((PAIR, length), BF),
        ],
        compiler_params=pltpu.CompilerParams(vmem_limit_bytes=56 * MIB),
        name="attend_backward",
    )(pic_block, tokens, gain, wqkv, wout, *tables, q, k, v, mixed, lse, dres, dres_f)


def middle_body(shard, tok, mixed, wout, gain, router_t, routes_t, resid_o, n2_o, n2p_o, comb_o):
    r = tok[...].astype(F32) + nn(mixed[...], wout[...])
    resid_o[...] = r
    inv = lax.rsqrt(jnp.mean(r * r, axis=1, keepdims=True) + EPS)
    n2 = (r * inv * gain[...]).astype(BF)
    n2_o[...] = n2
    half = D // 2
    swapped = jnp.concatenate([n2[:, half:], n2[:, :half]], axis=1)
    n2p_o[...] = jnp.where(shard[0] == 0, n2, swapped)
    logits = nt(router_t[...], n2)
    expert = lax.broadcasted_iota(jnp.int32, logits.shape, 0)
    picks = [expert == routes_t[k : k + 1, :] for k in range(2)]
    chosen = [jnp.sum(jnp.where(p, logits, 0.0), axis=0, keepdims=True) for p in picks]
    top = jnp.maximum(chosen[0], chosen[1])
    weights = [jnp.exp(v - top) for v in chosen]
    total = weights[0] + weights[1]
    gates = [w / total for w in weights]
    comb_o[...] = jnp.where(picks[0], gates[0], 0.0) + jnp.where(picks[1], gates[1], 0.0)


def middle(shard, tokens, mixed, wout, gain, router_t, routes_t):
    length = tokens.shape[0]
    block = 256
    rows = pl.BlockSpec((block, D), lambda i: (i, 0))
    cols = pl.BlockSpec((8, block), lambda i: (0, i))
    return pl.pallas_call(
        middle_body,
        grid=(length // block,),
        in_specs=[
            pl.BlockSpec(memory_space=pltpu.SMEM),
            rows,
            rows,
            resident((D, D)),
            resident((1, D)),
            resident((8, D)),
            cols,
        ],
        out_specs=[rows, rows, rows, cols],
        out_shape=[
            jax.ShapeDtypeStruct((length, D), F32),
            jax.ShapeDtypeStruct((length, D), BF),
            jax.ShapeDtypeStruct((length, D), BF),
            jax.ShapeDtypeStruct((8, length), F32),
        ],
        compiler_params=pltpu.CompilerParams(vmem_limit_bytes=40 * MIB),
        name="middle",
    )(shard, tokens, mixed, wout, gain, router_t, routes_t)


def join_body(shard, dy, resid, gain, dlog, router_t, *refs):
    outs, dxs = refs[:6], refs[6:12]
    out_o, dres_o, dlow_o, ggain_o = refs[12:]
    r = resid[...]
    total = r
    for part in outs:
        total = total + part[...].astype(F32)
    out_o[...] = total.astype(BF)
    up = dxs[0][...].astype(F32)
    for part in dxs[1:]:
        up = up + part[...].astype(F32)
    half = D // 2
    swapped = jnp.concatenate([up[:, half:], up[:, :half]], axis=1)
    up = jnp.where(shard[0] == 0, up, swapped)
    up = up + nn(dlog[...], router_t[...])
    inv = lax.rsqrt(jnp.mean(r * r, axis=1, keepdims=True) + EPS)
    n = r * inv
    add = jnp.sum(up * n, axis=0, keepdims=True)

    @pl.when(pl.program_id(0) == 0)
    def _():
        ggain_o[...] = add

    @pl.when(pl.program_id(0) > 0)
    def _():
        ggain_o[...] = ggain_o[...] + add

    u = up * gain[...]
    d = dy[...].astype(F32) + inv * (u - n * jnp.mean(u * n, axis=1, keepdims=True))
    dres_o[...] = d
    dlow_o[...] = d.astype(BF)


def join(shard, dy, resid, gain, dlog, router_t, outs, dxs):
    length = dy.shape[0]
    block = 256
    rows = pl.BlockSpec((block, D), lambda i: (i, 0))

    def part_spec(part):
        if part.ndim == 3:
            return pl.BlockSpec((None, block, D), lambda i: (0, i, 0))
        return rows

    return pl.pallas_call(
        join_body,
        grid=(length // block,),
        in_specs=[
            pl.BlockSpec(memory_space=pltpu.SMEM),
            rows,
            rows,
            resident((1, D)),
            pl.BlockSpec((block, 128), lambda i: (i, 0)),
            resident((128, D)),
        ]
        + [part_spec(p) for p in outs]
        + [part_spec(p) for p in dxs],
        out_specs=[rows, rows, rows, pl.BlockSpec((1, D), lambda i: (0, 0))],
        out_shape=[
            jax.ShapeDtypeStruct((length, D), BF),
            jax.ShapeDtypeStruct((length, D), F32),
            jax.ShapeDtypeStruct((length, D), BF),
            jax.ShapeDtypeStruct((1, D), F32),
        ],
        compiler_params=pltpu.CompilerParams(vmem_limit_bytes=40 * MIB),
        name="join",
    )(shard, dy, resid, gain, dlog, router_t, *outs, *dxs)


def ffn_body(routed, steps, chunk, where, tok, dy, *refs):
    if routed:
        slot_row, slot_col, gate_row = refs[:3]
        refs = refs[3:]
    g_own, g_oth, u_own, u_oth, d_own, d_oth = refs[:6]
    refs = refs[6:]
    out_o, dx_o = refs[:2]
    refs = refs[2:]
    if routed:
        dgate_o = refs[0]
        refs = refs[1:]
    kg_o, sg_o, ku_o, su_o, kd_o, sd_o = refs[:6]
    refs = refs[6:]
    wg, wu, wd, y_acc, dx_acc, hid_s, dg_s, du_s, x_t, de_t = refs[:10]
    refs = refs[10:]
    i = pl.program_id(0)
    srcs, length = tok.shape[0], tok.shape[1]
    rows_all = y_acc.shape[0]
    hold = rows_all // srcs
    half = D // 2
    if routed:
        x_s, de_s, dys, gate_s = refs
    tile = 128

    @pl.when(i == 0)
    def _():
        for src in range(srcs):
            if routed:
                for lo in range(0, hold, tile):
                    slot = lax.broadcasted_iota(jnp.int32, (tile, length), 0) + lo
                    mine = slot == slot_row[src : src + 1, :]
                    pick = jnp.where(mine, 1.0, 0.0).astype(BF)
                    rows = slice(src * hold + lo, src * hold + lo + tile)
                    x = nn(pick, tok[src]).astype(BF)
                    d_raw = nn(pick, dy[src])
                    gate = jnp.sum(jnp.where(mine, gate_row[src : src + 1, :], 0.0), axis=1, keepdims=True)
                    gate_s[rows, :] = jnp.broadcast_to(gate, (tile, 128))
                    d_e = (d_raw * gate).astype(BF)
                    x_s[rows, :] = x
                    dys[rows, :] = d_raw.astype(BF)
                    de_s[rows, :] = d_e
                    x_t[:, rows] = jnp.transpose(x)
                    de_t[:, rows] = jnp.transpose(d_e)
            else:
                for lo in range(0, hold, 256):
                    rows = slice(src * hold + lo, src * hold + lo + 256)
                    x_t[:, rows] = jnp.transpose(tok[src, lo : lo + 256, :])
                    de_t[:, rows] = jnp.transpose(dy[src, lo : lo + 256, :])

    wg[:half, :] = g_own[...]
    wg[half:, :] = g_oth[...]
    wu[:half, :] = u_own[...]
    wu[half:, :] = u_oth[...]

    @pl.when(i < steps // 2)
    def _():
        wd[...] = d_own[...]

    @pl.when(i >= steps // 2)
    def _():
        wd[...] = d_oth[...]

    def piece(j, first):
        rows = pl.ds(pl.multiple_of(j * chunk, chunk), chunk)
        if routed:
            x, de = x_s[rows, :], de_s[rows, :]
        else:
            per = length // chunk
            inner = pl.ds(pl.multiple_of((j % per) * chunk, chunk), chunk)
            x, de = tok[j // per, inner, :], dy[j // per, inner, :]
        g = nn(x, wg[...])
        u = nn(x, wu[...])
        dh = nt(de, wd[...])
        s = 1.0 / (1.0 + jnp.exp(-g))
        act = g * s
        hid = (act * u).astype(BF)
        du = (dh * act).astype(BF)
        dg = (dh * u * s * (1.0 + g * (1.0 - s))).astype(BF)
        hid_s[rows, :] = hid
        dg_s[rows, :] = dg
        du_s[rows, :] = du
        y = nn(hid, wd[...])
        dx = nt(dg, wg[...]) + nt(du, wu[...])
        if first:
            y_acc[rows, :] = y
            dx_acc[rows, :] = dx
        else:
            y_acc[rows, :] = y_acc[rows, :] + y
            dx_acc[rows, :] = dx_acc[rows, :] + dx

    @pl.when(i == 0)
    def _():
        @pl.loop(0, rows_all // chunk)
        def _(j):
            piece(j, True)

    @pl.when(i > 0)
    def _():
        @pl.loop(0, rows_all // chunk)
        def _(j):
            piece(j, False)

    gg = nn(x_t[...], dg_s[...])
    kg_o[...] = gg[:half, :].astype(BF)
    sg_o[...] = gg[half:, :].astype(BF)
    gu = nn(x_t[...], du_s[...])
    ku_o[...] = gu[:half, :].astype(BF)
    su_o[...] = gu[half:, :].astype(BF)
    gd = jnp.transpose(nn(de_t[...], hid_s[...])).astype(BF)

    @pl.when(i < steps // 2)
    def _():
        kd_o[...] = gd

    @pl.when(i >= steps // 2)
    def _():
        sd_o[...] = gd

    @pl.when(i == steps - 1)
    def _():
        for src in range(srcs):
            if routed:
                total = jnp.zeros((1, length), F32)
                for lo in range(0, hold, tile):
                    rows = slice(src * hold + lo, src * hold + lo + tile)
                    y = y_acc[rows, :]
                    dgate = jnp.sum(dys[rows, :].astype(F32) * y, axis=1, keepdims=True)
                    slot = lax.broadcasted_iota(jnp.int32, (tile, length), 0) + lo
                    mine = slot == slot_row[src : src + 1, :]
                    total = total + jnp.sum(jnp.where(mine, dgate, 0.0), axis=0, keepdims=True)
                    x_s[rows, :] = (y * gate_s[rows, 0:1]).astype(BF)
                    de_s[rows, :] = dx_acc[rows, :].astype(BF)
                dgate_o[src : src + 1, :] = total
                held = slice(src * hold, (src + 1) * hold)
                for lo in range(0, length, tile):
                    slot = lax.broadcasted_iota(jnp.int32, (tile, hold), 1)
                    mine = slot == slot_col[src * length + lo : src * length + lo + tile, :]
                    pick = jnp.where(mine, 1.0, 0.0).astype(BF)
                    out_o[src, lo : lo + tile, :] = nn(pick, x_s[held, :]).astype(BF)
                    dx_o[src, lo : lo + tile, :] = nn(pick, de_s[held, :]).astype(BF)
            else:
                held = slice(src * hold, (src + 1) * hold)
                out_o[src] = y_acc[held, :].astype(BF)
                dx_o[src] = dx_acc[held, :].astype(BF)


def ffn(where, tok, dy, gate, up, down, gate_oth, up_oth, down_oth, route=None):
    routed = route is not None
    srcs, length = tok.shape[0], tok.shape[1]
    block = 512
    half = D // 2
    if routed:
        total_cols = gate_oth.shape[1]
        steps = total_cols // block
        rows_all = srcs * CAP
        chunk = 256
    else:
        total_cols = gate_oth.shape[1]
        steps = total_cols // block
        rows_all = srcs * length
        chunk = 256
    per = steps // 2

    def compact(i, w):
        return jnp.where(i < per, w[0] * per + i, (1 - w[0]) * per + i - per)

    if routed:
        gate_spec = pl.BlockSpec((None, half, block), lambda i, w: (w[2], 0, compact(i, w)))
        down_spec = pl.BlockSpec((None, block, D), lambda i, w: (w[2], jnp.minimum(i, per - 1), 0))
    else:
        cores = gate.shape[1] // total_cols
        gate_spec = pl.BlockSpec((half, block), lambda i, w: (0, compact(i, w) * cores + w[1]))
        down_spec = pl.BlockSpec((block, D), lambda i, w: (w[1], 0))
    gate_oth_spec = pl.BlockSpec((half, block), lambda i, w: (0, compact(i, w)))
    first_half = pl.BlockSpec((block, D), lambda i, w: (jnp.minimum(i, per - 1), 0))
    last_half = pl.BlockSpec((block, D), lambda i, w: (jnp.maximum(i - per, 0), 0))
    in_specs = [resident((srcs, length, D)), resident((srcs, length, D))]
    operands = [tok, dy]
    if routed:
        slot_row, slot_col, gate_row = route
        in_specs += [resident(slot_row.shape), resident(slot_col.shape), resident(gate_row.shape)]
        operands += [slot_row, slot_col, gate_row]
    in_specs += [gate_spec, gate_oth_spec, gate_spec, gate_oth_spec, down_spec, last_half]
    operands += [gate, gate_oth, up, up_oth, down, down_oth]
    wide = jax.ShapeDtypeStruct((srcs, length, D), BF)
    out_specs = [resident((srcs, length, D)), resident((srcs, length, D))]
    out_shape = [wide, wide]
    if routed:
        out_specs.append(resident((srcs, length)))
        out_shape.append(jax.ShapeDtypeStruct((srcs, length), F32))
    col_grad = jax.ShapeDtypeStruct((half, total_cols), BF)
    row_grad = jax.ShapeDtypeStruct((total_cols // 2, D), BF)
    out_specs += [gate_oth_spec] * 4 + [first_half, last_half]
    out_shape += [col_grad] * 4 + [row_grad] * 2
    scratch = [
        pltpu.VMEM((D, block), BF),
        pltpu.VMEM((D, block), BF),
        pltpu.VMEM((block, D), BF),
        pltpu.VMEM((rows_all, D), F32),
        pltpu.VMEM((rows_all, D), F32),
        pltpu.VMEM((rows_all, block), BF),
        pltpu.VMEM((rows_all, block), BF),
        pltpu.VMEM((rows_all, block), BF),
        pltpu.VMEM((D, rows_all), BF),
        pltpu.VMEM((D, rows_all), BF),
    ]
    if routed:
        scratch += [
            pltpu.VMEM((rows_all, D), BF),
            pltpu.VMEM((rows_all, D), BF),
            pltpu.VMEM((rows_all, D), BF),
            pltpu.VMEM((rows_all, 128), F32),
        ]
    flops = 9 * 2 * rows_all * D * block * steps
    return pl.pallas_call(
        functools.partial(ffn_body, routed, steps, chunk),
        grid_spec=pltpu.PrefetchScalarGridSpec(
            num_scalar_prefetch=1,
            grid=(steps,),
            in_specs=in_specs,
            out_specs=out_specs,
            scratch_shapes=scratch,
        ),
        out_shape=out_shape,
        compiler_params=pltpu.CompilerParams(vmem_limit_bytes=60 * MIB),
        cost_estimate=pl.CostEstimate(flops=flops, transcendentals=0, bytes_accessed=20 * MIB),
        name="ffn_routed" if routed else "ffn_shared",
    )(where, *operands)


def on_device(
    tokens,
    routes,
    pic_block,
    norm1_gain,
    w_query,
    w_key,
    w_value,
    w_out,
    norm2_gain,
    router,
    expert_gate,
    expert_up,
    expert_down,
    shared_gate,
    shared_up,
    shared_down,
    cotangent,
):
    reps = lax.axis_size("rep")
    shards = lax.axis_size("shard")
    rep = lax.axis_index("rep")
    shard = lax.axis_index("shard")
    core = rep % 2
    length = tokens.shape[0]
    half = D // 2
    experts = router.shape[1]

    def swap(value, rep_bit, shard_bit):
        perm = [
            (r * shards + s, (r ^ rep_bit) * shards + (s ^ shard_bit))
            for r in range(reps)
            for s in range(shards)
        ]
        return lax.ppermute(value, ALL, perm)

    def over_core(value):
        return swap(value, 1, 0)

    def over_x(value):
        return swap(value, 0, 1)

    def in_order(index, mine, theirs, axis):
        return jnp.where(
            index == 0,
            jnp.concatenate([mine, theirs], axis=axis),
            jnp.concatenate([theirs, mine], axis=axis),
        )

    extra = jnp.concatenate([norm1_gain[:, None], norm2_gain[:, None], router], axis=1)
    extra = jnp.pad(extra, ((0, 0), (0, 256 - extra.shape[1])))
    small = jnp.concatenate([w_query, w_key, w_value, w_out, extra], axis=1)
    width = small.shape[1] // 2
    got = over_x(lax.dynamic_slice_in_dim(small, core * width, width, axis=1))
    small_oth = in_order(core, got, over_core(got), 1)
    small_full = in_order(shard, small, small_oth, 0)
    wqkv = small_full[:, : 3 * D].reshape(D, 3, PAIRS, PAIR).transpose(0, 2, 1, 3).reshape(D, 3 * D)
    wout = small_full[:, 3 * D : 4 * D]
    gain_one = small_full[:, 4 * D].astype(F32).reshape(1, D)
    gain_two = small_full[:, 4 * D + 1].astype(F32).reshape(1, D)
    router_t = jnp.transpose(small_full[:, 4 * D + 2 : 4 * D + 2 + experts])
    router_t8 = jnp.pad(router_t, ((0, 8 - experts), (0, 0)))
    router_t128 = jnp.pad(router_t, ((0, 128 - experts), (0, 0)))

    def later(value, after):
        return lax.optimization_barrier((value, after))[0]

    def shared_cols(weight):
        return jnp.concatenate(
            [
                lax.dynamic_slice_in_dim(weight, s * 1024 + core * 512, 512, axis=1)
                for s in range(shards)
            ],
            axis=1,
        )

    shared_send = [
        shared_cols(shared_gate),
        shared_cols(shared_up),
        lax.dynamic_slice_in_dim(shared_down, core * 512, 512, axis=0),
    ]
    shared_oth = [over_x(later(v, got)) for v in shared_send]
    per_core = experts // 2
    expert_oth = []
    previous = shared_oth[0]
    for j in range(per_core):
        sends = [
            lax.dynamic_index_in_dim(weight, core * per_core + j, 0, keepdims=False)
            for weight in (expert_gate, expert_up, expert_down)
        ]
        gots = [over_x(later(v, previous)) for v in sends]
        previous = gots[0]
        expert_oth.append(gots)

    def slot_tables(picks):
        expert_ids = jnp.arange(8)[:, None, None]
        picked = jnp.any(picks.T[None] == expert_ids, axis=1)
        earlier = jnp.arange(length)[:, None] < jnp.arange(length)[None, :]
        rank = jnp.dot(picked.astype(BF), earlier.astype(BF), preferred_element_type=F32)
        return jnp.where(picked, rank.astype(jnp.int32), -1)

    routes_oth = over_core(routes)
    slots = jnp.stack([slot_tables(routes), slot_tables(routes_oth)])
    dy_both = jnp.stack([cotangent, over_core(cotangent)])
    tables = rotary_tables(length)
    routes_t = jnp.pad(routes.T, ((0, 6), (0, 0)))

    q, k, v, mixed, lse = attend_forward(pic_block, tokens, gain_one, wqkv, tables)
    shard_s = shard.astype(jnp.int32).reshape(1)
    resid, n2, n2p, comb = middle(shard_s, tokens, mixed, wout, gain_two, router_t8, routes_t)
    n2_both = jnp.stack([n2p, over_core(n2p)])
    combs = jnp.stack([comb, over_core(comb)])

    def where_of(expert):
        return jnp.stack([shard, core, expert]).astype(jnp.int32)

    res = ffn(where_of(core), n2_both, dy_both, shared_gate, shared_up, shared_down, *shared_oth)
    outs, dxs, grads = [res[0]], [res[1]], [res[2:]]
    dgates = []
    for j in range(per_core):
        expert = core * per_core + j
        slot_row = lax.dynamic_index_in_dim(slots, expert, 1, keepdims=False)
        gate_row = lax.dynamic_index_in_dim(combs, expert, 1, keepdims=False)
        route = (slot_row, slot_row.reshape(-1, 1), gate_row)
        res = ffn(
            where_of(expert), n2_both, dy_both, expert_gate, expert_up, expert_down,
            *expert_oth[j], route=route,
        )
        outs.append(res[0])
        dxs.append(res[1])
        dgates.append(res[2])
        grads.append(res[3:])
    out_parts, dx_parts = [], []
    for part in outs:
        out_parts += [part, over_core(part[1])]
    for part in dxs:
        dx_parts += [part, over_core(part[1])]
    dgates = jnp.stack(dgates)
    dgate = in_order(core, dgates[:, 0], over_core(dgates[:, 1]), 0)
    comb_e = comb[:experts]
    dlog_t = (comb_e * (dgate - jnp.sum(comb_e * dgate, axis=0, keepdims=True))).astype(BF)
    dlog = jnp.pad(dlog_t.T, ((0, 0), (0, 128 - experts)))
    output, d_resid, d_low, ggain_two = join(
        shard_s, cotangent, resid, gain_two, dlog, router_t128, out_parts, dx_parts
    )
    grad_router = jnp.dot(dlog_t, n2, preferred_element_type=F32)
    gqkv, gout, input_grad, ggain_one = attend_backward(
        pic_block, tokens, gain_one, wqkv, wout, tables, q, k, v, mixed, lse, d_low, d_resid
    )

    groups = [[r for r in range(reps) if r % 2 == c] for c in range(2)]

    def reduce_rep(value):
        piece = lax.psum_scatter(
            value, "rep", scatter_dimension=0, tiled=True, axis_index_groups=groups
        )
        return lax.all_gather(piece, "rep", axis=0, tiled=True, axis_index_groups=groups)

    def summed(keep, send):
        return (keep.astype(F32) + over_x(send).astype(F32)).astype(BF)

    finals = []
    for keep_g, send_g, keep_u, send_u, keep_d, send_d in grads:
        trio = []
        for keep, send in ((keep_g, send_g), (keep_u, send_u), (keep_d, send_d)):
            mine = reduce_rep(summed(keep, send))
            trio.append((mine, over_core(mine)))
        finals.append(trio)

    def shared_out(mine, theirs, axis):
        blocks = mine.shape[axis] // 512
        parts = []
        for b in range(blocks):
            cut = functools.partial(lax.slice_in_dim, start_index=b * 512, limit_index=(b + 1) * 512, axis=axis)
            parts.append(in_order(core, cut(mine), cut(theirs), axis))
        return jnp.concatenate(parts, axis=axis).astype(F32)

    shared_grads = [
        shared_out(*finals[0][0], 1),
        shared_out(*finals[0][1], 1),
        shared_out(*finals[0][2], 0),
    ]
    expert_grads = []
    for m in range(3):
        mine = jnp.stack([finals[1 + j][m][0] for j in range(per_core)])
        theirs = jnp.stack([finals[1 + j][m][1] for j in range(per_core)])
        expert_grads.append(in_order(core, mine, theirs, 0).astype(F32))

    extra_grad = jnp.concatenate([ggain_one, ggain_two, grad_router], axis=0).astype(BF)
    extra_grad = jnp.pad(extra_grad.T, ((0, 0), (0, 128 - extra_grad.shape[0])))
    tail = jnp.concatenate([gqkv, gout, extra_grad], axis=1)
    tail = tail.reshape(shards, reps, half // reps, tail.shape[1]).transpose(1, 0, 2, 3)
    tail = tail.reshape(D, -1)
    piece = lax.psum_scatter(tail, ALL, scatter_dimension=0, tiled=True)
    full = lax.all_gather(piece, "rep", axis=0, tiled=True).astype(F32)
    gq = full[:, : 3 * D].reshape(half, PAIRS, 3, PAIR).transpose(2, 0, 1, 3).reshape(3, half, D)
    g_out = full[:, 3 * D : 4 * D]
    return (
        output,
        input_grad,
        full[:, 4 * D],
        gq[0],
        gq[1],
        gq[2],
        g_out,
        full[:, 4 * D + 1],
        full[:, 4 * D + 2 : 4 * D + 2 + experts],
        expert_grads[0],
        expert_grads[1],
        expert_grads[2],
        shared_grads[0],
        shared_grads[1],
        shared_grads[2],
    )


def solution(mesh):
    both = P(("rep", "shard"), None)
    rows = P("shard", None)
    vec = P("shard")
    mid = P(None, "shard", None)
    return jax.shard_map(
        on_device,
        mesh=mesh,
        in_specs=(
            both, both, P(("rep", "shard")),
            vec, rows, rows, rows, rows, vec, rows, mid, mid, mid, rows, rows, rows,
            both,
        ),
        out_specs=(both, both, vec, rows, rows, rows, rows, vec, rows, mid, mid, mid, rows, rows, rows),
        check_vma=False,
    )
```

time: 5720 us -> 1520 us (0.27); the launches traced: 5650 us -> 1520 us
  local copies, waits for them, and re-layouts: 2160 us -> 87 us
  waiting for transfers between devices: 2670 us -> 933 us
  matrix products: 584 us -> 2.5 us
  Pallas kernels: 0 us -> 277 us
  other arithmetic: 206 us -> 80.3 us
  blocking collectives: 14 us -> 99.9 us
    unnamed x14 -> x18, waiting for transfers between devices: 2270 us -> 109 us
    unnamed x324 -> x99, local copies, waits for them, and re-layouts: 1590 us -> 18.2 us
    dot_general x45 -> x3, matrix products: 584 us -> 2.5 us  [the longest x1 1.88 us: on_device(): grad_router = jnp.dot(dlog_t, n2, preferred_element_type=F32)]
    ppermute x0 -> x40, waiting for transfers between devices: none -> 478 us  [swap(): return lax.ppermute(value, ALL, perm)]
    reshape x27 -> x4, local copies, waits for them, and re-layouts: 318 us -> 11 us  [the longest x1 5.73 us: on_device(): small_full[:, :3 * D].reshape(D, 3, PAIRS, PAIR).transpose(0, 2, 1, 3)]
    pallas_call x0 -> x7, Pallas kernels: none -> 277 us  [the longest x3 176 us: ffn(): pl.pallas_call(functools.partial(ffn_body, routed, steps, chunk), grid_sp...]
    all_gather x10 -> x7, waiting for transfers between devices: 396 us -> 248 us  [the longest x6 230 us: reduce_rep(): lax.all_gather(piece, 'rep', axis=0, tiled=True, axis_index_groups=groups)]
    transpose x1 -> x0, other arithmetic: 124 us -> none  [on_device(): ordered = jnp.transpose(ordered, (1, 0, 2)).reshape(-1)]
  transfers between devices with their start and end apart: 12 -> 57, of which waited for: 6 -> 29; matrix products, arithmetic and copies ran while one was open for 5% -> 9% of each run, Pallas kernels for 0% -> 14%
where the time goes in v1:
time: 1520 us
  waiting for transfers between devices  933 us (61%)
  Pallas kernels  277 us (18%)
  blocking collectives  99.9 us (7%)
  local copies, waits for them, and re-layouts  87 us (6%)
  other arithmetic  80.3 us (5%)
  starting transfers between devices  21 us (1%)
  between operations  15.7 us (1%)
    ppermute x40, waiting for transfers between devices, swap(): return lax.ppermute(value, ALL, perm)  478 us
    all_gather x6, waiting for transfers between devices, reduce_rep(): lax.all_gather(piece, 'rep', axis=0, tiled=True, axis_index_groups=groups)  230 us
    pallas_call x3, Pallas kernels, ffn(): pl.pallas_call(functools.partial(ffn_body, routed, steps, chunk), grid_sp...  176 us
    unnamed x18, waiting for transfers between devices  109 us
    all_gather x3, blocking collectives, reduce_rep(): lax.all_gather(piece, 'rep', axis=0, tiled=True, axis_index_groups=groups)  99.9 us
    reduce_scatter x9, waiting for transfers between devices, reduce_rep(): lax.psum_scatter(value, 'rep', scatter_dimension=0, tiled=True, axis_inde...  96.7 us
    pallas_call x1, Pallas kernels, attend_backward(): pl.pallas_call(attend_backward_body, grid=(PAIRS,), in_specs=[pl.BlockSpe...  56.3 us
    pallas_call x1, Pallas kernels, attend_forward(): pl.pallas_call(attend_forward_body, grid=(PAIRS,), in_specs=[pl.BlockSpec...  30.5 us
  transfers between devices with their start and end apart: 57, of which 29 were waited for; matrix products, arithmetic and copies ran while one was open for 9% of the time, Pallas kernels for 14%

profile of v1, /device:TPU:0, one launch (start us, length us, event | category | flops | bytes accessed | tf_op | source)
XLA Modules:
  0.0 1516.1 jit_solution(8963705377027282495)
XLA Ops:
  17.3 27.1 %collective-permute-done = bf16[384,1664]{1,0:T(8,128)(2,1)} collective-permute-done((bf16[384,1664]{1,0:T(8,128)(2,1)}, bf16[384,1664]{1,0:T(8,128)(2,1)}, u32[]{:S(2)}, u32[]{:S(2)}) %collective-permute-start) | collective-permute-done | bytes 1277984 | tf_op jit(solution)/shard_map/ppermute | solution.py:658
  50.5 4.2 dynamic-slice_bitcast_fusion.5
  66.8 5.9 copy.167
  72.7 4.1 copy.168
  76.8 5.7 copy.169.wqkv
  85.8 30.5 %attend_forward.1 = (bf16[1024,768]{1,0:T(8,128)(2,1)S(1)}, bf16[1024,768]{1,0:T(8,128)(2,1)S(1)}, bf16[1024,768]{1,0:T(8,128)(2,1)}, bf16[1024,768]{1,0:T(8,128)(2,1)}, f32[6,8,1024]{2,1,0:T(8,128)S(1)}) custom-call(s32[1]{0:T(128)S(6)} %copy.211.pic, bf16[1024,768]{1,0:T(8,128)(2,1)} %tok.5, f32[1,768]{1,0:T(1,128)S(1)} %reshape.106.gain, ...), custom_call_target="tpu_custom_call" | custom-call | tf_op jit(solution)/shard_map/attend_forward/pallas_call | solution.py:111
  123.5 5.1 dynamic-slice_bitcast_fusion.3
  134.3 3.8 pad_maximum_fusion.1.dy
  140.7 25.6 %collective-permute-done.7.refs_4_ = bf16[384,2048]{1,0:T(8,128)(2,1)} collective-permute-done((bf16[384,2048]{1,0:T(8,128)(2,1)}, bf16[384,2048]{1,0:T(8,128)(2,1)}, u32[]{:S(2)}, u32[]{:S(2)}) %collective-permute-start.7) | collective-permute-done | bytes 1572896 | tf_op jit(solution)/shard_map/ppermute | solution.py:658
  166.3 33.7 %collective-permute-done.8.refs_6_ = bf16[384,2048]{1,0:T(8,128)(2,1)} collective-permute-done((bf16[384,2048]{1,0:T(8,128)(2,1)}, bf16[384,2048]{1,0:T(8,128)(2,1)}, u32[]{:S(2)}, u32[]{:S(2)}) %collective-permute-start.8) | collective-permute-done | bytes 1572896 | tf_op jit(solution)/shard_map/ppermute | solution.py:658
  200.0 33.0 %collective-permute-done.9.refs_8_ = bf16[1024,768]{1,0:T(8,128)(2,1)} collective-permute-done((bf16[1024,768]{1,0:T(8,128)(2,1)}, bf16[1024,768]{1,0:T(8,128)(2,1)}, u32[]{:S(2)}, u32[]{:S(2)}) %collective-permute-start.9) | collective-permute-done | bytes 1572896 | tf_op jit(solution)/shard_map/ppermute | solution.py:658
  233.0 65.2 %ffn_routed.2 = (bf16[2,1024,768]{2,1,0:T(8,128)(2,1)}, bf16[2,1024,768]{2,1,0:T(8,128)(2,1)}, f32[2,1024]{1,0:T(2,128)}, bf16[384,2048]{1,0:T(8,128)(2,1)}, bf1...) custom-call(s32[3]{0:T(128)} %pad_add_fusion.where, ...), custom_call_target="tpu_custom_call" | custom-call | flops 36238786560 | bytes 20971520 | tf_op jit(solution)/shard_map/ffn_routed/pallas_call | solution.py:608
  305.5 30.3 %collective-permute-done.22 = bf16[384,2048]{1,0:T(8,128)(2,1)S(1)} collective-permute-done((bf16[384,2048]{1,0:T(8,128)(2,1)}, bf16[384,2048]{1,0:T(8,128)(2,1)S(1)}, u32[]{:S(2)}, u32[]{:S(2)}) %collective-permute-start.22) | collective-permute-done | bytes 1572896 | tf_op jit(solution)/shard_map/ppermute | solution.py:658
  339.1 30.6 %collective-permute-done.10.refs_4_ = bf16[384,2048]{1,0:T(8,128)(2,1)} collective-permute-done((bf16[384,2048]{1,0:T(8,128)(2,1)}, bf16[384,2048]{1,0:T(8,128)(2,1)}, u32[]{:S(2)}, u32[]{:S(2)}) %collective-permute-start.10) | collective-permute-done | bytes 1572896 | tf_op jit(solution)/shard_map/ppermute | solution.py:658
  369.6 33.7 %collective-permute-done.11.refs_6_ = bf16[384,2048]{1,0:T(8,128)(2,1)} collective-permute-done((bf16[384,2048]{1,0:T(8,128)(2,1)S(1)}, bf16[384,2048]{1,0:T(8,128)(2,1)}, u32[]{:S(2)}, u32[]{:S(2)}) %collective-permute-start.11) | collective-permute-done | bytes 1572896 | tf_op jit(solution)/shard_map/ppermute | solution.py:658
  403.3 32.1 %collective-permute-done.12.refs_8_ = bf16[1024,768]{1,0:T(8,128)(2,1)} collective-permute-done((bf16[1024,768]{1,0:T(8,128)(2,1)}, bf16[1024,768]{1,0:T(8,128)(2,1)}, u32[]{:S(2)}, u32[]{:S(2)}) %collective-permute-start.12) | collective-permute-done | bytes 1572896 | tf_op jit(solution)/shard_map/ppermute | solution.py:658
  435.4 65.2 %ffn_routed.3 = (bf16[2,1024,768]{2,1,0:T(8,128)(2,1)}, bf16[2,1024,768]{2,1,0:T(8,128)(2,1)}, f32[2,1024]{1,0:T(2,128)}, bf16[384,2048]{1,0:T(8,128)(2,1)}, bf1...) custom-call(s32[3]{0:T(128)} %pad_add_fusion.2.where, ...), custom_call_target="tpu_custom_call" | custom-call | flops 36238786560 | bytes 20971520 | tf_op jit(solution)/shard_map/ffn_routed/pallas_call | solution.py:608
  501.0 34.6 %collective-permute-done.23 = bf16[384,2048]{1,0:T(8,128)(2,1)S(1)} collective-permute-done((bf16[384,2048]{1,0:T(8,128)(2,1)}, bf16[384,2048]{1,0:T(8,128)(2,1)S(1)}, u32[]{:S(2)}, u32[]{:S(2)}) %collective-permute-start.23) | collective-permute-done | bytes 1572896 | tf_op jit(solution)/shard_map/ppermute | solution.py:658
  539.4 33.5 %collective-permute-done.26 = bf16[384,2048]{1,0:T(8,128)(2,1)S(1)} collective-permute-done((bf16[384,2048]{1,0:T(8,128)(2,1)S(1)}, bf16[384,2048]{1,0:T(8,128)(2,1)S(1)}, u32[]{:S(2)}, u32[]{:S(2)}) %collective-permute-start.26) | collective-permute-done | bytes 1572896 | tf_op jit(solution)/shard_map/ppermute | solution.py:658
  575.2 32.8 %collective-permute-done.27 = bf16[384,2048]{1,0:T(8,128)(2,1)S(1)} collective-permute-done((bf16[384,2048]{1,0:T(8,128)(2,1)}, bf16[384,2048]{1,0:T(8,128)(2,1)S(1)}, u32[]{:S(2)}, u32[]{:S(2)}) %collective-permute-start.27) | collective-permute-done | bytes 1572896 | tf_op jit(solution)/shard_map/ppermute | solution.py:658
  610.4 32.2 %collective-permute-done.30 = bf16[1024,768]{1,0:T(8,128)(2,1)S(1)} collective-permute-done((bf16[1024,768]{1,0:T(8,128)(2,1)}, bf16[1024,768]{1,0:T(8,128)(2,1)S(1)}, u32[]{:S(2)}, u32[]{:S(2)}) %collective-permute-start.30) | collective-permute-done | bytes 1572896 | tf_op jit(solution)/shard_map/ppermute | solution.py:658
  650.8 31.1 %collective-permute-done.31 = bf16[1024,768]{1,0:T(8,128)(2,1)S(1)} collective-permute-done((bf16[1024,768]{1,0:T(8,128)(2,1)}, bf16[1024,768]{1,0:T(8,128)(2,1)S(1)}, u32[]{:S(2)}, u32[]{:S(2)}) %collective-permute-start.31) | collective-permute-done | bytes 1572896 | tf_op jit(solution)/shard_map/ppermute | solution.py:658
  683.6 15.3 %collective-permute-done.14.refs_3_ = bf16[384,1024]{1,0:T(8,128)(2,1)} collective-permute-done((bf16[384,1024]{1,0:T(8,128)(2,1)}, bf16[384,1024]{1,0:T(8,128)(2,1)}, u32[]{:S(2)}, u32[]{:S(2)}) %collective-permute-start.14) | collective-permute-done | bytes 786464 | tf_op jit(solution)/shard_map/ppermute | solution.py:658
  698.9 10.9 collective-permute-done.15.refs_5_
  709.8 45.8 %ffn_shared.1 = (bf16[2,1024,768]{2,1,0:T(8,128)(2,1)}, bf16[2,1024,768]{2,1,0:T(8,128)(2,1)}, bf16[384,1024]{1,0:T(8,128)(2,1)}, bf16[384,1024]{1,0:T(8,128)(2,...) custom-call(s32[3]{0:T(128)} %pad_add_fusion.3.where, ...), custom_call_target="tpu_custom_call" | custom-call | flops 28991029248 | bytes 20971520 | tf_op jit(solution)/shard_map/ffn_shared/pallas_call | solution.py:608
  756.3 14.8 collective-permute-done.34
  774.2 15.3 %collective-permute-done.36 = bf16[384,1024]{1,0:T(8,128)(2,1)S(1)} collective-permute-done((bf16[384,1024]{1,0:T(8,128)(2,1)S(1)}, bf16[384,1024]{1,0:T(8,128)(2,1)S(1)}, u32[]{:S(2)}, u32[]{:S(2)}) %collective-permute-start.36) | collective-permute-done | bytes 786464 | tf_op jit(solution)/shard_map/ppermute | solution.py:658
  791.7 11.5 collective-permute-done.38
  828.9 10.5 join.1
  840.5 56.3 %attend_backward.1 = (bf16[768,2304]{1,0:T(8,128)(2,1)}, bf16[768,768]{1,0:T(8,128)(2,1)}, f32[1024,768]{1,0:T(8,128)}, f32[1,768]{1,0:T(1,128)}) custom-call(s32[1]{0:T(128)S(6)} %copy.211.pic, bf16[1024,768]{1,0:T(8,128)(2,1)} %tok.5, f32[1,768]{1,0:T(1,128)} %copy-done.12, bf16[768,2304]{1,0:T(8,128)(2,1)} %copy.169.wqkv, bf16[768,768]{1,0:T(8,128)(2,1)} %copy-done.1, ...), custom_call_target="tpu_custom_call" | custom-call | tf_op jit(solution)/shard_map/attend_backward/pallas_call | solution.py:234
  906.0 32.7 %reduce-scatter.25.cloned.1.call-done = bf16[48,1024]{1,0:T(8,128)(2,1)} async-done(((bf16[384,1024]{1,0:T(8,128)(2,1)}), bf16[48,1024]{1,0:T(8,128)(2,1)}) %reduce-scatter.25.cloned.1.call-update) | async-done | bytes 98320 | tf_op jit(solution)/shard_map/reduce_scatter | solution.py:777
  938.7 33.3 %all_gather.37 = bf16[384,1024]{1,0:T(8,128)(2,1)S(1)} all-gather(bf16[48,1024]{1,0:T(8,128)(2,1)} %reduce-scatter.25.cloned.1.call-done), channel_id=1, replica_groups={{0,4,8,12,16,20,24,28},{2,6,10,14,18,22,26,30},{1,5,9,13,17,21,25,29},{..., dimensions={0}, use_global_device_ids=true | all-gather | bytes 884736 | tf_op jit(solution)/shard_map/all_gather | solution.py:780
  972.0 32.4 %reduce-scatter.27.cloned.1.call-done = bf16[48,1024]{1,0:T(8,128)(2,1)} async-done(((bf16[384,1024]{1,0:T(8,128)(2,1)}), bf16[48,1024]{1,0:T(8,128)(2,1)}) %reduce-scatter.27.cloned.1.call-update) | async-done | bytes 98320 | tf_op jit(solution)/shard_map/reduce_scatter | solution.py:777
  1004.4 33.5 %all_gather.38 = bf16[384,1024]{1,0:T(8,128)(2,1)S(1)} all-gather(bf16[48,1024]{1,0:T(8,128)(2,1)} %reduce-scatter.27.cloned.1.call-done), channel_id=1, replica_groups={{0,4,8,12,16,20,24,28},{2,6,10,14,18,22,26,30},{1,5,9,13,17,21,25,29},{..., dimensions={0}, use_global_device_ids=true | all-gather | bytes 884736 | tf_op jit(solution)/shard_map/all_gather | solution.py:780
  1037.8 31.5 %reduce-scatter.29.cloned.1.call-done = bf16[64,768]{1,0:T(8,128)(2,1)} async-done(((bf16[512,768]{1,0:T(8,128)(2,1)}), bf16[64,768]{1,0:T(8,128)(2,1)}) %reduce-scatter.29.cloned.1.call-update) | async-done | bytes 98320 | tf_op jit(solution)/shard_map/reduce_scatter | solution.py:777
  1069.4 33.1 %all_gather.39 = bf16[512,768]{1,0:T(8,128)(2,1)S(1)} all-gather(bf16[64,768]{1,0:T(8,128)(2,1)} %reduce-scatter.29.cloned.1.call-done), channel_id=1, replica_groups={{0,4,8,12,16,20,24,28},{2,6,10,14,18,22,26,30},{1,5,9,13,17,21,25,29},{..., dimensions={0}, use_global_device_ids=true | all-gather | bytes 884736 | tf_op jit(solution)/shard_map/all_gather | solution.py:780
  1103.4 13.7 all-gather.10.cloned.1.call-done
  1117.1 45.5 %all-gather.12.cloned.1.call-done = bf16[384,2048]{1,0:T(8,128)(2,1)} async-done(((bf16[48,2048]{1,0:T(8,128)(2,1)}), bf16[384,2048]{1,0:T(8,128)(2,1)}) %all-gather.12.cloned.1.call-update) | async-done | bytes 1572880 | tf_op jit(solution)/shard_map/all_gather | solution.py:780
  1165.8 106.6 %reduce-scatter.31.cloned.1.call-done = bf16[24,3200]{1,0:T(8,128)(2,1)} async-done(((bf16[768,3200]{1,0:T(8,128)(2,1)}), bf16[24,3200]{1,0:T(8,128)(2,1)}) %reduce-scatter.31.cloned.1.call-update) | async-done | bytes 153616
  1279.9 37.8 %all-gather.14.cloned.1.call-done = bf16[384,2048]{1,0:T(8,128)(2,1)} async-done(((bf16[48,2048]{1,0:T(8,128)(2,1)}), bf16[384,2048]{1,0:T(8,128)(2,1)}) %all-gather.14.cloned.1.call-update) | async-done | bytes 1572880 | tf_op jit(solution)/shard_map/all_gather | solution.py:780
  1317.8 45.1 %all-gather.16.cloned.1.call-done = bf16[384,2048]{1,0:T(8,128)(2,1)} async-done(((bf16[48,2048]{1,0:T(8,128)(2,1)}), bf16[384,2048]{1,0:T(8,128)(2,1)}) %all-gather.16.cloned.1.call-update) | async-done | bytes 1572880 | tf_op jit(solution)/shard_map/all_gather | solution.py:780
  1365.4 42.5 %all-gather.18.cloned.1.call-done = bf16[1024,768]{1,0:T(8,128)(2,1)} async-done(((bf16[128,768]{1,0:T(8,128)(2,1)}), bf16[1024,768]{1,0:T(8,128)(2,1)}) %all-gather.18.cloned.1.call-update) | async-done | bytes 1572880 | tf_op jit(solution)/shard_map/all_gather | solution.py:780
  1407.9 45.1 %all-gather.20.cloned.1.call-done = bf16[1024,768]{1,0:T(8,128)(2,1)} async-done(((bf16[128,768]{1,0:T(8,128)(2,1)}), bf16[1024,768]{1,0:T(8,128)(2,1)}) %all-gather.20.cloned.1.call-update) | async-done | bytes 1572880 | tf_op jit(solution)/shard_map/all_gather | solution.py:780
  1453.0 8.8 fusion.1
  1461.8 8.8 fusion.2
  1470.6 7.4 fusion.3
  1478.0 18.5 %all-gather.8.cloned.1.call-done = bf16[384,3200]{1,0:T(8,128)(2,1)} async-done(((bf16[24,3200]{1,0:T(8,128)(2,1)}), bf16[384,3200]{1,0:T(8,128)(2,1)}) %all-gather.8.cloned.1.call-update) | async-done | bytes 2457616 | tf_op jit(solution)/shard_map/all_gather | solution.py:818
  1496.4 4.2 copy.182
  (291 shorter events, 139.6 us)
Async XLA Ops:
  7.2 798.3 %reduce-scatter.13.cloned.1.call-start = ((), (), s32[]{:S(2)}) async-start(), calls=%async_computation.11 | async-start | bytes 1769472 | tf_op jit(solution)/shard_map/reduce_scatter | solution.py:777
  13.2 31.3 %collective-permute-start = (bf16[384,1664]{1,0:T(8,128)(2,1)}, bf16[384,1664]{1,0:T(8,128)(2,1)}, u32[]{:S(2)}, u32[]{:S(2)}) collective-permute-start(bf16[384,1664]{1,0:T(8,128)(2,1)} %constant_dynamic-slice_fusion.5), channel_id=1, source_target_pairs={{0,1},{1,0},{2,3},{3,2},{4,5},{5,4},{6,7},{7,6},{8,9},{9,8},{10,11... | collective-permute-start | bytes 3833864 | tf_op jit(solution)/shard_map/ppermute | solution.py:658
  16.1 118.2 %collective-permute-start.3 = (bf16[1024,768]{1,0:T(8,128)(2,1)}, bf16[1024,768]{1,0:T(8,128)(2,1)}, u32[]{:S(2)}, u32[]{:S(2)}) collective-permute-start(bf16[1024,768]{1,0:T(8,128)(2,1)} %dy.1), channel_id=1, source_target_pairs={{0,2},{1,3},{2,0},{3,1},{4,6},{5,7},{6,4},{7,5},{8,10},{9,11},{10,... | collective-permute-start | bytes 4718600 | tf_op jit(solution)/shard_map/ppermute | solution.py:658
  16.1 114.7 %collective-permute-start.4 = (s32[1024,2]{0,1:T(2,128)S(1)}, s32[1024,2]{0,1:T(2,128)S(1)}, u32[]{:S(2)}, u32[]{:S(2)}) collective-permute-start(s32[1024,2]{0,1:T(2,128)S(1)} %copy-done.35), channel_id=1, source_target_pairs={{0,2},{1,3},{2,0},{3,1},{4,6},{5,7},{6,4},{7,5},{8,10},{9,11},{10,... | collective-permute-start | bytes 24584 | tf_op jit(solution)/shard_map/ppermute | solution.py:658
  56.8 71.9 %collective-permute-start.6 = (bf16[384,1024]{1,0:T(8,128)(2,1)}, bf16[384,1024]{1,0:T(8,128)(2,1)}, u32[]{:S(2)}, u32[]{:S(2)}) collective-permute-start(bf16[384,1024]{1,0:T(8,128)(2,1)} %pad_maximum_fusion.2), channel_id=1, source_target_pairs={{0,1},{1,0},{2,3},{3,2},{4,5},{5,4},{6,7},{7,6},{8,9},{9,8},{10,11... | collective-permute-start | bytes 2359304 | tf_op jit(solution)/shard_map/ppermute | solution.py:658
  123.3 15.5 %collective-permute-start.2 = (bf16[1024,768]{1,0:T(8,128)(2,1)S(1)}, bf16[1024,768]{1,0:T(8,128)(2,1)S(1)}, u32[]{:S(2)}, u32[]{:S(2)}) collective-permute-start(bf16[1024,768]{1,0:T(8,128)(2,1)S(1)} %get-tuple-element.70), channel_id=1, source_target_pairs={{0,2},{1,3},{2,0},{3,1},{4,6},{5,7},{6,4},{7,5},{8,10},{9,11},{10,... | collective-permute-start | bytes 4718600 | tf_op jit(solution)/shard_map/ppermute | solution.py:658
  128.7 37.6 %collective-permute-start.7 = (bf16[384,2048]{1,0:T(8,128)(2,1)}, bf16[384,2048]{1,0:T(8,128)(2,1)}, u32[]{:S(2)}, u32[]{:S(2)}) collective-permute-start(bf16[384,2048]{1,0:T(8,128)(2,1)} %get-tuple-element.72), channel_id=1, source_target_pairs={{0,1},{1,0},{2,3},{3,2},{4,5},{5,4},{6,7},{7,6},{8,9},{9,8},{10,11... | collective-permute-start | bytes 4718600 | tf_op jit(solution)/shard_map/ppermute | solution.py:658
  129.1 71.0 %collective-permute-start.8 = (bf16[384,2048]{1,0:T(8,128)(2,1)}, bf16[384,2048]{1,0:T(8,128)(2,1)}, u32[]{:S(2)}, u32[]{:S(2)}) collective-permute-start(bf16[384,2048]{1,0:T(8,128)(2,1)} %get-tuple-element.73), channel_id=1, source_target_pairs={{0,1},{1,0},{2,3},{3,2},{4,5},{5,4},{6,7},{7,6},{8,9},{9,8},{10,11... | collective-permute-start | bytes 4718600 | tf_op jit(solution)/shard_map/ppermute | solution.py:658
  130.8 102.2 %collective-permute-start.9 = (bf16[1024,768]{1,0:T(8,128)(2,1)}, bf16[1024,768]{1,0:T(8,128)(2,1)}, u32[]{:S(2)}, u32[]{:S(2)}) collective-permute-start(bf16[1024,768]{1,0:T(8,128)(2,1)} %get-tuple-element.74), channel_id=1, source_target_pairs={{0,1},{1,0},{2,3},{3,2},{4,5},{5,4},{6,7},{7,6},{8,9},{9,8},{10,11... | collective-permute-start | bytes 4718600 | tf_op jit(solution)/shard_map/ppermute | solution.py:658
  298.2 37.6 %collective-permute-start.22 = (bf16[384,2048]{1,0:T(8,128)(2,1)}, bf16[384,2048]{1,0:T(8,128)(2,1)S(1)}, u32[]{:S(2)}, u32[]{:S(2)}) collective-permute-start(bf16[384,2048]{1,0:T(8,128)(2,1)} %get-tuple-element.102), channel_id=1, source_target_pairs={{0,1},{1,0},{2,3},{3,2},{4,5},{5,4},{6,7},{7,6},{8,9},{9,8},{10,11... | collective-permute-start | bytes 4718600 | tf_op jit(solution)/shard_map/ppermute | solution.py:658
  298.6 71.0 %collective-permute-start.10 = (bf16[384,2048]{1,0:T(8,128)(2,1)}, bf16[384,2048]{1,0:T(8,128)(2,1)}, u32[]{:S(2)}, u32[]{:S(2)}) collective-permute-start(bf16[384,2048]{1,0:T(8,128)(2,1)} %get-tuple-element.76), channel_id=1, source_target_pairs={{0,1},{1,0},{2,3},{3,2},{4,5},{5,4},{6,7},{7,6},{8,9},{9,8},{10,11... | collective-permute-start | bytes 4718600 | tf_op jit(solution)/shard_map/ppermute | solution.py:658
  300.3 103.0 %collective-permute-start.11 = (bf16[384,2048]{1,0:T(8,128)(2,1)S(1)}, bf16[384,2048]{1,0:T(8,128)(2,1)}, u32[]{:S(2)}, u32[]{:S(2)}) collective-permute-start(bf16[384,2048]{1,0:T(8,128)(2,1)S(1)} %copy-done.23), channel_id=1, source_target_pairs={{0,1},{1,0},{2,3},{3,2},{4,5},{5,4},{6,7},{7,6},{8,9},{9,8},{10,11... | collective-permute-start | bytes 4718600 | tf_op jit(solution)/shard_map/ppermute | solution.py:658
  300.6 134.8 %collective-permute-start.12 = (bf16[1024,768]{1,0:T(8,128)(2,1)}, bf16[1024,768]{1,0:T(8,128)(2,1)}, u32[]{:S(2)}, u32[]{:S(2)}) collective-permute-start(bf16[1024,768]{1,0:T(8,128)(2,1)} %get-tuple-element.78), channel_id=1, source_target_pairs={{0,1},{1,0},{2,3},{3,2},{4,5},{5,4},{6,7},{7,6},{8,9},{9,8},{10,11... | collective-permute-start | bytes 4718600 | tf_op jit(solution)/shard_map/ppermute | solution.py:658
  339.0 474.9 %reduce-scatter.15.cloned.1.call-start = ((), (), s32[]{:S(2)}) async-start(), calls=%async_computation.13 | async-start | bytes 1769472 | tf_op jit(solution)/shard_map/reduce_scatter | solution.py:777
  500.6 35.0 %collective-permute-start.23 = (bf16[384,2048]{1,0:T(8,128)(2,1)}, bf16[384,2048]{1,0:T(8,128)(2,1)S(1)}, u32[]{:S(2)}, u32[]{:S(2)}) collective-permute-start(bf16[384,2048]{1,0:T(8,128)(2,1)} %get-tuple-element.104), channel_id=1, source_target_pairs={{0,1},{1,0},{2,3},{3,2},{4,5},{5,4},{6,7},{7,6},{8,9},{9,8},{10,11... | collective-permute-start | bytes 4718600 | tf_op jit(solution)/shard_map/ppermute | solution.py:658
  538.9 364.6 %reduce-scatter.17.cloned.1.call-start = ((), (), s32[]{:S(2)}) async-start(), calls=%async_computation.15 | async-start | bytes 1769472 | tf_op jit(solution)/shard_map/reduce_scatter | solution.py:777
  539.0 33.9 %collective-permute-start.26 = (bf16[384,2048]{1,0:T(8,128)(2,1)S(1)}, bf16[384,2048]{1,0:T(8,128)(2,1)S(1)}, u32[]{:S(2)}, u32[]{:S(2)}) collective-permute-start(bf16[384,2048]{1,0:T(8,128)(2,1)S(1)} %copy-done.38), channel_id=1, source_target_pairs={{0,1},{1,0},{2,3},{3,2},{4,5},{5,4},{6,7},{7,6},{8,9},{9,8},{10,11... | collective-permute-start | bytes 4718600 | tf_op jit(solution)/shard_map/ppermute | solution.py:658
  574.7 329.6 %reduce-scatter.19.cloned.1.call-start = ((), (), s32[]{:S(2)}) async-start(), calls=%async_computation.17 | async-start | bytes 1769472 | tf_op jit(solution)/shard_map/reduce_scatter | solution.py:777
  574.7 33.3 %collective-permute-start.27 = (bf16[384,2048]{1,0:T(8,128)(2,1)}, bf16[384,2048]{1,0:T(8,128)(2,1)S(1)}, u32[]{:S(2)}, u32[]{:S(2)}) collective-permute-start(bf16[384,2048]{1,0:T(8,128)(2,1)} %get-tuple-element.108), channel_id=1, source_target_pairs={{0,1},{1,0},{2,3},{3,2},{4,5},{5,4},{6,7},{7,6},{8,9},{9,8},{10,11... | collective-permute-start | bytes 4718600 | tf_op jit(solution)/shard_map/ppermute | solution.py:658
  609.8 295.1 %reduce-scatter.21.cloned.1.call-start = ((), (), s32[]{:S(2)}) async-start(), calls=%async_computation.19 | async-start | bytes 1769472 | tf_op jit(solution)/shard_map/reduce_scatter | solution.py:777
  609.9 32.7 %collective-permute-start.30 = (bf16[1024,768]{1,0:T(8,128)(2,1)}, bf16[1024,768]{1,0:T(8,128)(2,1)S(1)}, u32[]{:S(2)}, u32[]{:S(2)}) collective-permute-start(bf16[1024,768]{1,0:T(8,128)(2,1)} %get-tuple-element.110), channel_id=1, source_target_pairs={{0,1},{1,0},{2,3},{3,2},{4,5},{5,4},{6,7},{7,6},{8,9},{9,8},{10,11... | collective-permute-start | bytes 4718600 | tf_op jit(solution)/shard_map/ppermute | solution.py:658
  644.3 261.2 %reduce-scatter.23.cloned.1.call-start = ((), (), s32[]{:S(2)}) async-start(), calls=%async_computation.21 | async-start | bytes 1769472 | tf_op jit(solution)/shard_map/reduce_scatter | solution.py:777
  644.3 37.6 %collective-permute-start.31 = (bf16[1024,768]{1,0:T(8,128)(2,1)}, bf16[1024,768]{1,0:T(8,128)(2,1)S(1)}, u32[]{:S(2)}, u32[]{:S(2)}) collective-permute-start(bf16[1024,768]{1,0:T(8,128)(2,1)} %get-tuple-element.112), channel_id=1, source_target_pairs={{0,1},{1,0},{2,3},{3,2},{4,5},{5,4},{6,7},{7,6},{8,9},{9,8},{10,11... | collective-permute-start | bytes 4718600 | tf_op jit(solution)/shard_map/ppermute | solution.py:658
  648.2 50.7 %collective-permute-start.14 = (bf16[384,1024]{1,0:T(8,128)(2,1)}, bf16[384,1024]{1,0:T(8,128)(2,1)}, u32[]{:S(2)}, u32[]{:S(2)}) collective-permute-start(bf16[384,1024]{1,0:T(8,128)(2,1)} %pad_maximum_fusion.3), channel_id=1, source_target_pairs={{0,1},{1,0},{2,3},{3,2},{4,5},{5,4},{6,7},{7,6},{8,9},{9,8},{10,11... | collective-permute-start | bytes 2359304 | tf_op jit(solution)/shard_map/ppermute | solution.py:658
  649.7 60.1 %collective-permute-start.15 = (bf16[512,768]{1,0:T(8,128)(2,1)}, bf16[512,768]{1,0:T(8,128)(2,1)}, u32[]{:S(2)}, u32[]{:S(2)}) collective-permute-start(bf16[512,768]{1,0:T(8,128)(2,1)} %constant_dynamic-slice_fusion), channel_id=1, source_target_pairs={{0,1},{1,0},{2,3},{3,2},{4,5},{5,4},{6,7},{7,6},{8,9},{9,8},{10,11... | collective-permute-start | bytes 2359304 | tf_op jit(solution)/shard_map/ppermute | solution.py:658
  683.5 255.2 %reduce-scatter.25.cloned.1.call-start = ((), (), s32[]{:S(2)}) async-start(), calls=%async_computation.23 | async-start | bytes 884736 | tf_op jit(solution)/shard_map/reduce_scatter | solution.py:777
  773.4 231.0 %reduce-scatter.27.cloned.1.call-start = ((), (), s32[]{:S(2)}) async-start(), calls=%async_computation.24 | async-start | bytes 884736 | tf_op jit(solution)/shard_map/reduce_scatter | solution.py:777
  773.5 16.1 %collective-permute-start.36 = (bf16[384,1024]{1,0:T(8,128)(2,1)S(1)}, bf16[384,1024]{1,0:T(8,128)(2,1)S(1)}, u32[]{:S(2)}, u32[]{:S(2)}) collective-permute-start(bf16[384,1024]{1,0:T(8,128)(2,1)S(1)} %copy-done.39), channel_id=1, source_target_pairs={{0,1},{1,0},{2,3},{3,2},{4,5},{5,4},{6,7},{7,6},{8,9},{9,8},{10,11... | collective-permute-start | bytes 2359304 | tf_op jit(solution)/shard_map/ppermute | solution.py:658
  790.7 278.6 %reduce-scatter.29.cloned.1.call-start = ((), (), s32[]{:S(2)}) async-start(), calls=%async_computation.25 | async-start | bytes 884736 | tf_op jit(solution)/shard_map/reduce_scatter | solution.py:777
  805.5 311.6 %all-gather.10.cloned.1.call-start = ((), (), s32[]{:S(2)}) async-start(), calls=%async_computation.12 | async-start | bytes 1769472 | tf_op jit(solution)/shard_map/all_gather | solution.py:780
  806.1 356.5 %all-gather.12.cloned.1.call-start = ((), (), s32[]{:S(2)}) async-start(), calls=%async_computation.14 | async-start | bytes 1769472 | tf_op jit(solution)/shard_map/all_gather | solution.py:780
  810.3 18.6 %collective-permute-start.17 = (bf16[1024,768]{1,0:T(8,128)(2,1)}, bf16[1024,768]{1,0:T(8,128)(2,1)S(1)}, u32[]{:S(2)}, u32[]{:S(2)}) collective-permute-start(bf16[1024,768]{1,0:T(8,128)(2,1)} %slice_bitcast_fusion.4), channel_id=1, source_target_pairs={{0,2},{1,3},{2,0},{3,1},{4,6},{5,7},{6,4},{7,5},{8,10},{9,11},{10,... | collective-permute-start | bytes 4718600 | tf_op jit(solution)/shard_map/ppermute | solution.py:658
  811.9 16.9 %collective-permute-start.19 = (bf16[1024,768]{1,0:T(8,128)(2,1)}, bf16[1024,768]{1,0:T(8,128)(2,1)}, u32[]{:S(2)}, u32[]{:S(2)}) collective-permute-start(bf16[1024,768]{1,0:T(8,128)(2,1)} %slice_bitcast_fusion.2), channel_id=1, source_target_pairs={{0,2},{1,3},{2,0},{3,1},{4,6},{5,7},{6,4},{7,5},{8,10},{9,11},{10,... | collective-permute-start | bytes 4718600 | tf_op jit(solution)/shard_map/ppermute | solution.py:658
  814.0 458.4 %reduce-scatter.31.cloned.1.call-start = ((), (), s32[]{:S(2)}) async-start(), calls=%async_computation.26 | async-start | bytes 5068800
  903.5 414.3 %all-gather.14.cloned.1.call-start = ((), (), s32[]{:S(2)}) async-start(), calls=%async_computation.16 | async-start | bytes 1769472 | tf_op jit(solution)/shard_map/all_gather | solution.py:780
  904.3 458.6 %all-gather.16.cloned.1.call-start = ((), (), s32[]{:S(2)}) async-start(), calls=%async_computation.18 | async-start | bytes 1769472 | tf_op jit(solution)/shard_map/all_gather | solution.py:780
  904.8 503.1 %all-gather.18.cloned.1.call-start = ((), (), s32[]{:S(2)}) async-start(), calls=%async_computation.20 | async-start | bytes 1769472 | tf_op jit(solution)/shard_map/all_gather | solution.py:780
  905.4 547.5 %all-gather.20.cloned.1.call-start = ((), (), s32[]{:S(2)}) async-start(), calls=%async_computation.22 | async-start | bytes 1769472 | tf_op jit(solution)/shard_map/all_gather | solution.py:780
  906.0 590.5 %all-gather.8.cloned.1.call-start = ((), (), s32[]{:S(2)}) async-start(), calls=%async_computation.10 | async-start | bytes 2611200 | tf_op jit(solution)/shard_map/all_gather | solution.py:818
  972.0 190.6 %collective-permute-start.35 = (bf16[384,1024]{1,0:T(8,128)(2,1)S(1)}, bf16[384,1024]{1,0:T(8,128)(2,1)}, u32[]{:S(2)}, u32[]{:S(2)}) collective-permute-start(bf16[384,1024]{1,0:T(8,128)(2,1)S(1)} %all_gather.37), channel_id=1, source_target_pairs={{0,2},{1,3},{2,0},{3,1},{4,6},{5,7},{6,4},{7,5},{8,10},{9,11},{10,... | collective-permute-start | bytes 2359304 | tf_op jit(solution)/shard_map/ppermute | solution.py:658
  1037.8 126.8 %collective-permute-start.37 = (bf16[384,1024]{1,0:T(8,128)(2,1)S(1)}, bf16[384,1024]{1,0:T(8,128)(2,1)}, u32[]{:S(2)}, u32[]{:S(2)}) collective-permute-start(bf16[384,1024]{1,0:T(8,128)(2,1)S(1)} %all_gather.38), channel_id=1, source_target_pairs={{0,2},{1,3},{2,0},{3,1},{4,6},{5,7},{6,4},{7,5},{8,10},{9,11},{10,... | collective-permute-start | bytes 2359304 | tf_op jit(solution)/shard_map/ppermute | solution.py:658
  1102.5 172.1 %collective-permute-start.39 = (bf16[512,768]{1,0:T(8,128)(2,1)S(1)}, bf16[512,768]{1,0:T(8,128)(2,1)}, u32[]{:S(2)}, u32[]{:S(2)}) collective-permute-start(bf16[512,768]{1,0:T(8,128)(2,1)S(1)} %all_gather.39), channel_id=1, source_target_pairs={{0,2},{1,3},{2,0},{3,1},{4,6},{5,7},{6,4},{7,5},{8,10},{9,11},{10,... | collective-permute-start | bytes 2359304 | tf_op jit(solution)/shard_map/ppermute | solution.py:658
  1117.1 335.9 %collective-permute-start.24 = (bf16[384,2048]{1,0:T(8,128)(2,1)}, bf16[384,2048]{1,0:T(8,128)(2,1)}, u32[]{:S(2)}, u32[]{:S(2)}) collective-permute-start(bf16[384,2048]{1,0:T(8,128)(2,1)} %all-gather.10.cloned.1.call-done), channel_id=1, source_target_pairs={{0,2},{1,3},{2,0},{3,1},{4,6},{5,7},{6,4},{7,5},{8,10},{9,11},{10,... | collective-permute-start | bytes 4718600 | tf_op jit(solution)/shard_map/ppermute | solution.py:658
  1162.6 290.4 %collective-permute-start.25 = (bf16[384,2048]{1,0:T(8,128)(2,1)}, bf16[384,2048]{1,0:T(8,128)(2,1)}, u32[]{:S(2)}, u32[]{:S(2)}) collective-permute-start(bf16[384,2048]{1,0:T(8,128)(2,1)} %all-gather.12.cloned.1.call-done), channel_id=1, source_target_pairs={{0,2},{1,3},{2,0},{3,1},{4,6},{5,7},{6,4},{7,5},{8,10},{9,11},{10,... | collective-permute-start | bytes 4718600 | tf_op jit(solution)/shard_map/ppermute | solution.py:658
  1317.8 144.0 %collective-permute-start.28 = (bf16[384,2048]{1,0:T(8,128)(2,1)}, bf16[384,2048]{1,0:T(8,128)(2,1)}, u32[]{:S(2)}, u32[]{:S(2)}) collective-permute-start(bf16[384,2048]{1,0:T(8,128)(2,1)} %all-gather.14.cloned.1.call-done), channel_id=1, source_target_pairs={{0,2},{1,3},{2,0},{3,1},{4,6},{5,7},{6,4},{7,5},{8,10},{9,11},{10,... | collective-permute-start | bytes 4718600 | tf_op jit(solution)/shard_map/ppermute | solution.py:658
  1362.8 98.9 %collective-permute-start.29 = (bf16[384,2048]{1,0:T(8,128)(2,1)}, bf16[384,2048]{1,0:T(8,128)(2,1)}, u32[]{:S(2)}, u32[]{:S(2)}) collective-permute-start(bf16[384,2048]{1,0:T(8,128)(2,1)} %all-gather.16.cloned.1.call-done), channel_id=1, source_target_pairs={{0,2},{1,3},{2,0},{3,1},{4,6},{5,7},{6,4},{7,5},{8,10},{9,11},{10,... | collective-permute-start | bytes 4718600 | tf_op jit(solution)/shard_map/ppermute | solution.py:658
  1407.9 62.7 %collective-permute-start.32 = (bf16[1024,768]{1,0:T(8,128)(2,1)}, bf16[1024,768]{1,0:T(8,128)(2,1)}, u32[]{:S(2)}, u32[]{:S(2)}) collective-permute-start(bf16[1024,768]{1,0:T(8,128)(2,1)} %all-gather.18.cloned.1.call-done), channel_id=1, source_target_pairs={{0,2},{1,3},{2,0},{3,1},{4,6},{5,7},{6,4},{7,5},{8,10},{9,11},{10,... | collective-permute-start | bytes 4718600 | tf_op jit(solution)/shard_map/ppermute | solution.py:658
  1452.9 17.6 %collective-permute-start.33 = (bf16[1024,768]{1,0:T(8,128)(2,1)}, bf16[1024,768]{1,0:T(8,128)(2,1)S(1)}, u32[]{:S(2)}, u32[]{:S(2)}) collective-permute-start(bf16[1024,768]{1,0:T(8,128)(2,1)} %all-gather.20.cloned.1.call-done), channel_id=1, source_target_pairs={{0,2},{1,3},{2,0},{3,1},{4,6},{5,7},{6,4},{7,5},{8,10},{9,11},{10,... | collective-permute-start | bytes 4718600 | tf_op jit(solution)/shard_map/ppermute | solution.py:658
  (51 other events, 847.1 us)
Sparse Core Ops, SparseCore 0:
  339.1 65.1 reduce-scatter.12
  539.0 65.1 reduce-scatter.14
  607.7 63.6 reduce-scatter.16
  675.1 63.7 reduce-scatter.18
  742.1 63.7 reduce-scatter.20
  809.6 63.6 reduce-scatter.22
  877.2 61.4 reduce-scatter.24
  942.9 61.3 reduce-scatter.26
  1007.7 61.6 reduce-scatter.28
  1071.6 45.4 all-gather.9
  1119.5 43.0 all-gather.11
  1169.7 102.6 reduce-scatter.30
  1274.6 43.1 all-gather.13
  1319.8 42.9 all-gather.15
  1364.9 42.9 all-gather.17
  1409.9 42.9 all-gather.19
  1454.9 41.4 all-gather.7

commit v2 on v1

v2 whole, which is shorter than its diff:
```python
import functools

import jax
import jax.numpy as jnp
from jax import lax
from jax.experimental import pallas as pl
from jax.experimental.pallas import tpu as pltpu
from jax.sharding import PartitionSpec as P

D = 768
HEADS = 12
HEAD_DIM = 64
PIC = 256
CAP = 640
PAIR = 2 * HEAD_DIM
PAIRS = HEADS // 2
QB = 256
EPS = 1e-05
BF = jnp.bfloat16
F32 = jnp.float32
ALL = ("rep", "shard")
MIB = 1 << 20
CHEAP = pl.CostEstimate(flops=1, transcendentals=0, bytes_accessed=1)
DEAR = pl.CostEstimate(flops=1 << 36, transcendentals=0, bytes_accessed=1)
HUGE = pl.CostEstimate(flops=1 << 38, transcendentals=0, bytes_accessed=1)
FAIR = pl.CostEstimate(flops=1 << 34, transcendentals=0, bytes_accessed=1)


def nn(a, b):
    return lax.dot_general(a, b, (((1,), (0,)), ((), ())), preferred_element_type=F32)


def nt(a, b):
    return lax.dot_general(a, b, (((1,), (1,)), ((), ())), preferred_element_type=F32)


def resident(shape):
    zeros = (0,) * len(shape)
    return pl.BlockSpec(shape, lambda *_: zeros, pipeline_mode=pl.Buffered(1))


def rotary_tables(length):
    halfway = HEAD_DIM // 2
    freqs_base = 10000.0 ** (-jnp.arange(halfway, dtype=F32) / halfway)
    angles = jnp.arange(length, dtype=F32)[:, None] * freqs_base[None, :]
    cosine = jnp.cos(angles)
    sine = jnp.sin(angles)
    zero = jnp.zeros_like(sine)
    cos_t = jnp.concatenate([cosine] * 4, axis=1)
    left = jnp.concatenate([-sine, zero, -sine, zero], axis=1)
    right = jnp.concatenate([zero, sine, zero, sine], axis=1)
    return cos_t, left, right


def turned(v, left, right):
    return pltpu.roll(v, 96, 1) * left + pltpu.roll(v, 32, 1) * right


def head_masks(rows):
    lane = lax.broadcasted_iota(jnp.int32, (rows, PAIR), 1)
    return lane < HEAD_DIM, lane >= HEAD_DIM


def attend_forward_body(
    where, pic, tok, gain, wq, wk, wv, mine, theirs, cos_t, left, right,
    q_o, k_o, v_o, mix_o, lse_o, w_o,
    xn,
):
    length = tok.shape[0]
    half = D // 2
    step = pl.program_id(0)

    @pl.when(step == 0)
    def _():
        for lo in range(0, length, QB):
            x = tok[lo : lo + QB, :].astype(F32)
            inv = lax.rsqrt(jnp.mean(x * x, axis=1, keepdims=True) + EPS)
            xn[lo : lo + QB, :] = (x * inv * gain[...]).astype(BF)

    own = pl.ds(pl.multiple_of(where[0] * half, half), half)
    quarter = half // 2
    first = pl.ds(pl.multiple_of((1 - where[0]) * half + where[1] * quarter, quarter), quarter)
    second = pl.ds(pl.multiple_of((1 - where[0]) * half + (1 - where[1]) * quarter, quarter), quarter)
    for m, w in enumerate((wq, wk, wv)):
        cols = slice(m * PAIR, (m + 1) * PAIR)
        w_o[own, cols] = w[...]
        w_o[first, cols] = mine[m]
        w_o[second, cols] = theirs[m]
    for lo in range(0, length, QB):
        rows = slice(lo, lo + QB)
        qkv = nn(xn[rows, :], w_o[...])
        q, k = qkv[:, :PAIR], qkv[:, PAIR : 2 * PAIR]
        c_, l_, r_ = cos_t[rows, :], left[rows, :], right[rows, :]
        q_o[rows, :] = (q * c_ + turned(q, l_, r_)).astype(BF) * jnp.asarray(0.125, BF)
        k_o[rows, :] = (k * c_ + turned(k, l_, r_)).astype(BF)
        v_o[rows, :] = qkv[:, 2 * PAIR :].astype(BF)
    masks = head_masks(QB)
    row = lax.broadcasted_iota(jnp.int32, (QB, QB), 0)
    col = lax.broadcasted_iota(jnp.int32, (QB, QB), 1)
    causal = col <= row
    for block in range(length // QB):
        rows = slice(block * QB, (block + 1) * QB)
        allowed = causal | (pic[0] == block)
        q = q_o[rows, :]
        outs = []
        for head in range(2):
            qm = jnp.where(masks[head], q, jnp.zeros_like(q))
            s_d = jnp.where(allowed, nt(qm, k_o[rows, :]), -1e30)
            top = jnp.max(s_d, axis=1, keepdims=True)
            if block:
                s_o = nt(qm, k_o[: block * QB, :])
                top = jnp.maximum(top, jnp.max(s_o, axis=1, keepdims=True))
            p_d = jnp.exp(s_d - top)
            total = jnp.sum(p_d, axis=1, keepdims=True)
            acc = nn(p_d.astype(BF), v_o[rows, :])
            if block:
                p_o = jnp.exp(s_o - top)
                total = total + jnp.sum(p_o, axis=1, keepdims=True)
                acc = acc + nn(p_o.astype(BF), v_o[: block * QB, :])
            outs.append(acc / total)
            lse = jnp.broadcast_to(top + jnp.log(total), (QB, PAIR))
            lse_o[0, head : head + 1, rows] = jnp.transpose(lse)[0:1, :]
        mix_o[rows, :] = jnp.where(masks[0], outs[0], outs[1]).astype(BF)


def attend_forward(where, pic_block, tokens, gain, weights, mine, theirs, tables):
    length = tokens.shape[0]
    half = D // 2
    pair = pl.BlockSpec((length, PAIR), lambda p: (0, p))
    wide = jax.ShapeDtypeStruct((length, D), BF)
    weight = pl.BlockSpec((half, PAIR), lambda p: (0, p))
    part = pl.BlockSpec((4, half // 2, PAIR), lambda p: (0, 0, p))
    return pl.pallas_call(
        attend_forward_body,
        cost_estimate=DEAR,
        grid=(PAIRS,),
        in_specs=[
            pl.BlockSpec(memory_space=pltpu.SMEM),
            pl.BlockSpec(memory_space=pltpu.SMEM),
            resident((length, D)),
            resident((1, D)),
            weight,
            weight,
            weight,
            part,
            part,
            resident((length, PAIR)),
            resident((length, PAIR)),
            resident((length, PAIR)),
        ],
        out_specs=[
            pair, pair, pair, pair,
            pl.BlockSpec((1, 8, length), lambda p: (p, 0, 0)),
            pl.BlockSpec((D, 3 * PAIR), lambda p: (0, p)),
        ],
        out_shape=[
            wide, wide, wide, wide,
            jax.ShapeDtypeStruct((PAIRS, 8, length), F32),
            jax.ShapeDtypeStruct((D, 3 * D), BF),
        ],
        scratch_shapes=[pltpu.VMEM((length, D), BF)],
        compiler_params=pltpu.CompilerParams(vmem_limit_bytes=48 * MIB),
        name="attend_forward",
    )(where, pic_block, tokens, gain, *weights, mine, theirs, *tables)


def attend_backward_body(
    last, where, pic, tok, gain, wqkv, wout, cos_t, left, right, q_i, k_i, v_i, mix_i, lse_i, dres, *refs
):
    if last:
        dres_f, dxn_i, keep_o, send_o, gout_o, igrad_o, ggain_o = refs[:7]
        refs = refs[7:]
    else:
        keep_o, send_o, gout_o, dxn_o = refs[:4]
        refs = refs[4:]
    xn_t, dxn, dmix, dqkv, dk_s, dv_s, k_t = refs
    length = tok.shape[0]
    half = D // 2
    step = pl.program_id(0)

    @pl.when(step == 0)
    def _():
        for lo in range(0, length, QB):
            x = tok[lo : lo + QB, :].astype(F32)
            inv = lax.rsqrt(jnp.mean(x * x, axis=1, keepdims=True) + EPS)
            n_t = jnp.transpose((x * inv * gain[...]).astype(BF))
            spot = pl.multiple_of(where[0] * half, half)
            xn_t[pl.ds(spot, half), lo : lo + QB] = n_t[:half, :]
            xn_t[pl.ds(half - spot, half), lo : lo + QB] = n_t[half:, :]

    dm = nt(dres[...], wout[...]).astype(BF)
    dmix[...] = dm
    mixed = mix_i[...]
    gout_o[...] = nn(jnp.transpose(mixed), dres[...]).astype(BF)
    prod = jnp.transpose(dm.astype(F32) * mixed.astype(F32))
    delta = (
        jnp.sum(prod[:HEAD_DIM, :], axis=0, keepdims=True),
        jnp.sum(prod[HEAD_DIM:, :], axis=0, keepdims=True),
    )
    k_t[...] = jnp.transpose(k_i[...])
    masks = head_masks(QB)
    key_row = lax.broadcasted_iota(jnp.int32, (QB, QB), 0)
    query_col = lax.broadcasted_iota(jnp.int32, (QB, QB), 1)
    causal = key_row <= query_col
    for block in reversed(range(length // QB)):
        rows = slice(block * QB, (block + 1) * QB)
        first = block == length // QB - 1
        allowed = causal | (pic[0] == block)
        q = q_i[rows, :]
        dm = dmix[rows, :]
        dq_t = []
        parts = {"d": [], "o": []}
        for head in range(2):
            qm = jnp.where(masks[head], q, jnp.zeros_like(q))
            dmm = jnp.where(masks[head], dm, jnp.zeros_like(dm))
            lse = lse_i[0, head : head + 1, rows]
            cent = delta[head][:, rows]
            lanes = slice(head * HEAD_DIM, (head + 1) * HEAD_DIM)
            dq = None
            for part, keys in (("d", rows), ("o", slice(0, block * QB))):
                if part == "o" and block == 0:
                    continue
                st = nt(k_i[keys, :], qm)
                pt = jnp.exp(st - lse)
                if part == "d":
                    pt = jnp.where(allowed, pt, 0.0)
                dpt = nt(v_i[keys, :], dmm)
                dst = (pt * (dpt - cent)).astype(BF)
                parts[part].append((nn(dst, qm), nn(pt.astype(BF), dmm)))
                add = nn(k_t[lanes, keys], dst)
                dq = add if dq is None else dq + add
            dq_t.append(dq)
        for part, keys in (("d", rows), ("o", slice(0, block * QB))):
            if not parts[part]:
                continue
            dk = parts[part][0][0] + parts[part][1][0]
            dv = parts[part][0][1] + parts[part][1][1]
            if first:
                dk_s[keys, :] = dk
                dv_s[keys, :] = dv
            else:
                dk_s[keys, :] = dk_s[keys, :] + dk
                dv_s[keys, :] = dv_s[keys, :] + dv
        dq = jnp.transpose(jnp.concatenate(dq_t, axis=0)) * 0.125
        c_, l_, r_ = cos_t[rows, :], left[rows, :], right[rows, :]
        dqkv[rows, :PAIR] = (dq * c_ - turned(dq, l_, r_)).astype(BF)
        dk = dk_s[rows, :]
        dqkv[rows, PAIR : 2 * PAIR] = (dk * c_ - turned(dk, l_, r_)).astype(BF)
        dqkv[rows, 2 * PAIR :] = dv_s[rows, :].astype(BF)
    gqkv = nn(xn_t[...], dqkv[...]).astype(BF)
    keep_o[...] = gqkv[:half, :]
    send_o[...] = gqkv[half:, :]
    add = nt(dqkv[...], wqkv[...])

    @pl.when(step == 0)
    def _():
        if last:
            dxn[...] = dxn_i[...] + add
        else:
            dxn[...] = add

    @pl.when(step > 0)
    def _():
        dxn[...] = dxn[...] + add

    @pl.when(step == pl.num_programs(0) - 1)
    def _():
        if not last:
            dxn_o[...] = dxn[...]
            return
        total = jnp.zeros((1, D), F32)
        for lo in range(0, length, QB):
            rows = slice(lo, lo + QB)
            x = tok[rows, :].astype(F32)
            inv = lax.rsqrt(jnp.mean(x * x, axis=1, keepdims=True) + EPS)
            n = x * inv
            up = dxn[rows, :]
            total = total + jnp.sum(up * n, axis=0, keepdims=True)
            u = up * gain[...]
            igrad_o[rows, :] = dres_f[rows, :] + inv * (u - n * jnp.mean(u * n, axis=1, keepdims=True))
        ggain_o[...] = total


def attend_backward(where, pic_block, tokens, gain, wqkv, wout, tables, q, k, v, mixed, lse, dres, more=None):
    length = tokens.shape[0]
    half = D // 2
    last = more is not None
    early = 2 * PAIRS // 3
    count = PAIRS - early if last else early
    off = early if last else 0
    pair = pl.BlockSpec((length, PAIR), lambda p: (0, p + off))
    grad = pl.BlockSpec((half, 3 * PAIR), lambda p: (0, p))
    wide = jax.ShapeDtypeStruct((length, D), F32)
    out_specs = [grad, grad, pl.BlockSpec((PAIR, D), lambda p: (p, 0)), resident((length, D))]
    out_shape = [
        jax.ShapeDtypeStruct((half, 3 * PAIR * count), BF),
        jax.ShapeDtypeStruct((half, 3 * PAIR * count), BF),
        jax.ShapeDtypeStruct((PAIR * count, D), BF),
        wide,
    ]
    if last:
        out_specs.append(resident((1, D)))
        out_shape.append(jax.ShapeDtypeStruct((1, D), F32))
    return pl.pallas_call(
        functools.partial(attend_backward_body, last),
        cost_estimate=DEAR,
        grid=(count,),
        in_specs=[
            pl.BlockSpec(memory_space=pltpu.SMEM),
            pl.BlockSpec(memory_space=pltpu.SMEM),
            resident((length, D)),
            resident((1, D)),
            pl.BlockSpec((D, 3 * PAIR), lambda p: (0, p + off)),
            pl.BlockSpec((PAIR, D), lambda p: (p + off, 0)),
            resident((length, PAIR)),
            resident((length, PAIR)),
            resident((length, PAIR)),
            pair, pair, pair, pair,
            pl.BlockSpec((1, 8, length), lambda p: (p + off, 0, 0)),
            resident((length, D)),
        ]
        + ([resident((length, D))] * 2 if last else []),
        out_specs=out_specs,
        out_shape=out_shape,
        scratch_shapes=[
            pltpu.VMEM((D, length), BF),
            pltpu.VMEM((length, D), F32),
            pltpu.VMEM((length, PAIR), BF),
            pltpu.VMEM((length, 3 * PAIR), BF),
            pltpu.VMEM((length, PAIR), F32),
            pltpu.VMEM((length, PAIR), F32),
            pltpu.VMEM((PAIR, length), BF),
        ],
        compiler_params=pltpu.CompilerParams(vmem_limit_bytes=56 * MIB),
        name="attend_backward_2" if last else "attend_backward_1",
    )(where, pic_block, tokens, gain, wqkv, wout, *tables, q, k, v, mixed, lse, dres, *(more or ()))


def middle_body(
    shard, tok, mixed, w_own, w_mine, w_theirs, gain, router_t, routes_t,
    resid_o, n2_o, n2p_o, comb_o, wout,
):
    @pl.when(pl.program_id(0) == 0)
    def _():
        half = D // 2
        quarter = half // 2
        other = (1 - shard[0]) * half
        wout[pl.ds(pl.multiple_of(shard[0] * half, half), half), :] = w_own[...]
        first = pl.multiple_of(other + shard[1] * quarter, quarter)
        second = pl.multiple_of(other + (1 - shard[1]) * quarter, quarter)
        wout[pl.ds(first, quarter), :] = w_mine[...]
        wout[pl.ds(second, quarter), :] = w_theirs[...]

    r = tok[...].astype(F32) + nn(mixed[...], wout[...])
    resid_o[...] = r
    inv = lax.rsqrt(jnp.mean(r * r, axis=1, keepdims=True) + EPS)
    n2 = (r * inv * gain[...]).astype(BF)
    n2_o[...] = n2
    half = D // 2
    swapped = jnp.concatenate([n2[:, half:], n2[:, :half]], axis=1)
    n2p_o[...] = jnp.where(shard[0] == 0, n2, swapped)
    logits = nt(router_t[...], n2)
    expert = lax.broadcasted_iota(jnp.int32, logits.shape, 0)
    picks = [expert == routes_t[k : k + 1, :] for k in range(2)]
    chosen = [jnp.sum(jnp.where(p, logits, 0.0), axis=0, keepdims=True) for p in picks]
    top = jnp.maximum(chosen[0], chosen[1])
    weights = [jnp.exp(v - top) for v in chosen]
    total = weights[0] + weights[1]
    gates = [w / total for w in weights]
    comb_o[...] = jnp.where(picks[0], gates[0], 0.0) + jnp.where(picks[1], gates[1], 0.0)


def middle(where, tokens, mixed, w_own, w_mine, w_theirs, gain, router_t, routes_t):
    length = tokens.shape[0]
    block = 256
    rows = pl.BlockSpec((block, D), lambda i: (i, 0))
    cols = pl.BlockSpec((8, block), lambda i: (0, i))
    return pl.pallas_call(
        middle_body,
        cost_estimate=CHEAP,
        grid=(length // block,),
        in_specs=[
            pl.BlockSpec(memory_space=pltpu.SMEM),
            rows,
            rows,
            resident((D // 2, D)),
            pl.BlockSpec((None, D // 4, D), lambda i: (3, 0, 0), pipeline_mode=pl.Buffered(1)),
            pl.BlockSpec((None, D // 4, D), lambda i: (3, 0, 0), pipeline_mode=pl.Buffered(1)),
            resident((1, D)),
            resident((8, D)),
            cols,
        ],
        out_specs=[rows, rows, rows, cols, resident((D, D))],
        out_shape=[
            jax.ShapeDtypeStruct((length, D), F32),
            jax.ShapeDtypeStruct((length, D), BF),
            jax.ShapeDtypeStruct((length, D), BF),
            jax.ShapeDtypeStruct((8, length), F32),
            jax.ShapeDtypeStruct((D, D), BF),
        ],
        compiler_params=pltpu.CompilerParams(vmem_limit_bytes=40 * MIB),
        name="middle",
    )(where, tokens, mixed, w_own, w_mine, w_theirs, gain, router_t, routes_t)


def join_body(shard, dy, resid, gain, dlog, router_t, *refs):
    parts = refs[:-4]
    out_o, dres_o, dlow_o, ggain_o = refs[-4:]
    r = resid[...]
    total = r
    for part in parts:
        total = total + part[0].astype(F32)
    out_o[...] = total.astype(BF)
    up = parts[0][1].astype(F32)
    for part in parts[1:]:
        up = up + part[1].astype(F32)
    half = D // 2
    swapped = jnp.concatenate([up[:, half:], up[:, :half]], axis=1)
    up = jnp.where(shard[0] == 0, up, swapped)
    up = up + nn(dlog[...], router_t[...])
    inv = lax.rsqrt(jnp.mean(r * r, axis=1, keepdims=True) + EPS)
    n = r * inv
    add = jnp.sum(up * n, axis=0, keepdims=True)

    @pl.when(pl.program_id(0) == 0)
    def _():
        ggain_o[...] = add

    @pl.when(pl.program_id(0) > 0)
    def _():
        ggain_o[...] = ggain_o[...] + add

    u = up * gain[...]
    d = dy[...].astype(F32) + inv * (u - n * jnp.mean(u * n, axis=1, keepdims=True))
    dres_o[...] = d
    dlow_o[...] = d.astype(BF)


def join(shard, dy, resid, gain, dlog, router_t, parts):
    length = dy.shape[0]
    block = 256
    rows = pl.BlockSpec((block, D), lambda i: (i, 0))

    return pl.pallas_call(
        join_body,
        cost_estimate=CHEAP,
        grid=(length // block,),
        in_specs=[
            pl.BlockSpec(memory_space=pltpu.SMEM),
            rows,
            rows,
            resident((1, D)),
            pl.BlockSpec((block, 128), lambda i: (i, 0)),
            resident((128, D)),
        ]
        + [pl.BlockSpec((2, block, D), lambda i: (0, i, 0))] * len(parts),
        out_specs=[rows, rows, rows, pl.BlockSpec((1, D), lambda i: (0, 0))],
        out_shape=[
            jax.ShapeDtypeStruct((length, D), BF),
            jax.ShapeDtypeStruct((length, D), F32),
            jax.ShapeDtypeStruct((length, D), BF),
            jax.ShapeDtypeStruct((1, D), F32),
        ],
        compiler_params=pltpu.CompilerParams(vmem_limit_bytes=40 * MIB),
        name="join",
    )(shard, dy, resid, gain, dlog, router_t, *parts)


def ffn_body(routed, steps, chunk, before, where, tok_a, tok_b, dy_a, dy_b, *refs):
    tok, dy = (tok_a, tok_b), (dy_a, dy_b)
    if routed:
        slot_row, slot_col, gate_row = refs[:3]
        refs = refs[3:]
    g_own, u_own, d_own = refs[:3]
    per = steps // 2
    gu_oth = refs[3 : 3 + 2 * per]
    d_oth = refs[3 + 2 * per : 3 + 4 * per]
    refs = refs[3 + 4 * per :]
    if before:
        theirs_i = refs[0]
        refs = refs[1:]
    sides = refs[:2]
    refs = refs[2:]
    if routed:
        dgate_o = refs[0]
        refs = refs[1:]
    keep, send, hold_y, push_y = refs[:4]
    refs = refs[4:]
    wg, wu, wd, y_acc, dx_acc, hid_s, dg_s, du_s, x_t, de_t = refs[:10]
    refs = refs[10:]
    i = pl.program_id(0)
    srcs, length = 2, tok_a.shape[0]
    rows_all = y_acc.shape[0]
    hold = rows_all // srcs
    half = D // 2
    if routed:
        x_s, de_s, dys, gate_s = refs
    tile = 128

    @pl.when(i == 0)
    def _():
        for src in range(srcs):
            if routed:
                for lo in range(0, hold, tile):
                    slot = lax.broadcasted_iota(jnp.int32, (tile, length), 0) + lo
                    mine = slot == slot_row[src : src + 1, :]
                    pick = jnp.where(mine, 1.0, 0.0).astype(BF)
                    rows = slice(src * hold + lo, src * hold + lo + tile)
                    x = nn(pick, tok[src][...]).astype(BF)
                    d_raw = nn(pick, dy[src][...])
                    gate = jnp.sum(jnp.where(mine, gate_row[src : src + 1, :], 0.0), axis=1, keepdims=True)
                    gate_s[rows, :] = jnp.broadcast_to(gate, (tile, 128))
                    d_e = (d_raw * gate).astype(BF)
                    x_s[rows, :] = x
                    dys[rows, :] = d_raw.astype(BF)
                    de_s[rows, :] = d_e
                    x_t[:, rows] = jnp.transpose(x)
                    de_t[:, rows] = jnp.transpose(d_e)
            else:
                for lo in range(0, hold, 256):
                    rows = slice(src * hold + lo, src * hold + lo + 256)
                    x_t[:, rows] = jnp.transpose(tok[src][lo : lo + 256, :])
                    de_t[:, rows] = jnp.transpose(dy[src][lo : lo + 256, :])

    wg[:half, :] = g_own[...]
    wu[:half, :] = u_own[...]
    part = half // 2
    block = wd.shape[0]
    for p in range(per):

        @pl.when(i // 2 == p)
        def _(p=p):
            for k in range(2):
                spot = pl.ds(pl.multiple_of(half + (where[4] ^ k) * part, part), part)
                ref = gu_oth[2 * p + k]
                for h in range(2):
                    lanes = slice(h * 256, (h + 1) * 256)
                    wg[spot, lanes] = ref[2 * h * part : (2 * h + 1) * part, :]
                    wu[spot, lanes] = ref[(2 * h + 1) * part : (2 * h + 2) * part, :]

    @pl.when(i % 2 == 0)
    def _():
        wd[...] = d_own[...]

    for p in range(per):

        @pl.when(i == 2 * p + 1)
        def _(p=p):
            for k in range(2):
                spot = pl.ds(pl.multiple_of((where[4] ^ k) * (block // 2), block // 2), block // 2)
                for h in range(3):
                    wd[spot, h * 256 : (h + 1) * 256] = d_oth[2 * p + k][h * 256 : (h + 1) * 256, :]

    def piece(j, src, first):
        inner = pl.ds(pl.multiple_of(j * chunk, chunk), chunk)
        if routed:
            rows = inner
            x, de = x_s[rows, :], de_s[rows, :]
        else:
            rows = pl.ds(pl.multiple_of(src * length + j * chunk, chunk), chunk)
            x, de = tok[src][inner, :], dy[src][inner, :]
        g = nn(x, wg[...])
        u = nn(x, wu[...])
        dh = nt(de, wd[...])
        s = 1.0 / (1.0 + jnp.exp(-g))
        act = g * s
        hid = (act * u).astype(BF)
        du = (dh * act).astype(BF)
        dg = (dh * u * s * (1.0 + g * (1.0 - s))).astype(BF)
        hid_s[rows, :] = hid
        dg_s[rows, :] = dg
        du_s[rows, :] = du
        y = nn(hid, wd[...])
        dx = nt(dg, wg[...]) + nt(du, wu[...])
        if first:
            y_acc[rows, :] = y
            dx_acc[rows, :] = dx
        else:
            y_acc[rows, :] = y_acc[rows, :] + y
            dx_acc[rows, :] = dx_acc[rows, :] + dx

    for first in (True, False):

        @pl.when((i == 0) == first)
        def _(first=first):
            for src in range(1 if routed else srcs):

                @pl.loop(0, (rows_all if routed else length) // chunk)
                def _(j, src=src, first=first):
                    piece(j, src, first)

    gg = nn(x_t[...], dg_s[...]).astype(BF)
    gu = nn(x_t[...], du_s[...]).astype(BF)
    gd = nn(de_t[...], hid_s[...]).astype(BF)
    for p in range(per):

        def put(side, tile, value, p=p):
            count = keep.shape[0]
            number = 6 * p + tile
            if number < count:
                (keep, send)[side][number] = value
            else:
                top, low = value[: half // 2, :], value[half // 2 :, :]
                hold_y[side, number - count] = jnp.where(where[4] == 0, top, low)
                push_y[side, number - count] = jnp.where(where[4] == 0, low, top)

        @pl.when(i == 2 * p)
        def _(put=put):
            put(0, 0, gg[:half, :])
            put(0, 1, gu[:half, :])
            put(0, 2, gd[:half, :])
            put(0, 3, gd[half:, :])
            put(1, 4, gg[half:, :])
            put(1, 5, gu[half:, :])

        @pl.when(i == 2 * p + 1)
        def _(put=put):
            put(0, 4, gg[:half, :])
            put(0, 5, gu[:half, :])
            put(1, 0, gg[half:, :])
            put(1, 1, gu[half:, :])
            put(1, 2, gd[:half, :])
            put(1, 3, gd[half:, :])

    @pl.when(i == steps - 1)
    def _():
        for src in range(srcs):
            if routed:
                total = jnp.zeros((1, length), F32)
                for lo in range(0, hold, tile):
                    rows = slice(src * hold + lo, src * hold + lo + tile)
                    y = y_acc[rows, :]
                    dgate = jnp.sum(dys[rows, :].astype(F32) * y, axis=1, keepdims=True)
                    slot = lax.broadcasted_iota(jnp.int32, (tile, length), 0) + lo
                    mine = slot == slot_row[src : src + 1, :]
                    total = total + jnp.sum(jnp.where(mine, dgate, 0.0), axis=0, keepdims=True)
                    x_s[rows, :] = (y * gate_s[rows, 0:1]).astype(BF)
                    de_s[rows, :] = dx_acc[rows, :].astype(BF)
                dgate_o[src : src + 1, :] = total
                held = slice(src * hold, (src + 1) * hold)
                for lo in range(0, length, tile):
                    slot = lax.broadcasted_iota(jnp.int32, (tile, hold), 1)
                    mine = slot == slot_col[src * length + lo : src * length + lo + tile, :]
                    pick = jnp.where(mine, 1.0, 0.0).astype(BF)
                    sides[src][0, lo : lo + tile, :] = nn(pick, x_s[held, :]).astype(BF)
                    sides[src][1, lo : lo + tile, :] = nn(pick, de_s[held, :]).astype(BF)
            else:
                held = slice(src * hold, (src + 1) * hold)
                for n, acc in enumerate((y_acc, dx_acc)):
                    total = acc[held, :]
                    if before and src == 1:
                        total = total + theirs_i[n].astype(F32)
                    sides[src][n] = total.astype(BF)


def ffn(where, toks, dys, gate, up, down, others, route=None, only=None, before=None):
    routed = route is not None
    srcs, length = 2, toks[0].shape[0]
    block = 512
    half = D // 2
    per = len(others) // 2
    total, start = (2, only) if only is not None else (per, 0)
    steps = 2 * per
    rows_all = srcs * (CAP if routed else length)
    chunk = 256

    def column(i, w):
        return (i % 2 + w[0] - 2 * w[0] * (i % 2)) * total + i // 2 + start

    if routed:
        gate_spec = pl.BlockSpec((None, half, block), lambda i, w: (w[2], 0, column(i, w)))
        down_spec = pl.BlockSpec((None, block, D), lambda i, w: (w[2], i // 2 + start, 0))
    else:
        gate_spec = pl.BlockSpec((half, block), lambda i, w: (0, column(i, w) * 2 + w[1]))
        down_spec = pl.BlockSpec((block, D), lambda i, w: (w[1], 0))
    def shard_block(i, w):
        return i % 2 + w[0] - 2 * w[0] * (i % 2)

    def gu_spec(p):
        first, last = 2 * p, 2 * p + 1
        return pl.BlockSpec((2 * half, 256), lambda i, w: (shard_block(jnp.clip(i, first, last), w), 0))

    d_spec = pl.BlockSpec((2 * half, 256), lambda i, w: (2, 0), pipeline_mode=pl.Buffered(1))
    in_specs = [resident((length, D))] * 4
    operands = [*toks, *dys]
    if routed:
        in_specs += [resident(r.shape) for r in route]
        operands += list(route)
    in_specs += [gate_spec, gate_spec, down_spec] + [gu_spec(n // 2) for n in range(2 * per)] + [d_spec] * (2 * per)
    operands += [gate, up, down, *others, *others]
    if before is not None:
        in_specs.append(resident(before.shape))
        operands.append(before)
    wide = jax.ShapeDtypeStruct((srcs, length, D), BF)
    out_specs = [resident((srcs, length, D)), resident((srcs, length, D))]
    out_shape = [wide, wide]
    if routed:
        out_specs.append(resident((srcs, length)))
        out_shape.append(jax.ShapeDtypeStruct((srcs, length), F32))
    for shape in ((3 * per, half, block), (2, 3 * per, half // 2, block)):
        out_specs += [resident(shape)] * 2
        out_shape += [jax.ShapeDtypeStruct(shape, BF)] * 2
    scratch = [
        pltpu.VMEM((D, block), BF),
        pltpu.VMEM((D, block), BF),
        pltpu.VMEM((block, D), BF),
        pltpu.VMEM((rows_all, D), F32),
        pltpu.VMEM((rows_all, D), F32),
        pltpu.VMEM((rows_all, block), BF),
        pltpu.VMEM((rows_all, block), BF),
        pltpu.VMEM((rows_all, block), BF),
        pltpu.VMEM((D, rows_all), BF),
        pltpu.VMEM((D, rows_all), BF),
    ]
    if routed:
        scratch += [
            pltpu.VMEM((rows_all, D), BF),
            pltpu.VMEM((rows_all, D), BF),
            pltpu.VMEM((rows_all, D), BF),
            pltpu.VMEM((rows_all, 128), F32),
        ]
    return pl.pallas_call(
        functools.partial(ffn_body, routed, steps, chunk, before is not None),
        cost_estimate=DEAR,
        grid_spec=pltpu.PrefetchScalarGridSpec(
            num_scalar_prefetch=1,
            grid=(steps,),
            in_specs=in_specs,
            out_specs=out_specs,
            scratch_shapes=scratch,
        ),
        out_shape=out_shape,
        compiler_params=pltpu.CompilerParams(vmem_limit_bytes=63 * MIB),
        name="ffn_routed" if routed else "ffn_shared",
    )(where, *operands)


def add(a, b):
    return a[...].astype(F32) + b[...].astype(F32)


def small_call(body, name, where, grid, ins, outs, cost=CHEAP):
    return pl.pallas_call(
        body,
        cost_estimate=cost,
        grid_spec=pltpu.PrefetchScalarGridSpec(
            num_scalar_prefetch=1,
            grid=grid,
            in_specs=[pl.BlockSpec(block, index) for _, block, index in ins],
            out_specs=[pl.BlockSpec(block, index) for _, block, index in outs],
        ),
        out_shape=[jax.ShapeDtypeStruct(shape, BF) for shape, _, _ in outs],
        compiler_params=pltpu.CompilerParams(vmem_limit_bytes=32 * MIB),
        name=name,
    )(where, *[array for array, _, _ in ins])


def sum_x(where, keep, got, cost=CHEAP):
    tiles, rows, cols = keep.shape
    block = (1, rows // 2, cols)

    def mine(t, w):
        return (t, w[4], 0)

    def other(t, w):
        return (t, 1 - w[4], 0)

    def body(w, k_m, g_m, k_o, g_o, send, hold):
        hold[...] = add(k_m, g_m).astype(BF)
        send[...] = add(k_o, g_o).astype(BF)

    ins = [(keep, block, mine), (got, block, mine), (keep, block, other), (got, block, other)]
    shape = (tiles, rows // 2, cols)
    here = (shape, block, lambda t, w: (t, 0, 0))
    return small_call(body, "sum_x", where, (tiles,), ins, [here, here], cost)


def sum_y(where, keep, got, cost=CHEAP):
    tiles, rows, cols = keep.shape
    step = 3 if tiles % 3 == 0 else 1
    block = (step, rows // 4, cols)

    def body(w, *refs):
        for k in range(4):
            refs[8 + k][...] = add(refs[k], refs[4 + k]).astype(BF)

    spots = [lambda t, w, k=k: (t, w[5] ^ k, 0) for k in range(4)]
    ins = [(keep, block, s) for s in spots] + [(got, block, s) for s in spots]
    here = ((tiles, rows // 4, cols), block, lambda t, w: (t, 0, 0))
    return small_call(body, "sum_y", where, (tiles // step,), ins, [here] * 4, cost)


def sum_z(where, parts, cost=CHEAP):
    shape = parts[0].shape
    step = 3 if shape[0] % 3 == 0 else 1
    block = (step,) + shape[1:]

    def body(w, a, b, c, d, out):
        out[...] = (add(a, b) + add(c, d)).astype(BF)

    def at(t, w):
        return (t, 0, 0)

    ins = [(p, block, at) for p in parts]
    return small_call(body, "sum_z", where, (shape[0] // step,), ins, [(shape, block, at)], cost)[0]


def pack(where, gate, up, down, units, per, cost=CHEAP):
    half = D // 2
    part = half // 2
    routed = gate.ndim == 3

    def body(w, *refs):
        for n in range(len(units)):
            g, u, d = refs[3 * n : 3 * n + 3]
            out = refs[3 * len(units) + n]

            @pl.when(pl.program_id(0) < 2)
            def _(g=g, u=u, out=out):
                for h in range(2):
                    for m, ref in enumerate((g, u)):
                        spot = (2 * h + m) * part
                        out[spot : spot + part, :] = ref[:, h * 256 : (h + 1) * 256]

            @pl.when(pl.program_id(0) == 2)
            def _(d=d, out=out):
                for h in range(3):
                    out[h * 256 : (h + 1) * 256, :] = d[:, h * 256 : (h + 1) * 256]

    in_specs = []
    for p, flip in units:

        def col_block(b, p=p):
            return jnp.minimum(b, 1) * per + p

        if routed:
            col = pl.BlockSpec((None, part, 512), lambda b, w, c=col_block, f=flip: (w[2], w[4] ^ f, c(b)))
            row = pl.BlockSpec((None, 256, D), lambda b, w, p=p, f=flip: (w[2], p * 2 + (w[4] ^ f), 0))
        else:
            col = pl.BlockSpec((part, 512), lambda b, w, c=col_block, f=flip: (w[4] ^ f, c(b) * 2 + w[1]))
            row = pl.BlockSpec((256, D), lambda b, w, f=flip: (w[1] * 2 + (w[4] ^ f), 0))
        in_specs += [col, col, row]
    out = pl.BlockSpec((2 * half, 256), lambda b, w: (b, 0))
    return pl.pallas_call(
        body,
        cost_estimate=cost,
        grid_spec=pltpu.PrefetchScalarGridSpec(
            num_scalar_prefetch=1, grid=(3,), in_specs=in_specs, out_specs=[out] * len(units)
        ),
        out_shape=[jax.ShapeDtypeStruct((6 * half, 256), BF)] * len(units),
        name="pack",
    )(where, *[gate, up, down] * len(units))


def pair_first(where, keep, got, hold, got_y, cost=CHEAP):
    tiles, rows, cols = keep.shape
    block = (1, rows // 2, cols)
    both = (2, 1, rows // 2, cols)

    def mine(t, w):
        return (t, w[4], 0)

    def other(t, w):
        return (t, 1 - w[4], 0)

    def two(t, w):
        return (0, t, 0, 0)

    def body(w, k_m, g_m, k_o, g_o, h, g, y_send, y_keep, x_send, x_keep):
        y_keep[...] = add(k_m, g_m).astype(BF)
        y_send[...] = add(k_o, g_o).astype(BF)
        total = add(h, g).astype(BF)
        x_keep[...] = total[0]
        x_send[...] = total[1]

    ins = [(keep, block, mine), (got, block, mine), (keep, block, other), (got, block, other)]
    ins += [(hold, both, two), (got_y, both, two)]
    here = ((tiles, rows // 2, cols), block, lambda t, w: (t, 0, 0))
    return small_call(body, "pair_first", where, (tiles,), ins, [here] * 4, cost)


def pair_second(where, a, b, c, d, cost=CHEAP):
    tiles, rows, cols = a.shape
    block = (3, rows // 4, cols)

    def body(w, *refs):
        for k in range(4):
            a_, b_, c_, d_ = refs[4 * k : 4 * k + 4]
            refs[16 + k][0] = add(a_, b_).astype(BF)
            refs[16 + k][1] = add(c_, d_).astype(BF)

    ins = []
    for k in range(4):
        ins += [(x, block, lambda t, w, k=k: (t, w[5] ^ k, 0)) for x in (a, b, c, d)]
    out = ((2, tiles) + block[1:], (2,) + block, lambda t, w: (0, t, 0, 0))
    return small_call(body, "pair_second", where, (tiles // 3,), ins, [out] * 4, cost)


def pair_scatter(where, a, b, c, d):
    tiles, rows, cols = a.shape
    block = (tiles, rows // 4, cols)

    def body(w, a_, b_, c_, d_, out):
        out[0] = add(a_, b_).astype(BF)
        out[1] = add(c_, d_).astype(BF)

    ins = [(x, block, lambda t, w: (0, t, 0)) for x in (a, b, c, d)]
    out = ((4, 2) + block, (None, 2) + block, lambda t, w: (t, 0, 0, 0, 0))
    return small_call(body, "pair_scatter", where, (4,), ins, [out])[0]


def pair_third(where, parts, cost=CHEAP):
    shape = parts[0].shape
    block = (None,) + shape[1:]

    def body(w, a, b, c, d, out):
        out[...] = (add(a, b) + add(c, d)).astype(BF)

    def at(n, w):
        return (n, 0, 0, 0)

    return small_call(body, "pair_third", where, (2,), [(p, block, at) for p in parts], [(shape, block, at)], cost)[0]


def attention_pack(where, first_keep, first_send, last_keep, last_send, gout_low, gout_high, gain_a, gain_b, router_g):
    half = D // 2
    wide = 2 * D + 128

    def body(w, lk, ls, hk, hs, gl, gh, ga, gb, gr, other, mine, rows, turned_rows):
        rows[...] = jnp.zeros(rows.shape, F32)
        rows[0:1, :] = ga[...]
        rows[1:2, :] = gb[...]
        rows[2 : 2 + gr.shape[0], :] = gr[...]
        turned_rows[...] = jnp.transpose(rows[...]).astype(BF)
        split = lk.shape[1]
        cut = wide - split
        rest = hk.shape[1] - cut
        for side, (low, high) in enumerate(((lk, hk), (ls, hs))):
            spot = pl.multiple_of((w[0] ^ side) * half, half)
            more = turned_rows[pl.ds(spot, half), :]
            for core in range(2):

                @pl.when(w[1] == core)
                def _(core=core, low=low, high=high, side=side, more=more):
                    first, last = (mine, other) if core == 0 else (other, mine)
                    first[side, :, :split] = low[...]
                    first[side, :, split:] = high[:, :cut]
                    last[side, :, :rest] = high[:, cut:]
                    last[side, :, rest + D : rest + D + 128] = more
                    last[side, :, rest + D + 128 :] = jnp.zeros((half, wide - rest - D - 128), BF)

            for core in range(2):
                for part in range(2):

                    @pl.when((w[1] == core) & ((w[0] ^ side) == part))
                    def _(core=core, part=part, side=side):
                        last = (other, mine)[core]
                        if part == 0:
                            last[side, :, rest : rest + D] = gl[:half, :]
                        else:
                            count = gl.shape[0] - half
                            last[side, :count, rest : rest + D] = gl[half:, :]
                            last[side, count:, rest : rest + D] = gh[...]

    last_core = (first_keep, first_send, last_keep, last_send, gout_low, gout_high, gain_a, gain_b, router_g)
    out = resident((2, half, wide))
    return pl.pallas_call(
        body,
        cost_estimate=CHEAP,
        grid_spec=pltpu.PrefetchScalarGridSpec(
            num_scalar_prefetch=1,
            grid=(1,),
            in_specs=[resident(v.shape) for v in last_core],
            out_specs=[out, out],
            scratch_shapes=[pltpu.VMEM((128, D), F32), pltpu.VMEM((D, 128), BF)],
        ),
        out_shape=[jax.ShapeDtypeStruct((2, half, wide), BF)] * 2,
        compiler_params=pltpu.CompilerParams(vmem_limit_bytes=40 * MIB),
        name="attention_pack",
    )(where, *last_core)


def attention_sum(where, mine, got):
    block = (1,) + mine.shape[1:]

    def body(w, a, b, c, d, keep, send):
        keep[...] = add(a, b).astype(BF)
        send[...] = add(c, d).astype(BF)

    ins = [(v, block, lambda t, w, n=n: (n, 0, 0)) for n in range(2) for v in (mine, got)]
    out = (block, block, lambda t, w: (0, 0, 0))
    return small_call(body, "attention_sum", where, (1,), ins, [out, out])


def attention_unpack(where, mine, theirs):
    half, wide = mine.shape[1:]

    def body(w, m, t, *outs):
        for core in range(2):

            @pl.when(w[1] == core)
            def _(core=core):
                both = (m, t) if core == 0 else (t, m)

                def cols(lo):
                    return both[lo // wide][0, :, lo % wide : lo % wide + 128].astype(F32)

                for pair in range(PAIRS):
                    for n in range(3):
                        outs[n][:, pair * PAIR : (pair + 1) * PAIR] = cols((3 * pair + n) * PAIR)
                for n in range(D // 128):
                    outs[3][:, n * 128 : (n + 1) * 128] = cols(3 * D + n * 128)
                outs[4][...] = cols(4 * D)

    shapes = [(half, D)] * 4 + [(half, 128)]
    return pl.pallas_call(
        body,
        cost_estimate=CHEAP,
        grid_spec=pltpu.PrefetchScalarGridSpec(
            num_scalar_prefetch=1,
            grid=(1,),
            in_specs=[resident(mine.shape)] * 2,
            out_specs=[resident(v) for v in shapes],
        ),
        out_shape=[jax.ShapeDtypeStruct(v, F32) for v in shapes],
        compiler_params=pltpu.CompilerParams(vmem_limit_bytes=40 * MIB),
        name="attention_unpack",
    )(where, mine, theirs)


def assemble(where, pieces):
    tiles, rows, cols = pieces[0].shape
    block = (tiles, rows, cols)

    def body(w, *refs):
        for k in range(8):

            @pl.when(pl.program_id(0) == k)
            def _(k=k):
                refs[8][...] = refs[k][...]

    ins = [(p, block, lambda t, w: (0, 0, 0)) for p in pieces]
    out = ((tiles, 8 * rows, cols), block, lambda t, w: (0, t ^ (w[4] * 4 + w[5]), 0))
    return small_call(body, "assemble", where, (8,), ins, [out])[0]


def place(where, j, full, shapes, before, cost=CHEAP):
    paired = isinstance(full, (list, tuple))
    count, _, rows, block = (full[0] if paired else full).shape[1:]
    half = 8 * rows
    routed = j is not None

    def core(t, w):
        return t + w[1] - 2 * t * w[1]

    def column(o, w):
        o = jnp.minimum(o, 1)
        return o + w[0] - 2 * o * w[0]

    def pick(o):
        return jnp.where(o == 0, 0, 3 - o)

    if paired:
        operands = list(full)

        def mine(t, p, o, w):
            return (0, jnp.where(t == 0, p, count - 1), jnp.where(t == 0, pick(o), 1), 0, 0)

        def theirs(t, p, o, w):
            return (0, jnp.where(t == 0, 0, p), jnp.where(t == 0, 0, pick(o)), 0, 0)

        tiles = [pl.BlockSpec((8, None, 2, rows, block), index) for index in (mine, theirs)]
    else:
        operands = [full.reshape((8, 2) + full.shape[1:])]
        tiles = [
            pl.BlockSpec((8, None, None, 2, rows, block), lambda t, p, o, w: (0, core(t, w), p, pick(o), 0, 0))
        ]

    def body(w, *refs):
        for which in range(len(tiles)):
            if paired:

                @pl.when(pl.program_id(0) == which)
                def _(which=which):
                    write(refs[which], *refs[-3:])

            else:
                write(refs[which], *refs[-3:])

    def write(tile, g_o, u_o, d_o):
        step = pl.program_id(2)

        @pl.when(step < 2)
        def _():
            for r in range(8):
                spot = ((r % 2) * 4 + r // 2) * rows
                g_o[spot : spot + rows, :] = tile[r, 0].astype(F32)
                u_o[spot : spot + rows, :] = tile[r, 1].astype(F32)

        @pl.when(step == 2)
        def _():
            for m in range(2):
                parts = [tile[(n % 4) * 2 + n // 4, m] for n in range(8)]
                d_o[:, m * half : (m + 1) * half] = jnp.transpose(jnp.concatenate(parts, axis=0)).astype(F32)

    if routed:
        col = pl.BlockSpec((None, half, block), lambda t, p, o, w: (core(t, w) * 2 + j, 0, column(o, w) * count + p))
        row = pl.BlockSpec((None, block, D), lambda t, p, o, w: (core(t, w) * 2 + j, p, 0))
    else:
        col = pl.BlockSpec((half, block), lambda t, p, o, w: (0, column(o, w) * 2 + core(t, w)))
        row = pl.BlockSpec((block, D), lambda t, p, o, w: (core(t, w), 0))
    before = before or ()
    return pl.pallas_call(
        body,
        cost_estimate=cost,
        grid_spec=pltpu.PrefetchScalarGridSpec(
            num_scalar_prefetch=1,
            grid=(2, count, 3),
            in_specs=tiles + [pl.BlockSpec(memory_space=pl.ANY)] * len(before),
            out_specs=[col, col, row],
        ),
        out_shape=[jax.ShapeDtypeStruct(s, F32) for s in shapes],
        input_output_aliases={1 + len(tiles) + k: k for k in range(len(before))},
        compiler_params=pltpu.CompilerParams(vmem_limit_bytes=40 * MIB),
        name="place",
    )(where, *operands, *before)


def on_device(
    tokens,
    routes,
    pic_block,
    norm1_gain,
    w_query,
    w_key,
    w_value,
    w_out,
    norm2_gain,
    router,
    expert_gate,
    expert_up,
    expert_down,
    shared_gate,
    shared_up,
    shared_down,
    cotangent,
):
    reps = lax.axis_size("rep")
    shards = lax.axis_size("shard")
    rep = lax.axis_index("rep")
    shard = lax.axis_index("shard")
    core = rep % 2
    quarter = (rep // 2) % 4
    length = tokens.shape[0]
    half = D // 2
    experts = router.shape[1]
    per_core = experts // 2

    def swap(value, rep_bit, shard_bit):
        perm = [
            (r * shards + s, (r ^ rep_bit) * shards + (s ^ shard_bit))
            for r in range(reps)
            for s in range(shards)
        ]
        return lax.ppermute(value, ALL, perm)

    def over_core(value):
        return swap(value, 1, 0)

    def over_x(value):
        return swap(value, 0, 1)

    def over_y(value):
        return swap(value, 2, 0)

    def over_z(value, bits):
        return swap(value, 4 * bits, 0)

    def in_order(index, mine, theirs, axis):
        return jnp.where(
            index == 0,
            jnp.concatenate([mine, theirs], axis=axis),
            jnp.concatenate([theirs, mine], axis=axis),
        )

    def later(value, after):
        return lax.optimization_barrier((value, after))[0]

    held = [None]

    def in_turn(call, *args, need=()):
        if held[0] is not None or need:
            args, _, _ = lax.optimization_barrier((args, held[0], need))
        result = call(*args)
        held[0] = result[0] if isinstance(result, (list, tuple)) else result
        return result

    def where_of(expert):
        return jnp.stack(
            [shard, core, expert, quarter, quarter % 2, (rep // 4) % 4]
        ).astype(jnp.int32)

    where = where_of(core * per_core)

    rows_c = functools.partial(lax.dynamic_slice_in_dim, start_index=core * (half // 2), slice_size=half // 2, axis=0)
    tiny = jnp.concatenate([norm1_gain[None], norm2_gain[None], router.T], axis=0)
    tiny = jnp.pad(tiny, ((0, 8 - tiny.shape[0]), (0, 0)))
    tiny_got = over_x(tiny)
    small_mine = over_x(later(jnp.stack([rows_c(w_query), rows_c(w_key), rows_c(w_value), rows_c(w_out)]), tiny_got))
    tiny_full = in_order(shard, tiny, tiny_got, 1)
    gain_one = tiny_full[0:1].astype(F32)
    gain_two = tiny_full[1:2].astype(F32)
    router_t = tiny_full[2 : 2 + experts]
    router_t8 = jnp.pad(router_t, ((0, 8 - experts), (0, 0)))
    router_t128 = jnp.pad(router_t, ((0, 128 - experts), (0, 0)))

    experts_w = (expert_gate, expert_up, expert_down)
    shared_w = (shared_gate, shared_up, shared_down)

    def fetch(weights, units, per, expert, cost=CHEAP, need=()):
        call = functools.partial(pack, units=units, per=per, cost=cost)
        return [over_x(v) for v in in_turn(call, where_of(expert), *weights, need=need)]

    def slot_tables(picks):
        expert_ids = jnp.arange(8)[:, None, None]
        picked = jnp.any(picks.T[None] == expert_ids, axis=1)
        earlier = jnp.arange(length)[:, None] < jnp.arange(length)[None, :]
        rank = jnp.dot(picked.astype(BF), earlier.astype(BF), preferred_element_type=F32)
        return jnp.where(picked, rank.astype(jnp.int32), -1)

    routes_oth = over_core(routes)
    slots = jnp.stack([slot_tables(routes), slot_tables(routes_oth)])
    dys = (cotangent, over_core(cotangent))
    tables = rotary_tables(length)
    routes_t = jnp.pad(routes.T, ((0, 6), (0, 0)))

    first_w = fetch(experts_w, ((0, 0), (1, 0)), 2, core * per_core)
    small_theirs = over_core(later(small_mine, held[0]))
    q, k, v, mixed, lse, wqkv = in_turn(
        attend_forward, where, pic_block, tokens, gain_one, (w_query, w_key, w_value), small_mine, small_theirs, tables,
    )
    first_w = [later(v, q) for v in first_w]
    first_w = (first_w[0], over_y(first_w[0]), first_w[1], over_y(first_w[1]))
    second_w = fetch(experts_w, ((0, 0), (1, 0), (1, 1)), 2, core * per_core + 1)
    resid, n2, n2p, comb, wout = in_turn(
        middle, where, tokens, mixed, w_out, small_mine, small_theirs, gain_two, router_t8, routes_t,
    )
    toks = (n2p, over_core(n2p))
    shared_fetched = fetch(
        shared_w, ((0, 0), (0, 1)), 1, core * per_core, DEAR, (first_w[1], first_w[3], second_w[0])
    )
    second_w = (second_w[0], over_y(second_w[0]), second_w[1], second_w[2])
    combs = jnp.stack([comb, over_core(comb)])

    near = [[h * 16 + r for r in range(16)] for h in range(reps // 16)]
    distant = [[h * 16 + g for h in range(reps // 16)] for g in range(16)]

    def distant_sum(piece):
        if reps > 16:
            flat = piece.reshape(-1, piece.shape[-1])
            flat = lax.psum_scatter(flat, "rep", scatter_dimension=0, tiled=True, axis_index_groups=distant)
            flat = lax.all_gather(flat, "rep", axis=0, tiled=True, axis_index_groups=distant)
            piece = flat.reshape(piece.shape)
        return piece

    def finish(piece):
        return lax.all_gather(distant_sum(piece), "rep", axis=0, tiled=False, axis_index_groups=near)

    def first(pair, cost=CHEAP):
        pair["sums"] = in_turn(functools.partial(pair_first, cost=cost), where, pair["keep"], pair["got"], pair["hold"], pair["got_y"])
        pair["got"] = (over_y(pair["sums"][0]), over_x(pair["sums"][2]))

    def second(pair, cost=CHEAP):
        call = functools.partial(pair_second, cost=cost)
        pair["sums"] = in_turn(call, where, pair["sums"][1], pair["got"][0], pair["sums"][3], pair["got"][1])
        pair["got"] = [pair["sums"][0]] + [over_z(pair["sums"][n], n) for n in range(1, 4)]

    def third(pair, cost=CHEAP):
        pair["piece"] = in_turn(functools.partial(pair_third, cost=cost), where, pair["got"])

    def new_pair(keep, send, hold, push):
        return {"keep": keep, "got": over_x(send), "hold": hold, "got_y": over_y(push)}

    def routing(j):
        expert = core * per_core + j
        slot_row = lax.dynamic_index_in_dim(slots, expert, 1, keepdims=False)
        gate_row = lax.dynamic_index_in_dim(combs, expert, 1, keepdims=False)
        return where_of(expert), (slot_row, slot_row.reshape(-1, 1), gate_row)

    def after_held(values):
        return [later(v, held[0]) for v in values]

    def add_pair(a, b):
        return ((a.astype(F32) + b.astype(F32)).astype(BF),)

    place_a, route_a = routing(0)
    place_b, route_b = routing(1)
    res_a = in_turn(functools.partial(ffn, route=route_a), place_a, toks, dys, *experts_w, first_w)
    pair_a = new_pair(*res_a[3:])
    res_b = in_turn(
        functools.partial(ffn, route=route_b, only=0), place_b, toks, dys, *experts_w, second_w[:2],
        need=tuple(shared_fetched),
    )
    first(pair_a)
    from_early = over_core(in_turn(add_pair, res_a[1], res_b[1])[0])
    pair_b = new_pair(*after_held(res_b[3:]))
    res_c = in_turn(functools.partial(ffn, route=route_b, only=1), place_b, toks, dys, *experts_w, second_w[2:])
    sums = pair_a["sums"]
    scattered = in_turn(pair_scatter, where, sums[1], pair_a["got"][0], sums[3], pair_a["got"][1])
    z_groups = [[h * 16 + z * 4 + g for z in range(4)] for h in range(reps // 16) for g in range(4)]
    piece_a = lax.psum_scatter(scattered, "rep", scatter_dimension=0, tiled=False, axis_index_groups=z_groups)
    gathered = finish(piece_a)
    first(pair_b)
    pair_c = new_pair(*after_held(res_c[3:]))
    res_s = in_turn(functools.partial(ffn, before=res_c[1]), where, toks, dys, *shared_w, shared_fetched)
    parts = [res_a[0], res_b[0], res_c[0], res_s[0], from_early, over_core(res_s[1])]
    dgates = jnp.stack([res_a[2], res_b[2] + res_c[2]])
    dgates_oth = over_core(dgates[:, 1])
    first(pair_c, DEAR)
    dgate = in_order(core, dgates[:, 0], dgates_oth, 0)
    comb_e = comb[:experts]
    dlog_t = (comb_e * (dgate - jnp.sum(comb_e * dgate, axis=0, keepdims=True))).astype(BF)
    dlog = jnp.pad(dlog_t.T, ((0, 0), (0, 128 - experts)))
    output, d_resid, d_low, ggain_two = in_turn(
        join, where, cotangent, resid, gain_two, dlog, router_t128, parts
    )
    grad_router = jnp.dot(dlog_t, n2, preferred_element_type=F32)
    second(pair_b)
    first_keep, first_send, gout_low, d_normed = in_turn(
        attend_backward, where, pic_block, tokens, gain_one, wqkv, wout, tables, q, k, v, mixed, lse, d_low
    )
    third(pair_b)
    second(pair_c)
    pair_s = new_pair(*after_held(res_s[2:]))
    last_keep, last_send, gout_high, input_grad, ggain_one = in_turn(
        attend_backward,
        where, pic_block, tokens, gain_one, wqkv, wout, tables, q, k, v, mixed, lse, d_low, (d_resid, d_normed),
    )

    for_other, for_me = in_turn(
        attention_pack, where, first_keep, first_send, last_keep, last_send, gout_low, gout_high,
        ggain_one, ggain_two, grad_router,
    )
    att_got = over_core(for_other)
    shared_shapes = [shared_gate.shape, shared_up.shape, shared_down.shape]
    expert_shapes = [expert_gate.shape, expert_up.shape, expert_down.shape]
    third(pair_c)
    piece_b = jnp.stack([pair_b["piece"], pair_c["piece"]])
    gathered_b = finish(piece_b.reshape((2, 6) + piece_b.shape[3:]))
    first(pair_s, FAIR)
    expert_grads = in_turn(lambda f: place(where, 0, f, expert_shapes, None, HUGE), gathered)
    att_keep, att_send = in_turn(attention_sum, where, for_me, att_got)
    x_got = over_x(att_send)
    second(pair_s, FAIR)
    y_send, y_keep = in_turn(functools.partial(sum_x, cost=FAIR), where, att_keep, x_got)
    y_got = over_y(y_send)
    third(pair_s, FAIR)
    shared_full = finish(pair_s["piece"])
    quarter_rows = in_turn(functools.partial(sum_y, cost=FAIR), where, y_keep, y_got)
    quarter_rows = [quarter_rows[0]] + [over_z(quarter_rows[n], n) for n in range(1, 4)]
    piece = distant_sum(in_turn(functools.partial(sum_z, cost=FAIR), where, quarter_rows))
    att = [piece] + [over_z(piece, n) for n in range(1, 4)]
    att = att + [over_y(p) for p in att]
    expert_grads = in_turn(
        lambda f, *old: place(where, 1, f, expert_shapes, old, HUGE), gathered_b, *expert_grads
    )
    att = in_turn(assemble, where, att)
    att_oth = over_core(att)
    shared_grads = in_turn(
        lambda f: place(where, None, f, shared_shapes, None),
        shared_full.reshape((16, 1, 6) + shared_full.shape[3:]),
    )
    gq, gk, gv, gout, small_grads = in_turn(attention_unpack, where, att, att_oth)
    return (
        output,
        input_grad,
        small_grads[:, 0],
        gq,
        gk,
        gv,
        gout,
        small_grads[:, 1],
        small_grads[:, 2 : 2 + experts],
        *expert_grads,
        *shared_grads,
    )


def solution(mesh):
    both = P(("rep", "shard"), None)
    rows = P("shard", None)
    vec = P("shard")
    mid = P(None, "shard", None)
    return jax.shard_map(
        on_device,
        mesh=mesh,
        in_specs=(
            both, both, P(("rep", "shard")),
            vec, rows, rows, rows, rows, vec, rows, mid, mid, mid, rows, rows, rows,
            both,
        ),
        out_specs=(both, both, vec, rows, rows, rows, rows, vec, rows, mid, mid, mid, rows, rows, rows),
        check_vma=False,
    )
```

time: 1520 us -> 734 us (0.48)
  waiting for transfers between devices: 933 us -> 159 us
  Pallas kernels: 277 us -> 408 us
  blocking collectives: 99.9 us -> 0 us
  other arithmetic: 80.3 us -> 9.32 us
  starting transfers between devices: 21 us -> 79.2 us
  local copies, waits for them, and re-layouts: 87 us -> 50.2 us
    ppermute x40 -> x59, waiting for transfers between devices: 478 us -> 140 us  [swap(): return lax.ppermute(value, ALL, perm)]
    all_gather x7 -> x3, waiting for transfers between devices: 248 us -> 19 us  [finish(): lax.all_gather(distant_sum(piece), 'rep', axis=0, tiled=False, axis_index...]
    pallas_call x7 -> x33, Pallas kernels: 277 us -> 408 us  [the longest x4 209 us: ffn(): pl.pallas_call(functools.partial(ffn_body, routed, steps, chunk, before i...]
    unnamed x18 -> x4, waiting for transfers between devices: 109 us -> 0.07 us
    all_gather x3 -> x0, blocking collectives: 99.9 us -> none  [reduce_rep(): lax.all_gather(piece, 'rep', axis=0, tiled=True, axis_index_groups=groups)]
    reduce_scatter x9 -> x1, waiting for transfers between devices: 96.7 us -> 0.01 us  [on_device(): lax.psum_scatter(scattered, 'rep', scatter_dimension=0, tiled=False, axis...]
    ppermute x40 -> x59, starting transfers between devices: 20.1 us -> 79 us  [swap(): return lax.ppermute(value, ALL, perm)]
    convert_element_type x17 -> x2, other arithmetic: 51.8 us -> 2.54 us  [the longest x1 2.53 us: add_pair(): return ((a.astype(F32) + b.astype(F32)).astype(BF),)]
  transfers between devices with their start and end apart: 57 -> 63, of which waited for: 29 -> 18; matrix products, arithmetic and copies ran while one was open for 9% -> 3% of each run, Pallas kernels for 14% -> 56%
where the time goes in v2:
time: 734 us; the launch traced here: 722 us
  Pallas kernels  408 us (56%)
  waiting for transfers between devices  159 us (22%)
  starting transfers between devices  79.2 us (11%)
  local copies, waits for them, and re-layouts  50.2 us (7%)
  between operations  15.7 us (2%)
  other arithmetic  9.32 us (1%)
    pallas_call x4, Pallas kernels, ffn(): pl.pallas_call(functools.partial(ffn_body, routed, steps, chunk, before i...  209 us
    ppermute x59, waiting for transfers between devices, swap(): return lax.ppermute(value, ALL, perm)  140 us
    ppermute x59, starting transfers between devices, swap(): return lax.ppermute(value, ALL, perm)  79 us
    pallas_call x2, Pallas kernels, attend_backward(): pl.pallas_call(functools.partial(attend_backward_body, last), cost_estima...  63.8 us
    pallas_call x16, Pallas kernels, small_call(): pl.pallas_call(body, cost_estimate=cost, grid_spec=pltpu.PrefetchScalarGr...  42.7 us
    unnamed x148, local copies, waits for them, and re-layouts  38.8 us
    pallas_call x1, Pallas kernels, attend_forward(): pl.pallas_call(attend_forward_body, cost_estimate=DEAR, grid=(PAIRS,), in...  30.5 us
    pallas_call x3, Pallas kernels, place(): pl.pallas_call(body, cost_estimate=cost, grid_spec=pltpu.PrefetchScalarGr...  29.2 us
  transfers between devices with their start and end apart: 63, of which 18 were waited for; matrix products, arithmetic and copies ran while one was open for 3% of the time, Pallas kernels for 56%

profile of v2, /device:TPU:0, one launch (start us, length us, event | category | flops | bytes accessed | tf_op | source)
XLA Modules:
  0.0 722.4 jit_solution(3071433711232191018)
XLA Ops:
  9.3 3.0 collective-permute-start
  16.5 4.1 pack.3
  20.7 21.5 %collective-permute-done.1.mine.w_mine = bf16[4,192,768]{2,1,0:T(8,128)(2,1)S(1)} collective-permute-done((bf16[4,192,768]{2,1,0:T(8,128)(2,1)S(1)}, bf16[4,192,768]{2,1,0:T(8,128)(2,1)S(1)}, u32[]{:S(2)}, u32[]{:S(2)}) %collective-permute-start.1) | collective-permute-done | bytes 1179680 | tf_op jit(solution)/shard_map/ppermute | solution.py:1165
  49.5 30.5 %attend_forward.1 = (bf16[1024,768]{1,0:T(8,128)(2,1)}, bf16[1024,768]{1,0:T(8,128)(2,1)}, bf16[1024,768]{1,0:T(8,128)(2,1)}, bf16[1024,768]{1,0:T(8,128)(2,1)},...) custom-call(s32[6]{0:T(128)S(1)} %copy-done.40, s32[1]{0:T(128)S(6)} %copy.98.pic, bf16[1024,768]{1,0:T(8,128)(2,1)} %tok.3, ...), custom_call_target="tpu_custom_call" | custom-call | flops 68719476736 | bytes 1 | tf_op jit(solution)/shard_map/attend_forward/pallas_call | solution.py:133
  80.1 4.9 pack.4
  87.2 9.4 %collective-permute-done.7.refs_8_.refs_12_ = bf16[2304,256]{1,0:T(8,128)(2,1)} collective-permute-done((bf16[2304,256]{1,0:T(8,128)(2,1)}, bf16[2304,256]{1,0:T(8,128)(2,1)}, u32[]{:S(2)}, u32[]{:S(2)}) %collective-permute-start.7) | collective-permute-done | bytes 1179680 | tf_op jit(solution)/shard_map/ppermute | solution.py:1165
  105.4 4.4 middle.1
  123.4 15.2 %collective-permute-done.8.refs_9_.refs_13_ = bf16[2304,256]{1,0:T(8,128)(2,1)} collective-permute-done((bf16[2304,256]{1,0:T(8,128)(2,1)}, bf16[2304,256]{1,0:T(8,128)(2,1)}, u32[]{:S(2)}, u32[]{:S(2)}) %collective-permute-start.8) | collective-permute-done | bytes 1179680 | tf_op jit(solution)/shard_map/ppermute | solution.py:1165
  138.6 4.1 pack.5
  146.5 77.9 %ffn_routed.3 = (bf16[2,1024,768]{2,1,0:T(8,128)(2,1)}, bf16[2,1024,768]{2,1,0:T(8,128)(2,1)}, f32[2,1024]{1,0:T(2,128)}, bf16[6,384,512]{2,1,0:T(8,128)(2,1)}, ...) custom-call(s32[6]{0:T(128)} %stack.58.w.where.shard, ...), custom_call_target="tpu_custom_call" | custom-call | flops 68719476736 | bytes 1 | tf_op jit(solution)/shard_map/ffn_routed/pallas_call | solution.py:722
  227.8 42.4 %ffn_routed.4 = (bf16[2,1024,768]{2,1,0:T(8,128)(2,1)}, bf16[2,1024,768]{2,1,0:T(8,128)(2,1)}, f32[2,1024]{1,0:T(2,128)}, bf16[3,384,512]{2,1,0:T(8,128)(2,1)}, ...) custom-call(s32[6]{0:T(128)} %stack.124.w.where, ...), custom_call_target="tpu_custom_call" | custom-call | flops 68719476736 | bytes 1 | tf_op jit(solution)/shard_map/ffn_routed/pallas_call | solution.py:722
  270.2 5.5 collective-permute-done.17.g_m.g_o
  280.8 6.6 pair_first.4
  289.0 2.5 add_convert_fusion
  294.2 42.1 %ffn_routed.5 = (bf16[2,1024,768]{2,1,0:T(8,128)(2,1)}, bf16[2,1024,768]{2,1,0:T(8,128)(2,1)}, f32[2,1024]{1,0:T(2,128)}, bf16[3,384,512]{2,1,0:T(8,128)(2,1)}, ...) custom-call(s32[6]{0:T(128)} %stack.124.w.where, ...), custom_call_target="tpu_custom_call" | custom-call | flops 68719476736 | bytes 1 | tf_op jit(solution)/shard_map/ffn_routed/pallas_call | solution.py:722
  343.0 4.7 pair_scatter.1
  349.3 3.9 pair_first.5
  356.4 46.9 %ffn_shared.1 = (bf16[2,1024,768]{2,1,0:T(8,128)(2,1)}, bf16[2,1024,768]{2,1,0:T(8,128)(2,1)}, bf16[3,384,512]{2,1,0:T(8,128)(2,1)}, bf16[3,384,512]{2,1,0:T(8,1...) custom-call(s32[6]{0:T(128)} %stack.58.w.where.shard, bf16[1024,768]{1,0:T(8,128)(2,1)} %copy-done.52, ...), custom_call_target="tpu_custom_call" | custom-call | flops 68719476736 | bytes 1 | tf_op jit(solution)/shard_map/ffn_shared/pallas_call | solution.py:722
  407.9 4.8 pair_first.6
  414.8 8.7 %join.1 = (bf16[1024,768]{1,0:T(8,128)(2,1)}, f32[1024,768]{1,0:T(8,128)S(1)}, bf16[1024,768]{1,0:T(8,128)(2,1)S(1)}, f32[1,768]{1,0:T(1,128)S(1)}) custom-call(s32[6]{0:T(128)S(1)} %copy-done.42, bf16[1024,768]{1,0:T(8,128)(2,1)S(1)} %copy-done.10, f32[1024,768]{1,0:T(8,128)S(1)} %copy-done.6, f32[1,768]{1,0:T(1,128)S(1)} %copy-done.46, ...), custom_call_target="tpu_custom_call" | custom-call | flops 1 | bytes 1 | tf_op jit(solution)/shard_map/join/pallas_call | solution.py:444
  423.5 2.7 pair_second.3
  427.9 2.6 collective-permute-start.33
  430.6 38.2 %attend_backward_1.1 = (bf16[384,1536]{1,0:T(8,128)(2,1)}, bf16[384,1536]{1,0:T(8,128)(2,1)}, bf16[512,768]{1,0:T(8,128)(2,1)}, f32[1024,768]{1,0:T(8,128)}) custom-call(s32[6]{0:T(128)} %stack.58.w.where.shard, s32[1]{0:T(128)S(6)} %copy.98.pic, bf16[1024,768]{1,0:T(8,128)(2,1)} %tok.3, f32[1,768]{1,0:T(1,128)} %copy-done.48, ...), custom_call_target="tpu_custom_call" | custom-call | flops 68719476736 | bytes 1 | tf_op jit(solution)/shard_map/attend_backward_1/pallas_call | solution.py:304
  471.2 15.5 %collective-permute-start.38 = (bf16[2,3,48,512]{3,2,1,0:T(8,128)(2,1)}, bf16[2,3,48,512]{3,2,1,0:T(8,128)(2,1)S(1)}, u32[]{:S(2)}, u32[]{:S(2)}) collective-permute-start(bf16[2,3,48,512]{3,2,1,0:T(8,128)(2,1)} %get-tuple-element.610), channel_id=1, source_target_pairs={{0,8},{1,9},{2,10},{3,11},{4,12},{5,13},{6,14},{7,15},{8,0},{9,1},... | collective-permute-start | bytes 884744 | tf_op jit(solution)/shard_map/ppermute | solution.py:1165
  492.0 25.7 %attend_backward_2.1 = (bf16[384,768]{1,0:T(8,128)(2,1)}, bf16[384,768]{1,0:T(8,128)(2,1)}, bf16[256,768]{1,0:T(8,128)(2,1)}, f32[1024,768]{1,0:T(8,128)}, f32[1,768]{1,0:T(1,128)}) custom-call(s32[6]{0:T(128)} %stack.58.w.where.shard, s32[1]{0:T(128)S(6)} %copy.98.pic, bf16[1024,768]{1,0:T(8,128)(2,1)} %tok.3, f32[1,768]{1,0:T(1,128)} %copy-done.48, ...), custom_call_target="tpu_custom_call" | custom-call | flops 68719476736 | bytes 1 | tf_op jit(solution)/shard_map/attend_backward_2/pallas_call | solution.py:304
  521.7 2.6 attention_pack.1
  529.5 4.3 pair_first.7
  536.5 4.1 copy-done.49
  540.6 11.4 %place.3 = (f32[4,384,2048]{2,1,0:T(8,128)}, f32[4,384,2048]{2,1,0:T(8,128)}, f32[4,1024,768]{2,1,0:T(8,128)}) custom-call(s32[6]{0:T(128)S(1)} %copy-done.44, bf16[8,2,2,6,48,512]{5,4,3,2,1,0:T(8,128)(2,1)S(1)} %bitcast.62), custom_call_target="tpu_custom_call" | custom-call | flops 274877906944 | bytes 1 | tf_op jit(solution)/shard_map/place/pallas_call | solution.py:1113
  552.0 2.8 attention_sum.1
  559.7 3.6 collective-permute-start.45
  565.7 20.9 %collective-permute-done.41.g_m.g_o = bf16[1,384,1664]{2,1,0:T(8,128)(2,1)S(1)} collective-permute-done((bf16[1,384,1664]{2,1,0:T(8,128)(2,1)S(1)}, bf16[1,384,1664]{2,1,0:T(8,128)(2,1)S(1)}, u32[]{:S(2)}, u32[]{:S(2)}) %collective-permute-start.41) | collective-permute-done | bytes 1277984 | tf_op jit(solution)/shard_map/ppermute | solution.py:1165
  588.8 4.6 collective-permute-done.46.c
  594.8 20.1 %collective-permute-done.44.refs_4_.refs_5_.refs_6_.refs_7_ = bf16[1,192,1664]{2,1,0:T(8,128)(2,1)S(1)} collective-permute-done((bf16[1,192,1664]{2,1,0:T(8,128)(2,1)S(1)}, bf16[1,192,1664]{2,1,0:T(8,128)(2,1)S(1)}, u32[]{:S(2)}, u32[]{:S(2)}) %collective-permute-start.44) | collective-permute-done | bytes 639008 | tf_op jit(solution)/shard_map/ppermute | solution.py:1165
  617.2 2.4 collective-permute-start.49
  620.1 12.3 %collective-permute-done.48.b = bf16[1,48,1664]{2,1,0:T(8,128)(2,1)S(1)} collective-permute-done((bf16[1,48,1664]{2,1,0:T(8,128)(2,1)S(1)}, bf16[1,48,1664]{2,1,0:T(8,128)(2,1)S(1)}, u32[]{:S(2)}, u32[]{:S(2)}) %collective-permute-start.48) | collective-permute-done | bytes 159776 | tf_op jit(solution)/shard_map/ppermute | solution.py:1165
  632.3 5.2 collective-permute-done.49.c
  637.5 2.9 collective-permute-done.50.d
  641.7 4.1 collective-permute-start.51
  645.8 2.4 collective-permute-start.53
  648.3 2.8 collective-permute-done.51.refs_1_
  651.1 12.2 %collective-permute-done.52.refs_2_ = bf16[1,48,1664]{2,1,0:T(8,128)(2,1)} collective-permute-done((bf16[1,48,1664]{2,1,0:T(8,128)(2,1)}, bf16[1,48,1664]{2,1,0:T(8,128)(2,1)}, u32[]{:S(2)}, u32[]{:S(2)}) %collective-permute-start.52) | collective-permute-done | bytes 159776 | tf_op jit(solution)/shard_map/ppermute | solution.py:1165
  665.3 3.7 copy-done.50
  669.0 11.4 %place.4 = (f32[4,384,2048]{2,1,0:T(8,128)}, f32[4,384,2048]{2,1,0:T(8,128)}, f32[4,1024,768]{2,1,0:T(8,128)}) custom-call(s32[6]{0:T(128)S(1)} %copy-done.44, bf16[8,2,2,6,48,512]{5,4,3,2,1,0:T(8,128)(2,1)S(1)} %bitcast.63, f32[4,384,2048]{2,1,0:T(8,128)} %get-tuple-element.668.refs_1_, ...), custom_call_target="tpu_custom_call", output_to_operand_aliasing={{0}: (2, {}), {1}: (3, {}), {2}: (4, {})} | custom-call | flops 274877906944 | bytes 1 | tf_op jit(solution)/shard_map/place/pallas_call | solution.py:1113
  680.5 2.5 assemble.1.m
  683.1 19.0 %all-gather.9.cloned.1.call-done = bf16[32,3,48,512]{3,2,1,0:T(8,128)(2,1)} async-done(((bf16[2,3,48,512]{3,2,1,0:T(8,128)(2,1)}), bf16[32,3,48,512]{3,2,1,0:T(8,128)(2,1)}) %all-gather.9.cloned.1.call-update) | async-done | bytes 4718608 | tf_op jit(solution)/shard_map/all_gather | solution.py:1267
  704.4 6.4 place.5
  710.9 3.1 attention_unpack.1
  (307 shorter events, 114.1 us)
Async XLA Ops:
  7.2 397.9 %reduce-scatter.2.cloned.1.call-start = ((), (), s32[]{:S(2)}) async-start(), calls=%async_computation.1 | async-start | bytes 2949120 | tf_op jit(solution)/shard_map/reduce_scatter | solution.py:1311
  14.7 27.5 %collective-permute-start.1 = (bf16[4,192,768]{2,1,0:T(8,128)(2,1)S(1)}, bf16[4,192,768]{2,1,0:T(8,128)(2,1)S(1)}, u32[]{:S(2)}, u32[]{:S(2)}) collective-permute-start(bf16[4,192,768]{2,1,0:T(8,128)(2,1)S(1)} %pad_maximum_fusion), channel_id=1, source_target_pairs={{0,1},{1,0},{2,3},{3,2},{4,5},{5,4},{6,7},{7,6},{8,9},{9,8},{10,11... | collective-permute-start | bytes 3538952 | tf_op jit(solution)/shard_map/ppermute | solution.py:1165
  42.2 43.3 %collective-permute-start.5 = (bf16[2304,256]{1,0:T(8,128)(2,1)}, bf16[2304,256]{1,0:T(8,128)(2,1)}, u32[]{:S(2)}, u32[]{:S(2)}) collective-permute-start(bf16[2304,256]{1,0:T(8,128)(2,1)} %get-tuple-element.356), channel_id=1, source_target_pairs={{0,1},{1,0},{2,3},{3,2},{4,5},{5,4},{6,7},{7,6},{8,9},{9,8},{10,11... | collective-permute-start | bytes 3538952 | tf_op jit(solution)/shard_map/ppermute | solution.py:1165
  42.5 54.0 %collective-permute-start.7 = (bf16[2304,256]{1,0:T(8,128)(2,1)}, bf16[2304,256]{1,0:T(8,128)(2,1)}, u32[]{:S(2)}, u32[]{:S(2)}) collective-permute-start(bf16[2304,256]{1,0:T(8,128)(2,1)} %get-tuple-element.390), channel_id=1, source_target_pairs={{0,1},{1,0},{2,3},{3,2},{4,5},{5,4},{6,7},{7,6},{8,9},{9,8},{10,11... | collective-permute-start | bytes 3538952 | tf_op jit(solution)/shard_map/ppermute | solution.py:1165
  85.0 36.4 %collective-permute-start.9 = (bf16[2304,256]{1,0:T(8,128)(2,1)}, bf16[2304,256]{1,0:T(8,128)(2,1)}, u32[]{:S(2)}, u32[]{:S(2)}) collective-permute-start(bf16[2304,256]{1,0:T(8,128)(2,1)} %get-tuple-element.376), channel_id=1, source_target_pairs={{0,1},{1,0},{2,3},{3,2},{4,5},{5,4},{6,7},{7,6},{8,9},{9,8},{10,11... | collective-permute-start | bytes 3538952 | tf_op jit(solution)/shard_map/ppermute | solution.py:1165
  85.4 36.3 %collective-permute-start.6 = (bf16[2304,256]{1,0:T(8,128)(2,1)}, bf16[2304,256]{1,0:T(8,128)(2,1)}, u32[]{:S(2)}, u32[]{:S(2)}) collective-permute-start(bf16[2304,256]{1,0:T(8,128)(2,1)} %collective-permute-done.5.refs_6_.refs_10_), channel_id=1, source_target_pairs={{0,4},{1,5},{2,6},{3,7},{4,0},{5,1},{6,2},{7,3},{8,12},{9,13},{10,... | collective-permute-start | bytes 3538952 | tf_op jit(solution)/shard_map/ppermute | solution.py:1165
  96.5 42.1 %collective-permute-start.8 = (bf16[2304,256]{1,0:T(8,128)(2,1)}, bf16[2304,256]{1,0:T(8,128)(2,1)}, u32[]{:S(2)}, u32[]{:S(2)}) collective-permute-start(bf16[2304,256]{1,0:T(8,128)(2,1)} %collective-permute-done.7.refs_8_.refs_12_), channel_id=1, source_target_pairs={{0,4},{1,5},{2,6},{3,7},{4,0},{5,1},{6,2},{7,3},{8,12},{9,13},{10,... | collective-permute-start | bytes 3538952 | tf_op jit(solution)/shard_map/ppermute | solution.py:1165
  98.0 46.4 %collective-permute-start.4 = (bf16[1024,768]{1,0:T(8,128)(2,1)S(1)}, bf16[1024,768]{1,0:T(8,128)(2,1)}, u32[]{:S(2)}, u32[]{:S(2)}) collective-permute-start(bf16[1024,768]{1,0:T(8,128)(2,1)S(1)} %copy-done.9), channel_id=1, source_target_pairs={{0,2},{1,3},{2,0},{3,1},{4,6},{5,7},{6,4},{7,5},{8,10},{9,11},{10,... | collective-permute-start | bytes 4718600 | tf_op jit(solution)/shard_map/ppermute | solution.py:1165
  118.6 26.2 %collective-permute-start.3 = (bf16[1024,768]{1,0:T(8,128)(2,1)S(1)}, bf16[1024,768]{1,0:T(8,128)(2,1)}, u32[]{:S(2)}, u32[]{:S(2)}) collective-permute-start(bf16[1024,768]{1,0:T(8,128)(2,1)S(1)} %copy-done.53), channel_id=1, source_target_pairs={{0,2},{1,3},{2,0},{3,1},{4,6},{5,7},{6,4},{7,5},{8,10},{9,11},{10,... | collective-permute-start | bytes 4718600 | tf_op jit(solution)/shard_map/ppermute | solution.py:1165
  121.4 170.1 %collective-permute-start.15 = (bf16[2304,256]{1,0:T(8,128)(2,1)}, bf16[2304,256]{1,0:T(8,128)(2,1)}, u32[]{:S(2)}, u32[]{:S(2)}) collective-permute-start(bf16[2304,256]{1,0:T(8,128)(2,1)} %get-tuple-element.423), channel_id=1, source_target_pairs={{0,1},{1,0},{2,3},{3,2},{4,5},{5,4},{6,7},{7,6},{8,9},{9,8},{10,11... | collective-permute-start | bytes 3538952 | tf_op jit(solution)/shard_map/ppermute | solution.py:1165
  121.7 169.8 %collective-permute-start.16 = (bf16[2304,256]{1,0:T(8,128)(2,1)}, bf16[2304,256]{1,0:T(8,128)(2,1)}, u32[]{:S(2)}, u32[]{:S(2)}) collective-permute-start(bf16[2304,256]{1,0:T(8,128)(2,1)} %get-tuple-element.424), channel_id=1, source_target_pairs={{0,1},{1,0},{2,3},{3,2},{4,5},{5,4},{6,7},{7,6},{8,9},{9,8},{10,11... | collective-permute-start | bytes 3538952 | tf_op jit(solution)/shard_map/ppermute | solution.py:1165
  142.7 81.7 %collective-permute-start.13 = (bf16[2304,256]{1,0:T(8,128)(2,1)}, bf16[2304,256]{1,0:T(8,128)(2,1)}, u32[]{:S(2)}, u32[]{:S(2)}) collective-permute-start(bf16[2304,256]{1,0:T(8,128)(2,1)} %get-tuple-element.396), channel_id=1, source_target_pairs={{0,1},{1,0},{2,3},{3,2},{4,5},{5,4},{6,7},{7,6},{8,9},{9,8},{10,11... | collective-permute-start | bytes 3538952 | tf_op jit(solution)/shard_map/ppermute | solution.py:1165
  144.5 81.4 %collective-permute-start.14 = (bf16[2304,256]{1,0:T(8,128)(2,1)}, bf16[2304,256]{1,0:T(8,128)(2,1)}, u32[]{:S(2)}, u32[]{:S(2)}) collective-permute-start(bf16[2304,256]{1,0:T(8,128)(2,1)} %get-tuple-element.411), channel_id=1, source_target_pairs={{0,1},{1,0},{2,3},{3,2},{4,5},{5,4},{6,7},{7,6},{8,9},{9,8},{10,11... | collective-permute-start | bytes 3538952 | tf_op jit(solution)/shard_map/ppermute | solution.py:1165
  144.8 82.9 %collective-permute-start.12 = (bf16[2304,256]{1,0:T(8,128)(2,1)}, bf16[2304,256]{1,0:T(8,128)(2,1)}, u32[]{:S(2)}, u32[]{:S(2)}) collective-permute-start(bf16[2304,256]{1,0:T(8,128)(2,1)} %collective-permute-done.9.refs_6_.refs_8_), channel_id=1, source_target_pairs={{0,4},{1,5},{2,6},{3,7},{4,0},{5,1},{6,2},{7,3},{8,12},{9,13},{10,... | collective-permute-start | bytes 3538952 | tf_op jit(solution)/shard_map/ppermute | solution.py:1165
  224.4 51.3 %collective-permute-start.17 = (bf16[6,384,512]{2,1,0:T(8,128)(2,1)}, bf16[6,384,512]{2,1,0:T(8,128)(2,1)}, u32[]{:S(2)}, u32[]{:S(2)}) collective-permute-start(bf16[6,384,512]{2,1,0:T(8,128)(2,1)} %get-tuple-element.428), channel_id=1, source_target_pairs={{0,1},{1,0},{2,3},{3,2},{4,5},{5,4},{6,7},{7,6},{8,9},{9,8},{10,11... | collective-permute-start | bytes 7077896 | tf_op jit(solution)/shard_map/ppermute | solution.py:1165
  225.8 51.6 %collective-permute-start.18 = (bf16[2,6,192,512]{3,2,1,0:T(8,128)(2,1)}, bf16[2,6,192,512]{3,2,1,0:T(8,128)(2,1)}, u32[]{:S(2)}, u32[]{:S(2)}) collective-permute-start(bf16[2,6,192,512]{3,2,1,0:T(8,128)(2,1)} %get-tuple-element.430), channel_id=1, source_target_pairs={{0,4},{1,5},{2,6},{3,7},{4,0},{5,1},{6,2},{7,3},{8,12},{9,13},{10,... | collective-permute-start | bytes 7077896 | tf_op jit(solution)/shard_map/ppermute | solution.py:1165
  287.4 54.7 %collective-permute-start.22 = (bf16[6,192,512]{2,1,0:T(8,128)(2,1)}, bf16[6,192,512]{2,1,0:T(8,128)(2,1)}, u32[]{:S(2)}, u32[]{:S(2)}) collective-permute-start(bf16[6,192,512]{2,1,0:T(8,128)(2,1)} %get-tuple-element.437), channel_id=1, source_target_pairs={{0,4},{1,5},{2,6},{3,7},{4,0},{5,1},{6,2},{7,3},{8,12},{9,13},{10,... | collective-permute-start | bytes 3538952 | tf_op jit(solution)/shard_map/ppermute | solution.py:1165
  291.6 50.6 %collective-permute-start.23 = (bf16[6,192,512]{2,1,0:T(8,128)(2,1)}, bf16[6,192,512]{2,1,0:T(8,128)(2,1)}, u32[]{:S(2)}, u32[]{:S(2)}) collective-permute-start(bf16[6,192,512]{2,1,0:T(8,128)(2,1)} %get-tuple-element.462), channel_id=1, source_target_pairs={{0,1},{1,0},{2,3},{3,2},{4,5},{5,4},{6,7},{7,6},{8,9},{9,8},{10,11... | collective-permute-start | bytes 3538952 | tf_op jit(solution)/shard_map/ppermute | solution.py:1165
  292.2 55.6 %collective-permute-start.21 = (bf16[2,3,192,512]{3,2,1,0:T(8,128)(2,1)}, bf16[2,3,192,512]{3,2,1,0:T(8,128)(2,1)}, u32[]{:S(2)}, u32[]{:S(2)}) collective-permute-start(bf16[2,3,192,512]{3,2,1,0:T(8,128)(2,1)} %get-tuple-element.459), channel_id=1, source_target_pairs={{0,4},{1,5},{2,6},{3,7},{4,0},{5,1},{6,2},{7,3},{8,12},{9,13},{10,... | collective-permute-start | bytes 3538952 | tf_op jit(solution)/shard_map/ppermute | solution.py:1165
  292.5 55.2 %collective-permute-start.20 = (bf16[3,384,512]{2,1,0:T(8,128)(2,1)}, bf16[3,384,512]{2,1,0:T(8,128)(2,1)}, u32[]{:S(2)}, u32[]{:S(2)}) collective-permute-start(bf16[3,384,512]{2,1,0:T(8,128)(2,1)} %get-tuple-element.455), channel_id=1, source_target_pairs={{0,1},{1,0},{2,3},{3,2},{4,5},{5,4},{6,7},{7,6},{8,9},{9,8},{10,11... | collective-permute-start | bytes 3538952 | tf_op jit(solution)/shard_map/ppermute | solution.py:1165
  338.4 75.8 %collective-permute-start.24 = (bf16[2,1024,768]{2,1,0:T(8,128)(2,1)}, bf16[2,1024,768]{2,1,0:T(8,128)(2,1)}, u32[]{:S(2)}, u32[]{:S(2)}) collective-permute-start(bf16[2,1024,768]{2,1,0:T(8,128)(2,1)} %add_convert_fusion), channel_id=1, source_target_pairs={{0,2},{1,3},{2,0},{3,1},{4,6},{5,7},{6,4},{7,5},{8,10},{9,11},{10,... | collective-permute-start | bytes 9437192 | tf_op jit(solution)/shard_map/ppermute | solution.py:1165
  347.7 188.9 %all-gather.5.cloned.1.call-start = ((), (), s32[]{:S(2)}) async-start(), calls=%async_computation.2 | async-start | bytes 10027008 | tf_op jit(solution)/shard_map/all_gather | solution.py:1267
  354.0 69.4 %collective-permute-start.28 = (bf16[3,192,512]{2,1,0:T(8,128)(2,1)}, bf16[3,192,512]{2,1,0:T(8,128)(2,1)}, u32[]{:S(2)}, u32[]{:S(2)}) collective-permute-start(bf16[3,192,512]{2,1,0:T(8,128)(2,1)} %get-tuple-element.473), channel_id=1, source_target_pairs={{0,4},{1,5},{2,6},{3,7},{4,0},{5,1},{6,2},{7,3},{8,12},{9,13},{10,... | collective-permute-start | bytes 1769480 | tf_op jit(solution)/shard_map/ppermute | solution.py:1165
  355.6 47.8 %collective-permute-start.27 = (bf16[2,3,192,512]{3,2,1,0:T(8,128)(2,1)}, bf16[2,3,192,512]{3,2,1,0:T(8,128)(2,1)}, u32[]{:S(2)}, u32[]{:S(2)}) collective-permute-start(bf16[2,3,192,512]{3,2,1,0:T(8,128)(2,1)} %get-tuple-element.494), channel_id=1, source_target_pairs={{0,4},{1,5},{2,6},{3,7},{4,0},{5,1},{6,2},{7,3},{8,12},{9,13},{10,... | collective-permute-start | bytes 3538952 | tf_op jit(solution)/shard_map/ppermute | solution.py:1165
  356.1 49.1 %collective-permute-start.26 = (bf16[3,384,512]{2,1,0:T(8,128)(2,1)}, bf16[3,384,512]{2,1,0:T(8,128)(2,1)}, u32[]{:S(2)}, u32[]{:S(2)}) collective-permute-start(bf16[3,384,512]{2,1,0:T(8,128)(2,1)} %get-tuple-element.490), channel_id=1, source_target_pairs={{0,1},{1,0},{2,3},{3,2},{4,5},{5,4},{6,7},{7,6},{8,9},{9,8},{10,11... | collective-permute-start | bytes 3538952 | tf_op jit(solution)/shard_map/ppermute | solution.py:1165
  405.2 243.1 %all-gather.7.cloned.1.call-start = ((), (), s32[]{:S(2)}) async-start(), calls=%async_computation.3 | async-start | bytes 10027008 | tf_op jit(solution)/shard_map/all_gather | solution.py:1267
  412.7 56.9 %collective-permute-start.30 = (bf16[3,192,512]{2,1,0:T(8,128)(2,1)}, bf16[3,192,512]{2,1,0:T(8,128)(2,1)S(1)}, u32[]{:S(2)}, u32[]{:S(2)}) collective-permute-start(bf16[3,192,512]{2,1,0:T(8,128)(2,1)} %get-tuple-element.500), channel_id=1, source_target_pairs={{0,4},{1,5},{2,6},{3,7},{4,0},{5,1},{6,2},{7,3},{8,12},{9,13},{10,... | collective-permute-start | bytes 1769480 | tf_op jit(solution)/shard_map/ppermute | solution.py:1165
  414.2 55.4 %collective-permute-start.31 = (bf16[3,192,512]{2,1,0:T(8,128)(2,1)S(1)}, bf16[3,192,512]{2,1,0:T(8,128)(2,1)S(1)}, u32[]{:S(2)}, u32[]{:S(2)}) collective-permute-start(bf16[3,192,512]{2,1,0:T(8,128)(2,1)S(1)} %get-tuple-element.548), channel_id=1, source_target_pairs={{0,1},{1,0},{2,3},{3,2},{4,5},{5,4},{6,7},{7,6},{8,9},{9,8},{10,11... | collective-permute-start | bytes 1769480 | tf_op jit(solution)/shard_map/ppermute | solution.py:1165
  426.2 42.6 %collective-permute-start.32 = (bf16[2,3,48,512]{3,2,1,0:T(8,128)(2,1)S(1)}, bf16[2,3,48,512]{3,2,1,0:T(8,128)(2,1)S(1)}, u32[]{:S(2)}, u32[]{:S(2)}) collective-permute-start(bf16[2,3,48,512]{3,2,1,0:T(8,128)(2,1)S(1)} %get-tuple-element.549), channel_id=1, source_target_pairs={{0,8},{1,9},{2,10},{3,11},{4,12},{5,13},{6,14},{7,15},{8,0},{9,1},... | collective-permute-start | bytes 884744 | tf_op jit(solution)/shard_map/ppermute | solution.py:1165
  427.9 40.9 %collective-permute-start.33 = (bf16[2,3,48,512]{3,2,1,0:T(8,128)(2,1)S(1)}, bf16[2,3,48,512]{3,2,1,0:T(8,128)(2,1)S(1)}, u32[]{:S(2)}, u32[]{:S(2)}) collective-permute-start(bf16[2,3,48,512]{3,2,1,0:T(8,128)(2,1)S(1)} %get-tuple-element.550), channel_id=1, source_target_pairs={{0,16},{1,17},{2,18},{3,19},{4,20},{5,21},{6,22},{7,23},{8,24},{9,... | collective-permute-start | bytes 884744 | tf_op jit(solution)/shard_map/ppermute | solution.py:1165
  430.4 38.4 %collective-permute-start.34 = (bf16[2,3,48,512]{3,2,1,0:T(8,128)(2,1)S(1)}, bf16[2,3,48,512]{3,2,1,0:T(8,128)(2,1)S(1)}, u32[]{:S(2)}, u32[]{:S(2)}) collective-permute-start(bf16[2,3,48,512]{3,2,1,0:T(8,128)(2,1)S(1)} %get-tuple-element.551), channel_id=1, source_target_pairs={{0,24},{1,25},{2,26},{3,27},{4,28},{5,29},{6,30},{7,31},{8,16},{9,... | collective-permute-start | bytes 884744 | tf_op jit(solution)/shard_map/ppermute | solution.py:1165
  471.2 53.1 %collective-permute-start.38 = (bf16[2,3,48,512]{3,2,1,0:T(8,128)(2,1)}, bf16[2,3,48,512]{3,2,1,0:T(8,128)(2,1)S(1)}, u32[]{:S(2)}, u32[]{:S(2)}) collective-permute-start(bf16[2,3,48,512]{3,2,1,0:T(8,128)(2,1)} %get-tuple-element.610), channel_id=1, source_target_pairs={{0,8},{1,9},{2,10},{3,11},{4,12},{5,13},{6,14},{7,15},{8,0},{9,1},... | collective-permute-start | bytes 884744 | tf_op jit(solution)/shard_map/ppermute | solution.py:1165
  486.7 37.6 %collective-permute-start.39 = (bf16[2,3,48,512]{3,2,1,0:T(8,128)(2,1)}, bf16[2,3,48,512]{3,2,1,0:T(8,128)(2,1)S(1)}, u32[]{:S(2)}, u32[]{:S(2)}) collective-permute-start(bf16[2,3,48,512]{3,2,1,0:T(8,128)(2,1)} %get-tuple-element.611), channel_id=1, source_target_pairs={{0,16},{1,17},{2,18},{3,19},{4,20},{5,21},{6,22},{7,23},{8,24},{9,... | collective-permute-start | bytes 884744 | tf_op jit(solution)/shard_map/ppermute | solution.py:1165
  488.4 35.9 %collective-permute-start.40 = (bf16[2,3,48,512]{3,2,1,0:T(8,128)(2,1)}, bf16[2,3,48,512]{3,2,1,0:T(8,128)(2,1)}, u32[]{:S(2)}, u32[]{:S(2)}) collective-permute-start(bf16[2,3,48,512]{3,2,1,0:T(8,128)(2,1)} %get-tuple-element.612), channel_id=1, source_target_pairs={{0,24},{1,25},{2,26},{3,27},{4,28},{5,29},{6,30},{7,31},{8,16},{9,... | collective-permute-start | bytes 884744 | tf_op jit(solution)/shard_map/ppermute | solution.py:1165
  489.8 37.0 %collective-permute-start.37 = (bf16[2,3,192,512]{3,2,1,0:T(8,128)(2,1)}, bf16[2,3,192,512]{3,2,1,0:T(8,128)(2,1)}, u32[]{:S(2)}, u32[]{:S(2)}) collective-permute-start(bf16[2,3,192,512]{3,2,1,0:T(8,128)(2,1)} %get-tuple-element.609), channel_id=1, source_target_pairs={{0,4},{1,5},{2,6},{3,7},{4,0},{5,1},{6,2},{7,3},{8,12},{9,13},{10,... | collective-permute-start | bytes 3538952 | tf_op jit(solution)/shard_map/ppermute | solution.py:1165
  490.6 36.3 %collective-permute-start.36 = (bf16[3,384,512]{2,1,0:T(8,128)(2,1)}, bf16[3,384,512]{2,1,0:T(8,128)(2,1)}, u32[]{:S(2)}, u32[]{:S(2)}) collective-permute-start(bf16[3,384,512]{2,1,0:T(8,128)(2,1)} %get-tuple-element.605), channel_id=1, source_target_pairs={{0,1},{1,0},{2,3},{3,2},{4,5},{5,4},{6,7},{7,6},{8,9},{9,8},{10,11... | collective-permute-start | bytes 3538952 | tf_op jit(solution)/shard_map/ppermute | solution.py:1165
  524.3 27.8 %collective-permute-start.35 = (bf16[2,384,1664]{2,1,0:T(8,128)(2,1)}, bf16[2,384,1664]{2,1,0:T(8,128)(2,1)}, u32[]{:S(2)}, u32[]{:S(2)}) collective-permute-start(bf16[2,384,1664]{2,1,0:T(8,128)(2,1)} %get-tuple-element.601), channel_id=1, source_target_pairs={{0,2},{1,3},{2,0},{3,1},{4,6},{5,7},{6,4},{7,5},{8,10},{9,11},{10,... | collective-permute-start | bytes 7667720 | tf_op jit(solution)/shard_map/ppermute | solution.py:1165
  526.8 175.3 %all-gather.9.cloned.1.call-start = ((), (), s32[]{:S(2)}) async-start(), calls=%async_computation.4 | async-start | bytes 5013504 | tf_op jit(solution)/shard_map/all_gather | solution.py:1267
  534.6 22.4 %collective-permute-start.42 = (bf16[3,192,512]{2,1,0:T(8,128)(2,1)}, bf16[3,192,512]{2,1,0:T(8,128)(2,1)}, u32[]{:S(2)}, u32[]{:S(2)}) collective-permute-start(bf16[3,192,512]{2,1,0:T(8,128)(2,1)} %get-tuple-element.623), channel_id=1, source_target_pairs={{0,4},{1,5},{2,6},{3,7},{4,0},{5,1},{6,2},{7,3},{8,12},{9,13},{10,... | collective-permute-start | bytes 1769480 | tf_op jit(solution)/shard_map/ppermute | solution.py:1165
  535.8 21.1 %collective-permute-start.43 = (bf16[3,192,512]{2,1,0:T(8,128)(2,1)}, bf16[3,192,512]{2,1,0:T(8,128)(2,1)}, u32[]{:S(2)}, u32[]{:S(2)}) collective-permute-start(bf16[3,192,512]{2,1,0:T(8,128)(2,1)} %get-tuple-element.633), channel_id=1, source_target_pairs={{0,1},{1,0},{2,3},{3,2},{4,5},{5,4},{6,7},{7,6},{8,9},{9,8},{10,11... | collective-permute-start | bytes 1769480 | tf_op jit(solution)/shard_map/ppermute | solution.py:1165
  557.0 29.7 %collective-permute-start.41 = (bf16[1,384,1664]{2,1,0:T(8,128)(2,1)S(1)}, bf16[1,384,1664]{2,1,0:T(8,128)(2,1)S(1)}, u32[]{:S(2)}, u32[]{:S(2)}) collective-permute-start(bf16[1,384,1664]{2,1,0:T(8,128)(2,1)S(1)} %get-tuple-element.630), channel_id=1, source_target_pairs={{0,1},{1,0},{2,3},{3,2},{4,5},{5,4},{6,7},{7,6},{8,9},{9,8},{10,11... | collective-permute-start | bytes 3833864 | tf_op jit(solution)/shard_map/ppermute | solution.py:1165
  559.7 29.1 %collective-permute-start.45 = (bf16[2,3,48,512]{3,2,1,0:T(8,128)(2,1)S(1)}, bf16[2,3,48,512]{3,2,1,0:T(8,128)(2,1)S(1)}, u32[]{:S(2)}, u32[]{:S(2)}) collective-permute-start(bf16[2,3,48,512]{3,2,1,0:T(8,128)(2,1)S(1)} %get-tuple-element.645), channel_id=1, source_target_pairs={{0,8},{1,9},{2,10},{3,11},{4,12},{5,13},{6,14},{7,15},{8,0},{9,1},... | collective-permute-start | bytes 884744 | tf_op jit(solution)/shard_map/ppermute | solution.py:1165
  563.3 30.1 %collective-permute-start.46 = (bf16[2,3,48,512]{3,2,1,0:T(8,128)(2,1)S(1)}, bf16[2,3,48,512]{3,2,1,0:T(8,128)(2,1)S(1)}, u32[]{:S(2)}, u32[]{:S(2)}) collective-permute-start(bf16[2,3,48,512]{3,2,1,0:T(8,128)(2,1)S(1)} %get-tuple-element.646), channel_id=1, source_target_pairs={{0,16},{1,17},{2,18},{3,19},{4,20},{5,21},{6,22},{7,23},{8,24},{9,... | collective-permute-start | bytes 884744 | tf_op jit(solution)/shard_map/ppermute | solution.py:1165
  563.9 29.5 %collective-permute-start.47 = (bf16[2,3,48,512]{3,2,1,0:T(8,128)(2,1)S(1)}, bf16[2,3,48,512]{3,2,1,0:T(8,128)(2,1)S(1)}, u32[]{:S(2)}, u32[]{:S(2)}) collective-permute-start(bf16[2,3,48,512]{3,2,1,0:T(8,128)(2,1)S(1)} %get-tuple-element.647), channel_id=1, source_target_pairs={{0,24},{1,25},{2,26},{3,27},{4,28},{5,29},{6,30},{7,31},{8,16},{9,... | collective-permute-start | bytes 884744 | tf_op jit(solution)/shard_map/ppermute | solution.py:1165
  587.5 27.4 %collective-permute-start.44 = (bf16[1,192,1664]{2,1,0:T(8,128)(2,1)S(1)}, bf16[1,192,1664]{2,1,0:T(8,128)(2,1)S(1)}, u32[]{:S(2)}, u32[]{:S(2)}) collective-permute-start(bf16[1,192,1664]{2,1,0:T(8,128)(2,1)S(1)} %get-tuple-element.644), channel_id=1, source_target_pairs={{0,4},{1,5},{2,6},{3,7},{4,0},{5,1},{6,2},{7,3},{8,12},{9,13},{10,... | collective-permute-start | bytes 1916936 | tf_op jit(solution)/shard_map/ppermute | solution.py:1165
  648.2 32.3 %collective-permute-start.54 = (bf16[1,48,1664]{2,1,0:T(8,128)(2,1)}, bf16[1,48,1664]{2,1,0:T(8,128)(2,1)}, u32[]{:S(2)}, u32[]{:S(2)}) collective-permute-start(bf16[1,48,1664]{2,1,0:T(8,128)(2,1)} %sum_z.1.refs_0_), channel_id=1, source_target_pairs={{0,4},{1,5},{2,6},{3,7},{4,0},{5,1},{6,2},{7,3},{8,12},{9,13},{10,... | collective-permute-start | bytes 479240 | tf_op jit(solution)/shard_map/ppermute | solution.py:1165
  651.1 29.3 %collective-permute-start.55 = (bf16[1,48,1664]{2,1,0:T(8,128)(2,1)}, bf16[1,48,1664]{2,1,0:T(8,128)(2,1)}, u32[]{:S(2)}, u32[]{:S(2)}) collective-permute-start(bf16[1,48,1664]{2,1,0:T(8,128)(2,1)} %collective-permute-done.51.refs_1_), channel_id=1, source_target_pairs={{0,4},{1,5},{2,6},{3,7},{4,0},{5,1},{6,2},{7,3},{8,12},{9,13},{10,... | collective-permute-start | bytes 479240 | tf_op jit(solution)/shard_map/ppermute | solution.py:1165
  683.0 27.8 %collective-permute-start.58 = (bf16[1,384,1664]{2,1,0:T(8,128)(2,1)S(1)}, bf16[1,384,1664]{2,1,0:T(8,128)(2,1)S(1)}, u32[]{:S(2)}, u32[]{:S(2)}) collective-permute-start(bf16[1,384,1664]{2,1,0:T(8,128)(2,1)S(1)} %assemble.1.m), channel_id=1, source_target_pairs={{0,2},{1,3},{2,0},{3,1},{4,6},{5,7},{6,4},{7,5},{8,10},{9,11},{10,... | collective-permute-start | bytes 3833864 | tf_op jit(solution)/shard_map/ppermute | solution.py:1165
  (86 other events, 1028.8 us)
Sparse Core Ops, SparseCore 0:
  347.8 48.3 reduce-scatter.1
  405.3 124.4 all-gather.4
  532.7 111.8 all-gather.6
  648.3 53.7 all-gather.8

commit v3 on v2

--- a/solution.py
+++ b/solution.py
@@ -531,7 +531,7 @@
         @pl.when(i // 2 == p)
         def _(p=p):
             for k in range(2):
-                spot = pl.ds(pl.multiple_of(half + (where[4] ^ k) * part, part), part)
+                spot = pl.ds(pl.multiple_of(half + (where[3] ^ k) * part, part), part)
                 ref = gu_oth[2 * p + k]
                 for h in range(2):
                     lanes = slice(h * 256, (h + 1) * 256)
@@ -547,7 +547,7 @@
         @pl.when(i == 2 * p + 1)
         def _(p=p):
             for k in range(2):
-                spot = pl.ds(pl.multiple_of((where[4] ^ k) * (block // 2), block // 2), block // 2)
+                spot = pl.ds(pl.multiple_of((where[3] ^ k) * (block // 2), block // 2), block // 2)
                 for h in range(3):
                     wd[spot, h * 256 : (h + 1) * 256] = d_oth[2 * p + k][h * 256 : (h + 1) * 256, :]
 
@@ -834,11 +834,11 @@
             return jnp.minimum(b, 1) * per + p
 
         if routed:
-            col = pl.BlockSpec((None, part, 512), lambda b, w, c=col_block, f=flip: (w[2], w[4] ^ f, c(b)))
-            row = pl.BlockSpec((None, 256, D), lambda b, w, p=p, f=flip: (w[2], p * 2 + (w[4] ^ f), 0))
+            col = pl.BlockSpec((None, part, 512), lambda b, w, c=col_block, f=flip: (w[2], w[3] ^ f, c(b)))
+            row = pl.BlockSpec((None, 256, D), lambda b, w, p=p, f=flip: (w[2], p * 2 + (w[3] ^ f), 0))
         else:
-            col = pl.BlockSpec((part, 512), lambda b, w, c=col_block, f=flip: (w[4] ^ f, c(b) * 2 + w[1]))
-            row = pl.BlockSpec((256, D), lambda b, w, f=flip: (w[1] * 2 + (w[4] ^ f), 0))
+            col = pl.BlockSpec((part, 512), lambda b, w, c=col_block, f=flip: (w[3] ^ f, c(b) * 2 + w[1]))
+            row = pl.BlockSpec((256, D), lambda b, w, f=flip: (w[1] * 2 + (w[3] ^ f), 0))
         in_specs += [col, col, row]
     out = pl.BlockSpec((2 * half, 256), lambda b, w: (b, 0))
     return pl.pallas_call(
@@ -1197,7 +1197,7 @@
 
     def where_of(expert):
         return jnp.stack(
-            [shard, core, expert, quarter, quarter % 2, (rep // 4) % 4]
+            [shard, core, expert, (quarter ^ (quarter // 2)) % 2, quarter % 2, (rep // 4) % 4]
         ).astype(jnp.int32)
 
     where = where_of(core * per_core)
@@ -1240,8 +1240,8 @@
         attend_forward, where, pic_block, tokens, gain_one, (w_query, w_key, w_value), small_mine, small_theirs, tables,
     )
     first_w = [later(v, q) for v in first_w]
-    first_w = (first_w[0], over_y(first_w[0]), first_w[1], over_y(first_w[1]))
-    second_w = fetch(experts_w, ((0, 0), (1, 0), (1, 1)), 2, core * per_core + 1)
+    first_w = (first_w[0], over_y(first_w[0]), first_w[1], over_z(first_w[1], 1))
+    second_w = fetch(experts_w, ((0, 0), (1, 0)), 2, core * per_core + 1)
     resid, n2, n2p, comb, wout = in_turn(
         middle, where, tokens, mixed, w_out, small_mine, small_theirs, gain_two, router_t8, routes_t,
     )
@@ -1249,7 +1249,7 @@
     shared_fetched = fetch(
         shared_w, ((0, 0), (0, 1)), 1, core * per_core, DEAR, (first_w[1], first_w[3], second_w[0])
     )
-    second_w = (second_w[0], over_y(second_w[0]), second_w[1], second_w[2])
+    second_w = (second_w[0], over_y(second_w[0]), second_w[1])
     combs = jnp.stack([comb, over_core(comb)])
 
     near = [[h * 16 + r for r in range(16)] for h in range(reps // 16)]
@@ -1297,6 +1297,7 @@
     place_b, route_b = routing(1)
     res_a = in_turn(functools.partial(ffn, route=route_a), place_a, toks, dys, *experts_w, first_w)
     pair_a = new_pair(*res_a[3:])
+    second_w += (over_z(later(second_w[2], res_a[0]), 1),)
     res_b = in_turn(
         functools.partial(ffn, route=route_b, only=0), place_b, toks, dys, *experts_w, second_w[:2],
         need=tuple(shared_fetched),
@@ -1347,12 +1348,12 @@
     third(pair_c)
     piece_b = jnp.stack([pair_b["piece"], pair_c["piece"]])
     gathered_b = finish(piece_b.reshape((2, 6) + piece_b.shape[3:]))
-    first(pair_s, FAIR)
-    expert_grads = in_turn(lambda f: place(where, 0, f, expert_shapes, None, HUGE), gathered)
+    first(pair_s, DEAR)
     att_keep, att_send = in_turn(attention_sum, where, for_me, att_got)
     x_got = over_x(att_send)
+    expert_grads = in_turn(lambda f: place(where, 0, f, expert_shapes, None, HUGE), gathered)
     second(pair_s, FAIR)
-    y_send, y_keep = in_turn(functools.partial(sum_x, cost=FAIR), where, att_keep, x_got)
+    y_send, y_keep = in_turn(sum_x, where, att_keep, x_got)
     y_got = over_y(y_send)
     third(pair_s, FAIR)
     shared_full = finish(pair_s["piece"])
@@ -1366,11 +1367,11 @@
     )
     att = in_turn(assemble, where, att)
     att_oth = over_core(att)
+    gq, gk, gv, gout, small_grads = in_turn(attention_unpack, where, att, att_oth)
     shared_grads = in_turn(
         lambda f: place(where, None, f, shared_shapes, None),
         shared_full.reshape((16, 1, 6) + shared_full.shape[3:]),
     )
-    gq, gk, gv, gout, small_grads = in_turn(attention_unpack, where, att, att_oth)
     return (
         output,
         input_grad,

time: 734 us -> 710 us (0.967)
  waiting for transfers between devices: 159 us -> 129 us
  starting transfers between devices: 79.2 us -> 90.6 us
    ppermute x59, waiting for transfers between devices: 140 us -> 111 us  [swap(): return lax.ppermute(value, ALL, perm)]
    ppermute x59, starting transfers between devices: 79 us -> 90.5 us  [swap(): return lax.ppermute(value, ALL, perm)]
    unnamed x148 -> x152, local copies, waits for them, and re-layouts: 38.8 us -> 39.3 us
  transfers between devices with their start and end apart: 63 -> 63, of which waited for: 18 -> 16; matrix products, arithmetic and copies ran while one was open for 3% -> 3% of each run, Pallas kernels for 56% -> 57%
where the time goes in v3:
time: 710 us; the launch traced here: 705 us
  Pallas kernels  409 us (58%)
  waiting for transfers between devices  129 us (18%)
  starting transfers between devices  90.6 us (13%)
  local copies, waits for them, and re-layouts  50.7 us (7%)
  between operations  15.7 us (2%)
  other arithmetic  9.33 us (1%)
    pallas_call x4, Pallas kernels, ffn(): pl.pallas_call(functools.partial(ffn_body, routed, steps, chunk, before i...  209 us
    ppermute x59, waiting for transfers between devices, swap(): return lax.ppermute(value, ALL, perm)  111 us
    ppermute x59, starting transfers between devices, swap(): return lax.ppermute(value, ALL, perm)  90.5 us
    pallas_call x2, Pallas kernels, attend_backward(): pl.pallas_call(functools.partial(attend_backward_body, last), cost_estima...  63.8 us
    pallas_call x16, Pallas kernels, small_call(): pl.pallas_call(body, cost_estimate=cost, grid_spec=pltpu.PrefetchScalarGr...  44.8 us
    unnamed x152, local copies, waits for them, and re-layouts  39.3 us
    pallas_call x1, Pallas kernels, attend_forward(): pl.pallas_call(attend_forward_body, cost_estimate=DEAR, grid=(PAIRS,), in...  30.5 us
    pallas_call x3, Pallas kernels, place(): pl.pallas_call(body, cost_estimate=cost, grid_spec=pltpu.PrefetchScalarGr...  29.2 us
  transfers between devices with their start and end apart: 63, of which 16 were waited for; matrix products, arithmetic and copies ran while one was open for 3% of the time, Pallas kernels for 57%

profile of v3, /device:TPU:0, one launch (start us, length us, event | category | flops | bytes accessed | tf_op | source)
XLA Modules:
  0.0 704.7 jit_solution(11565295040734815944)
XLA Ops:
  9.3 3.0 collective-permute-start
  16.5 4.1 pack.3
  20.6 21.5 %collective-permute-done.1.mine.w_mine = bf16[4,192,768]{2,1,0:T(8,128)(2,1)S(1)} collective-permute-done((bf16[4,192,768]{2,1,0:T(8,128)(2,1)S(1)}, bf16[4,192,768]{2,1,0:T(8,128)(2,1)S(1)}, u32[]{:S(2)}, u32[]{:S(2)}) %collective-permute-start.1) | collective-permute-done | bytes 1179680 | tf_op jit(solution)/shard_map/ppermute | solution.py:1165
  49.5 30.5 %attend_forward.1 = (bf16[1024,768]{1,0:T(8,128)(2,1)}, bf16[1024,768]{1,0:T(8,128)(2,1)}, bf16[1024,768]{1,0:T(8,128)(2,1)}, bf16[1024,768]{1,0:T(8,128)(2,1)},...) custom-call(s32[6]{0:T(128)S(1)} %copy-done.37, s32[1]{0:T(128)S(6)} %copy.98.pic, bf16[1024,768]{1,0:T(8,128)(2,1)} %tok.3, ...), custom_call_target="tpu_custom_call" | custom-call | flops 68719476736 | bytes 1 | tf_op jit(solution)/shard_map/attend_forward/pallas_call | solution.py:133
  81.7 14.4 %collective-permute-done.7.refs_8_.refs_12_ = bf16[2304,256]{1,0:T(8,128)(2,1)} collective-permute-done((bf16[2304,256]{1,0:T(8,128)(2,1)}, bf16[2304,256]{1,0:T(8,128)(2,1)}, u32[]{:S(2)}, u32[]{:S(2)}) %collective-permute-start.7) | collective-permute-done | bytes 1179680 | tf_op jit(solution)/shard_map/ppermute | solution.py:1165
  97.7 4.1 pack.4
  109.8 4.4 middle.1
  125.8 5.3 collective-permute-done.9.refs_6_.refs_8_
  131.1 4.1 pack.5
  138.9 77.9 %ffn_routed.3 = (bf16[2,1024,768]{2,1,0:T(8,128)(2,1)}, bf16[2,1024,768]{2,1,0:T(8,128)(2,1)}, f32[2,1024]{1,0:T(2,128)}, bf16[6,384,512]{2,1,0:T(8,128)(2,1)}, ...) custom-call(s32[6]{0:T(128)} %stack.58.w.where.shard, ...), custom_call_target="tpu_custom_call" | custom-call | flops 68719476736 | bytes 1 | tf_op jit(solution)/shard_map/ffn_routed/pallas_call | solution.py:722
  217.9 42.3 %ffn_routed.4 = (bf16[2,1024,768]{2,1,0:T(8,128)(2,1)}, bf16[2,1024,768]{2,1,0:T(8,128)(2,1)}, f32[2,1024]{1,0:T(2,128)}, bf16[3,384,512]{2,1,0:T(8,128)(2,1)}, ...) custom-call(s32[6]{0:T(128)} %stack.124.w.where, ...), custom_call_target="tpu_custom_call" | custom-call | flops 68719476736 | bytes 1 | tf_op jit(solution)/shard_map/ffn_routed/pallas_call | solution.py:722
  260.3 6.0 collective-permute-done.17.g_m.g_o
  269.9 6.6 pair_first.4
  277.0 2.5 add_convert_fusion
  283.3 42.1 %ffn_routed.5 = (bf16[2,1024,768]{2,1,0:T(8,128)(2,1)}, bf16[2,1024,768]{2,1,0:T(8,128)(2,1)}, f32[2,1024]{1,0:T(2,128)}, bf16[3,384,512]{2,1,0:T(8,128)(2,1)}, ...) custom-call(s32[6]{0:T(128)} %stack.124.w.where, ...), custom_call_target="tpu_custom_call" | custom-call | flops 68719476736 | bytes 1 | tf_op jit(solution)/shard_map/ffn_routed/pallas_call | solution.py:722
  332.0 4.7 pair_scatter.1
  338.3 3.9 pair_first.5
  346.6 46.9 %ffn_shared.1 = (bf16[2,1024,768]{2,1,0:T(8,128)(2,1)}, bf16[2,1024,768]{2,1,0:T(8,128)(2,1)}, bf16[3,384,512]{2,1,0:T(8,128)(2,1)}, bf16[3,384,512]{2,1,0:T(8,1...) custom-call(s32[6]{0:T(128)} %stack.58.w.where.shard, bf16[1024,768]{1,0:T(8,128)(2,1)} %copy-done.54, ...), custom_call_target="tpu_custom_call" | custom-call | flops 68719476736 | bytes 1 | tf_op jit(solution)/shard_map/ffn_shared/pallas_call | solution.py:722
  396.9 4.8 pair_first.6
  403.7 8.7 %join.1 = (bf16[1024,768]{1,0:T(8,128)(2,1)}, f32[1024,768]{1,0:T(8,128)S(1)}, bf16[1024,768]{1,0:T(8,128)(2,1)S(1)}, f32[1,768]{1,0:T(1,128)S(1)}) custom-call(s32[6]{0:T(128)S(1)} %copy-done.39, bf16[1024,768]{1,0:T(8,128)(2,1)S(1)} %copy-done.12, f32[1024,768]{1,0:T(8,128)S(1)} %copy-done.8, f32[1,768]{1,0:T(1,128)S(1)} %copy-done.48, ...), custom_call_target="tpu_custom_call" | custom-call | flops 1 | bytes 1 | tf_op jit(solution)/shard_map/join/pallas_call | solution.py:444
  412.4 2.7 pair_second.3
  415.7 2.6 collective-permute-start.33
  419.6 38.1 %attend_backward_1.1 = (bf16[384,1536]{1,0:T(8,128)(2,1)}, bf16[384,1536]{1,0:T(8,128)(2,1)}, bf16[512,768]{1,0:T(8,128)(2,1)}, f32[1024,768]{1,0:T(8,128)}) custom-call(s32[6]{0:T(128)} %stack.58.w.where.shard, s32[1]{0:T(128)S(6)} %copy.98.pic, bf16[1024,768]{1,0:T(8,128)(2,1)} %tok.3, f32[1,768]{1,0:T(1,128)} %copy-done.50, ...), custom_call_target="tpu_custom_call" | custom-call | flops 68719476736 | bytes 1 | tf_op jit(solution)/shard_map/attend_backward_1/pallas_call | solution.py:304
  460.1 15.3 %collective-permute-start.38 = (bf16[2,3,48,512]{3,2,1,0:T(8,128)(2,1)}, bf16[2,3,48,512]{3,2,1,0:T(8,128)(2,1)S(1)}, u32[]{:S(2)}, u32[]{:S(2)}) collective-permute-start(bf16[2,3,48,512]{3,2,1,0:T(8,128)(2,1)} %get-tuple-element.610), channel_id=1, source_target_pairs={{0,8},{1,9},{2,10},{3,11},{4,12},{5,13},{6,14},{7,15},{8,0},{9,1},... | collective-permute-start | bytes 884744 | tf_op jit(solution)/shard_map/ppermute | solution.py:1165
  481.1 25.7 %attend_backward_2.1 = (bf16[384,768]{1,0:T(8,128)(2,1)}, bf16[384,768]{1,0:T(8,128)(2,1)}, bf16[256,768]{1,0:T(8,128)(2,1)}, f32[1024,768]{1,0:T(8,128)}, f32[1,768]{1,0:T(1,128)}) custom-call(s32[6]{0:T(128)} %stack.58.w.where.shard, s32[1]{0:T(128)S(6)} %copy.98.pic, bf16[1024,768]{1,0:T(8,128)(2,1)} %tok.3, f32[1,768]{1,0:T(1,128)} %copy-done.50, ...), custom_call_target="tpu_custom_call" | custom-call | flops 68719476736 | bytes 1 | tf_op jit(solution)/shard_map/attend_backward_2/pallas_call | solution.py:304
  510.6 2.6 attention_pack.1
  518.5 4.3 pair_first.7
  525.4 3.6 attention_sum.1
  530.9 3.7 copy-done.51
  534.6 11.4 %place.3 = (f32[4,384,2048]{2,1,0:T(8,128)}, f32[4,384,2048]{2,1,0:T(8,128)}, f32[4,1024,768]{2,1,0:T(8,128)}) custom-call(s32[6]{0:T(128)S(1)} %copy-done.41, bf16[8,2,2,6,48,512]{5,4,3,2,1,0:T(8,128)(2,1)S(1)} %bitcast.62), custom_call_target="tpu_custom_call" | custom-call | flops 274877906944 | bytes 1 | tf_op jit(solution)/shard_map/place/pallas_call | solution.py:1113
  548.3 3.5 collective-permute-start.45
  554.2 13.1 %collective-permute-done.41.g_m.g_o = bf16[1,384,1664]{2,1,0:T(8,128)(2,1)} collective-permute-done((bf16[1,384,1664]{2,1,0:T(8,128)(2,1)}, bf16[1,384,1664]{2,1,0:T(8,128)(2,1)}, u32[]{:S(2)}, u32[]{:S(2)}) %collective-permute-start.41) | collective-permute-done | bytes 1277984 | tf_op jit(solution)/shard_map/ppermute | solution.py:1165
  570.9 16.2 %collective-permute-done.46.c = bf16[2,3,48,512]{3,2,1,0:T(8,128)(2,1)S(1)} collective-permute-done((bf16[2,3,48,512]{3,2,1,0:T(8,128)(2,1)S(1)}, bf16[2,3,48,512]{3,2,1,0:T(8,128)(2,1)S(1)}, u32[]{:S(2)}, u32[]{:S(2)}) %collective-permute-start.46) | collective-permute-done | bytes 294944 | tf_op jit(solution)/shard_map/ppermute | solution.py:1165
  588.5 8.8 %collective-permute-done.44.refs_4_.refs_5_.refs_6_.refs_7_ = bf16[1,192,1664]{2,1,0:T(8,128)(2,1)S(1)} collective-permute-done((bf16[1,192,1664]{2,1,0:T(8,128)(2,1)S(1)}, bf16[1,192,1664]{2,1,0:T(8,128)(2,1)S(1)}, u32[]{:S(2)}, u32[]{:S(2)}) %collective-permute-start.44) | collective-permute-done | bytes 639008 | tf_op jit(solution)/shard_map/ppermute | solution.py:1165
  598.0 10.2 %collective-permute-start.48 = (bf16[1,48,1664]{2,1,0:T(8,128)(2,1)S(1)}, bf16[1,48,1664]{2,1,0:T(8,128)(2,1)S(1)}, u32[]{:S(2)}, u32[]{:S(2)}) collective-permute-start(bf16[1,48,1664]{2,1,0:T(8,128)(2,1)S(1)} %get-tuple-element.657), channel_id=1, source_target_pairs={{0,8},{1,9},{2,10},{3,11},{4,12},{5,13},{6,14},{7,15},{8,0},{9,1},... | collective-permute-start | bytes 479240 | tf_op jit(solution)/shard_map/ppermute | solution.py:1165
  608.2 2.8 collective-permute-start.49
  612.5 6.0 collective-permute-done.48.b
  618.4 7.8 %collective-permute-done.49.c = bf16[1,48,1664]{2,1,0:T(8,128)(2,1)S(1)} collective-permute-done((bf16[1,48,1664]{2,1,0:T(8,128)(2,1)S(1)}, bf16[1,48,1664]{2,1,0:T(8,128)(2,1)S(1)}, u32[]{:S(2)}, u32[]{:S(2)}) %collective-permute-start.49) | collective-permute-done | bytes 159776 | tf_op jit(solution)/shard_map/ppermute | solution.py:1165
  627.5 4.9 collective-permute-start.51
  640.1 4.0 collective-permute-done.52.refs_2_
  646.1 3.7 copy-done.52
  649.8 11.4 %place.4 = (f32[4,384,2048]{2,1,0:T(8,128)}, f32[4,384,2048]{2,1,0:T(8,128)}, f32[4,1024,768]{2,1,0:T(8,128)}) custom-call(s32[6]{0:T(128)S(1)} %copy-done.41, bf16[8,2,2,6,48,512]{5,4,3,2,1,0:T(8,128)(2,1)S(1)} %bitcast.63, f32[4,384,2048]{2,1,0:T(8,128)} %get-tuple-element.668.refs_1_, ...), custom_call_target="tpu_custom_call", output_to_operand_aliasing={{0}: (2, {}), {1}: (3, {}), {2}: (4, {})} | custom-call | flops 274877906944 | bytes 1 | tf_op jit(solution)/shard_map/place/pallas_call | solution.py:1113
  661.3 2.5 assemble.1.m
  663.9 3.0 collective-permute-done.58.t
  666.9 3.1 attention_unpack.1
  671.6 17.6 %all-gather.9.cloned.1.call-done = bf16[32,3,48,512]{3,2,1,0:T(8,128)(2,1)} async-done(((bf16[2,3,48,512]{3,2,1,0:T(8,128)(2,1)}), bf16[32,3,48,512]{3,2,1,0:T(8,128)(2,1)}) %all-gather.9.cloned.1.call-update) | async-done | bytes 4718608 | tf_op jit(solution)/shard_map/all_gather | solution.py:1267
  689.2 2.3 copy-done.6
  691.5 6.4 place.5
  (311 shorter events, 113.7 us)
Async XLA Ops:
  7.2 387.0 %reduce-scatter.2.cloned.1.call-start = ((), (), s32[]{:S(2)}) async-start(), calls=%async_computation.1 | async-start | bytes 2949120 | tf_op jit(solution)/shard_map/reduce_scatter | solution.py:1312
  14.7 27.5 %collective-permute-start.1 = (bf16[4,192,768]{2,1,0:T(8,128)(2,1)S(1)}, bf16[4,192,768]{2,1,0:T(8,128)(2,1)S(1)}, u32[]{:S(2)}, u32[]{:S(2)}) collective-permute-start(bf16[4,192,768]{2,1,0:T(8,128)(2,1)S(1)} %pad_maximum_fusion), channel_id=1, source_target_pairs={{0,1},{1,0},{2,3},{3,2},{4,5},{5,4},{6,7},{7,6},{8,9},{9,8},{10,11... | collective-permute-start | bytes 3538952 | tf_op jit(solution)/shard_map/ppermute | solution.py:1165
  42.2 38.0 %collective-permute-start.5 = (bf16[2304,256]{1,0:T(8,128)(2,1)}, bf16[2304,256]{1,0:T(8,128)(2,1)}, u32[]{:S(2)}, u32[]{:S(2)}) collective-permute-start(bf16[2304,256]{1,0:T(8,128)(2,1)} %get-tuple-element.356), channel_id=1, source_target_pairs={{0,1},{1,0},{2,3},{3,2},{4,5},{5,4},{6,7},{7,6},{8,9},{9,8},{10,11... | collective-permute-start | bytes 3538952 | tf_op jit(solution)/shard_map/ppermute | solution.py:1165
  42.5 53.6 %collective-permute-start.7 = (bf16[2304,256]{1,0:T(8,128)(2,1)}, bf16[2304,256]{1,0:T(8,128)(2,1)}, u32[]{:S(2)}, u32[]{:S(2)}) collective-permute-start(bf16[2304,256]{1,0:T(8,128)(2,1)} %get-tuple-element.390), channel_id=1, source_target_pairs={{0,1},{1,0},{2,3},{3,2},{4,5},{5,4},{6,7},{7,6},{8,9},{9,8},{10,11... | collective-permute-start | bytes 3538952 | tf_op jit(solution)/shard_map/ppermute | solution.py:1165
  80.1 44.2 %collective-permute-start.6 = (bf16[2304,256]{1,0:T(8,128)(2,1)}, bf16[2304,256]{1,0:T(8,128)(2,1)}, u32[]{:S(2)}, u32[]{:S(2)}) collective-permute-start(bf16[2304,256]{1,0:T(8,128)(2,1)} %collective-permute-done.5.refs_6_.refs_10_), channel_id=1, source_target_pairs={{0,4},{1,5},{2,6},{3,7},{4,0},{5,1},{6,2},{7,3},{8,12},{9,13},{10,... | collective-permute-start | bytes 3538952 | tf_op jit(solution)/shard_map/ppermute | solution.py:1165
  96.1 29.7 %collective-permute-start.8 = (bf16[2304,256]{1,0:T(8,128)(2,1)}, bf16[2304,256]{1,0:T(8,128)(2,1)}, u32[]{:S(2)}, u32[]{:S(2)}) collective-permute-start(bf16[2304,256]{1,0:T(8,128)(2,1)} %collective-permute-done.7.refs_8_.refs_12_), channel_id=1, source_target_pairs={{0,8},{1,9},{2,10},{3,11},{4,12},{5,13},{6,14},{7,15},{8,0},{9,1},... | collective-permute-start | bytes 3538952 | tf_op jit(solution)/shard_map/ppermute | solution.py:1165
  101.8 29.3 %collective-permute-start.9 = (bf16[2304,256]{1,0:T(8,128)(2,1)}, bf16[2304,256]{1,0:T(8,128)(2,1)}, u32[]{:S(2)}, u32[]{:S(2)}) collective-permute-start(bf16[2304,256]{1,0:T(8,128)(2,1)} %get-tuple-element.376), channel_id=1, source_target_pairs={{0,1},{1,0},{2,3},{3,2},{4,5},{5,4},{6,7},{7,6},{8,9},{9,8},{10,11... | collective-permute-start | bytes 3538952 | tf_op jit(solution)/shard_map/ppermute | solution.py:1165
  102.4 34.9 %collective-permute-start.4 = (bf16[1024,768]{1,0:T(8,128)(2,1)S(1)}, bf16[1024,768]{1,0:T(8,128)(2,1)}, u32[]{:S(2)}, u32[]{:S(2)}) collective-permute-start(bf16[1024,768]{1,0:T(8,128)(2,1)S(1)} %copy-done.11), channel_id=1, source_target_pairs={{0,2},{1,3},{2,0},{3,1},{4,6},{5,7},{6,4},{7,5},{8,10},{9,11},{10,... | collective-permute-start | bytes 4718600 | tf_op jit(solution)/shard_map/ppermute | solution.py:1165
  124.3 92.6 %collective-permute-start.15 = (bf16[2304,256]{1,0:T(8,128)(2,1)}, bf16[2304,256]{1,0:T(8,128)(2,1)}, u32[]{:S(2)}, u32[]{:S(2)}) collective-permute-start(bf16[2304,256]{1,0:T(8,128)(2,1)} %get-tuple-element.423), channel_id=1, source_target_pairs={{0,1},{1,0},{2,3},{3,2},{4,5},{5,4},{6,7},{7,6},{8,9},{9,8},{10,11... | collective-permute-start | bytes 3538952 | tf_op jit(solution)/shard_map/ppermute | solution.py:1165
  135.2 82.2 %collective-permute-start.13 = (bf16[2304,256]{1,0:T(8,128)(2,1)}, bf16[2304,256]{1,0:T(8,128)(2,1)}, u32[]{:S(2)}, u32[]{:S(2)}) collective-permute-start(bf16[2304,256]{1,0:T(8,128)(2,1)} %get-tuple-element.396), channel_id=1, source_target_pairs={{0,1},{1,0},{2,3},{3,2},{4,5},{5,4},{6,7},{7,6},{8,9},{9,8},{10,11... | collective-permute-start | bytes 3538952 | tf_op jit(solution)/shard_map/ppermute | solution.py:1165
  135.3 82.6 %collective-permute-start.14 = (bf16[2304,256]{1,0:T(8,128)(2,1)}, bf16[2304,256]{1,0:T(8,128)(2,1)}, u32[]{:S(2)}, u32[]{:S(2)}) collective-permute-start(bf16[2304,256]{1,0:T(8,128)(2,1)} %get-tuple-element.411), channel_id=1, source_target_pairs={{0,1},{1,0},{2,3},{3,2},{4,5},{5,4},{6,7},{7,6},{8,9},{9,8},{10,11... | collective-permute-start | bytes 3538952 | tf_op jit(solution)/shard_map/ppermute | solution.py:1165
  137.3 80.6 %collective-permute-start.12 = (bf16[2304,256]{1,0:T(8,128)(2,1)}, bf16[2304,256]{1,0:T(8,128)(2,1)}, u32[]{:S(2)}, u32[]{:S(2)}) collective-permute-start(bf16[2304,256]{1,0:T(8,128)(2,1)} %collective-permute-done.9.refs_6_.refs_8_), channel_id=1, source_target_pairs={{0,4},{1,5},{2,6},{3,7},{4,0},{5,1},{6,2},{7,3},{8,12},{9,13},{10,... | collective-permute-start | bytes 3538952 | tf_op jit(solution)/shard_map/ppermute | solution.py:1165
  216.8 49.5 %collective-permute-start.17 = (bf16[6,384,512]{2,1,0:T(8,128)(2,1)}, bf16[6,384,512]{2,1,0:T(8,128)(2,1)}, u32[]{:S(2)}, u32[]{:S(2)}) collective-permute-start(bf16[6,384,512]{2,1,0:T(8,128)(2,1)} %get-tuple-element.428), channel_id=1, source_target_pairs={{0,1},{1,0},{2,3},{3,2},{4,5},{5,4},{6,7},{7,6},{8,9},{9,8},{10,11... | collective-permute-start | bytes 7077896 | tf_op jit(solution)/shard_map/ppermute | solution.py:1165
  216.9 49.6 %collective-permute-start.18 = (bf16[2,6,192,512]{3,2,1,0:T(8,128)(2,1)}, bf16[2,6,192,512]{3,2,1,0:T(8,128)(2,1)}, u32[]{:S(2)}, u32[]{:S(2)}) collective-permute-start(bf16[2,6,192,512]{3,2,1,0:T(8,128)(2,1)} %get-tuple-element.430), channel_id=1, source_target_pairs={{0,4},{1,5},{2,6},{3,7},{4,0},{5,1},{6,2},{7,3},{8,12},{9,13},{10,... | collective-permute-start | bytes 7077896 | tf_op jit(solution)/shard_map/ppermute | solution.py:1165
  217.5 62.1 %collective-permute-start.16 = (bf16[2304,256]{1,0:T(8,128)(2,1)}, bf16[2304,256]{1,0:T(8,128)(2,1)}, u32[]{:S(2)}, u32[]{:S(2)}) collective-permute-start(bf16[2304,256]{1,0:T(8,128)(2,1)} %collective-permute-done.15.refs_6_.refs_8_), channel_id=1, source_target_pairs={{0,8},{1,9},{2,10},{3,11},{4,12},{5,13},{6,14},{7,15},{8,0},{9,1},... | collective-permute-start | bytes 3538952 | tf_op jit(solution)/shard_map/ppermute | solution.py:1165
  276.5 54.7 %collective-permute-start.22 = (bf16[6,192,512]{2,1,0:T(8,128)(2,1)}, bf16[6,192,512]{2,1,0:T(8,128)(2,1)}, u32[]{:S(2)}, u32[]{:S(2)}) collective-permute-start(bf16[6,192,512]{2,1,0:T(8,128)(2,1)} %get-tuple-element.437), channel_id=1, source_target_pairs={{0,4},{1,5},{2,6},{3,7},{4,0},{5,1},{6,2},{7,3},{8,12},{9,13},{10,... | collective-permute-start | bytes 3538952 | tf_op jit(solution)/shard_map/ppermute | solution.py:1165
  279.6 51.6 %collective-permute-start.23 = (bf16[6,192,512]{2,1,0:T(8,128)(2,1)}, bf16[6,192,512]{2,1,0:T(8,128)(2,1)}, u32[]{:S(2)}, u32[]{:S(2)}) collective-permute-start(bf16[6,192,512]{2,1,0:T(8,128)(2,1)} %get-tuple-element.462), channel_id=1, source_target_pairs={{0,1},{1,0},{2,3},{3,2},{4,5},{5,4},{6,7},{7,6},{8,9},{9,8},{10,11... | collective-permute-start | bytes 3538952 | tf_op jit(solution)/shard_map/ppermute | solution.py:1165
  281.1 55.6 %collective-permute-start.21 = (bf16[2,3,192,512]{3,2,1,0:T(8,128)(2,1)}, bf16[2,3,192,512]{3,2,1,0:T(8,128)(2,1)}, u32[]{:S(2)}, u32[]{:S(2)}) collective-permute-start(bf16[2,3,192,512]{3,2,1,0:T(8,128)(2,1)} %get-tuple-element.459), channel_id=1, source_target_pairs={{0,4},{1,5},{2,6},{3,7},{4,0},{5,1},{6,2},{7,3},{8,12},{9,13},{10,... | collective-permute-start | bytes 3538952 | tf_op jit(solution)/shard_map/ppermute | solution.py:1165
  282.7 54.1 %collective-permute-start.20 = (bf16[3,384,512]{2,1,0:T(8,128)(2,1)}, bf16[3,384,512]{2,1,0:T(8,128)(2,1)}, u32[]{:S(2)}, u32[]{:S(2)}) collective-permute-start(bf16[3,384,512]{2,1,0:T(8,128)(2,1)} %get-tuple-element.455), channel_id=1, source_target_pairs={{0,1},{1,0},{2,3},{3,2},{4,5},{5,4},{6,7},{7,6},{8,9},{9,8},{10,11... | collective-permute-start | bytes 3538952 | tf_op jit(solution)/shard_map/ppermute | solution.py:1165
  327.4 74.8 %collective-permute-start.24 = (bf16[2,1024,768]{2,1,0:T(8,128)(2,1)}, bf16[2,1024,768]{2,1,0:T(8,128)(2,1)}, u32[]{:S(2)}, u32[]{:S(2)}) collective-permute-start(bf16[2,1024,768]{2,1,0:T(8,128)(2,1)} %add_convert_fusion), channel_id=1, source_target_pairs={{0,2},{1,3},{2,0},{3,1},{4,6},{5,7},{6,4},{7,5},{8,10},{9,11},{10,... | collective-permute-start | bytes 9437192 | tf_op jit(solution)/shard_map/ppermute | solution.py:1165
  336.7 194.2 %all-gather.5.cloned.1.call-start = ((), (), s32[]{:S(2)}) async-start(), calls=%async_computation.2 | async-start | bytes 10027008 | tf_op jit(solution)/shard_map/all_gather | solution.py:1267
  343.0 69.4 %collective-permute-start.28 = (bf16[3,192,512]{2,1,0:T(8,128)(2,1)}, bf16[3,192,512]{2,1,0:T(8,128)(2,1)}, u32[]{:S(2)}, u32[]{:S(2)}) collective-permute-start(bf16[3,192,512]{2,1,0:T(8,128)(2,1)} %get-tuple-element.473), channel_id=1, source_target_pairs={{0,4},{1,5},{2,6},{3,7},{4,0},{5,1},{6,2},{7,3},{8,12},{9,13},{10,... | collective-permute-start | bytes 1769480 | tf_op jit(solution)/shard_map/ppermute | solution.py:1165
  343.5 50.0 %collective-permute-start.27 = (bf16[2,3,192,512]{3,2,1,0:T(8,128)(2,1)}, bf16[2,3,192,512]{3,2,1,0:T(8,128)(2,1)}, u32[]{:S(2)}, u32[]{:S(2)}) collective-permute-start(bf16[2,3,192,512]{3,2,1,0:T(8,128)(2,1)} %get-tuple-element.494), channel_id=1, source_target_pairs={{0,4},{1,5},{2,6},{3,7},{4,0},{5,1},{6,2},{7,3},{8,12},{9,13},{10,... | collective-permute-start | bytes 3538952 | tf_op jit(solution)/shard_map/ppermute | solution.py:1165
  345.1 49.1 %collective-permute-start.26 = (bf16[3,384,512]{2,1,0:T(8,128)(2,1)}, bf16[3,384,512]{2,1,0:T(8,128)(2,1)}, u32[]{:S(2)}, u32[]{:S(2)}) collective-permute-start(bf16[3,384,512]{2,1,0:T(8,128)(2,1)} %get-tuple-element.490), channel_id=1, source_target_pairs={{0,1},{1,0},{2,3},{3,2},{4,5},{5,4},{6,7},{7,6},{8,9},{9,8},{10,11... | collective-permute-start | bytes 3538952 | tf_op jit(solution)/shard_map/ppermute | solution.py:1165
  393.5 18.9 %collective-permute-start.29 = (bf16[3,192,512]{2,1,0:T(8,128)(2,1)}, bf16[3,192,512]{2,1,0:T(8,128)(2,1)S(1)}, u32[]{:S(2)}, u32[]{:S(2)}) collective-permute-start(bf16[3,192,512]{2,1,0:T(8,128)(2,1)} %copy-done.58), channel_id=1, source_target_pairs={{0,1},{1,0},{2,3},{3,2},{4,5},{5,4},{6,7},{7,6},{8,9},{9,8},{10,11... | collective-permute-start | bytes 1769480 | tf_op jit(solution)/shard_map/ppermute | solution.py:1165
  394.2 242.1 %all-gather.7.cloned.1.call-start = ((), (), s32[]{:S(2)}) async-start(), calls=%async_computation.3 | async-start | bytes 10027008 | tf_op jit(solution)/shard_map/all_gather | solution.py:1267
  401.8 56.7 %collective-permute-start.30 = (bf16[3,192,512]{2,1,0:T(8,128)(2,1)}, bf16[3,192,512]{2,1,0:T(8,128)(2,1)S(1)}, u32[]{:S(2)}, u32[]{:S(2)}) collective-permute-start(bf16[3,192,512]{2,1,0:T(8,128)(2,1)} %get-tuple-element.500), channel_id=1, source_target_pairs={{0,4},{1,5},{2,6},{3,7},{4,0},{5,1},{6,2},{7,3},{8,12},{9,13},{10,... | collective-permute-start | bytes 1769480 | tf_op jit(solution)/shard_map/ppermute | solution.py:1165
  402.2 56.3 %collective-permute-start.31 = (bf16[3,192,512]{2,1,0:T(8,128)(2,1)S(1)}, bf16[3,192,512]{2,1,0:T(8,128)(2,1)S(1)}, u32[]{:S(2)}, u32[]{:S(2)}) collective-permute-start(bf16[3,192,512]{2,1,0:T(8,128)(2,1)S(1)} %get-tuple-element.548), channel_id=1, source_target_pairs={{0,1},{1,0},{2,3},{3,2},{4,5},{5,4},{6,7},{7,6},{8,9},{9,8},{10,11... | collective-permute-start | bytes 1769480 | tf_op jit(solution)/shard_map/ppermute | solution.py:1165
  415.1 42.6 %collective-permute-start.32 = (bf16[2,3,48,512]{3,2,1,0:T(8,128)(2,1)S(1)}, bf16[2,3,48,512]{3,2,1,0:T(8,128)(2,1)S(1)}, u32[]{:S(2)}, u32[]{:S(2)}) collective-permute-start(bf16[2,3,48,512]{3,2,1,0:T(8,128)(2,1)S(1)} %get-tuple-element.549), channel_id=1, source_target_pairs={{0,8},{1,9},{2,10},{3,11},{4,12},{5,13},{6,14},{7,15},{8,0},{9,1},... | collective-permute-start | bytes 884744 | tf_op jit(solution)/shard_map/ppermute | solution.py:1165
  415.7 42.0 %collective-permute-start.33 = (bf16[2,3,48,512]{3,2,1,0:T(8,128)(2,1)S(1)}, bf16[2,3,48,512]{3,2,1,0:T(8,128)(2,1)S(1)}, u32[]{:S(2)}, u32[]{:S(2)}) collective-permute-start(bf16[2,3,48,512]{3,2,1,0:T(8,128)(2,1)S(1)} %get-tuple-element.550), channel_id=1, source_target_pairs={{0,16},{1,17},{2,18},{3,19},{4,20},{5,21},{6,22},{7,23},{8,24},{9,... | collective-permute-start | bytes 884744 | tf_op jit(solution)/shard_map/ppermute | solution.py:1165
  418.3 39.5 %collective-permute-start.34 = (bf16[2,3,48,512]{3,2,1,0:T(8,128)(2,1)S(1)}, bf16[2,3,48,512]{3,2,1,0:T(8,128)(2,1)S(1)}, u32[]{:S(2)}, u32[]{:S(2)}) collective-permute-start(bf16[2,3,48,512]{3,2,1,0:T(8,128)(2,1)S(1)} %get-tuple-element.551), channel_id=1, source_target_pairs={{0,24},{1,25},{2,26},{3,27},{4,28},{5,29},{6,30},{7,31},{8,16},{9,... | collective-permute-start | bytes 884744 | tf_op jit(solution)/shard_map/ppermute | solution.py:1165
  460.1 53.1 %collective-permute-start.38 = (bf16[2,3,48,512]{3,2,1,0:T(8,128)(2,1)}, bf16[2,3,48,512]{3,2,1,0:T(8,128)(2,1)S(1)}, u32[]{:S(2)}, u32[]{:S(2)}) collective-permute-start(bf16[2,3,48,512]{3,2,1,0:T(8,128)(2,1)} %get-tuple-element.610), channel_id=1, source_target_pairs={{0,8},{1,9},{2,10},{3,11},{4,12},{5,13},{6,14},{7,15},{8,0},{9,1},... | collective-permute-start | bytes 884744 | tf_op jit(solution)/shard_map/ppermute | solution.py:1165
  475.4 37.9 %collective-permute-start.39 = (bf16[2,3,48,512]{3,2,1,0:T(8,128)(2,1)}, bf16[2,3,48,512]{3,2,1,0:T(8,128)(2,1)S(1)}, u32[]{:S(2)}, u32[]{:S(2)}) collective-permute-start(bf16[2,3,48,512]{3,2,1,0:T(8,128)(2,1)} %get-tuple-element.611), channel_id=1, source_target_pairs={{0,16},{1,17},{2,18},{3,19},{4,20},{5,21},{6,22},{7,23},{8,24},{9,... | collective-permute-start | bytes 884744 | tf_op jit(solution)/shard_map/ppermute | solution.py:1165
  477.4 35.9 %collective-permute-start.40 = (bf16[2,3,48,512]{3,2,1,0:T(8,128)(2,1)}, bf16[2,3,48,512]{3,2,1,0:T(8,128)(2,1)}, u32[]{:S(2)}, u32[]{:S(2)}) collective-permute-start(bf16[2,3,48,512]{3,2,1,0:T(8,128)(2,1)} %get-tuple-element.612), channel_id=1, source_target_pairs={{0,24},{1,25},{2,26},{3,27},{4,28},{5,29},{6,30},{7,31},{8,16},{9,... | collective-permute-start | bytes 884744 | tf_op jit(solution)/shard_map/ppermute | solution.py:1165
  478.8 37.1 %collective-permute-start.37 = (bf16[2,3,192,512]{3,2,1,0:T(8,128)(2,1)}, bf16[2,3,192,512]{3,2,1,0:T(8,128)(2,1)}, u32[]{:S(2)}, u32[]{:S(2)}) collective-permute-start(bf16[2,3,192,512]{3,2,1,0:T(8,128)(2,1)} %get-tuple-element.609), channel_id=1, source_target_pairs={{0,4},{1,5},{2,6},{3,7},{4,0},{5,1},{6,2},{7,3},{8,12},{9,13},{10,... | collective-permute-start | bytes 3538952 | tf_op jit(solution)/shard_map/ppermute | solution.py:1165
  479.3 36.6 %collective-permute-start.36 = (bf16[3,384,512]{2,1,0:T(8,128)(2,1)}, bf16[3,384,512]{2,1,0:T(8,128)(2,1)}, u32[]{:S(2)}, u32[]{:S(2)}) collective-permute-start(bf16[3,384,512]{2,1,0:T(8,128)(2,1)} %get-tuple-element.605), channel_id=1, source_target_pairs={{0,1},{1,0},{2,3},{3,2},{4,5},{5,4},{6,7},{7,6},{8,9},{9,8},{10,11... | collective-permute-start | bytes 3538952 | tf_op jit(solution)/shard_map/ppermute | solution.py:1165
  515.8 173.4 %all-gather.9.cloned.1.call-start = ((), (), s32[]{:S(2)}) async-start(), calls=%async_computation.4 | async-start | bytes 5013504 | tf_op jit(solution)/shard_map/all_gather | solution.py:1267
  523.6 22.5 %collective-permute-start.42 = (bf16[3,192,512]{2,1,0:T(8,128)(2,1)}, bf16[3,192,512]{2,1,0:T(8,128)(2,1)}, u32[]{:S(2)}, u32[]{:S(2)}) collective-permute-start(bf16[3,192,512]{2,1,0:T(8,128)(2,1)} %get-tuple-element.623), channel_id=1, source_target_pairs={{0,4},{1,5},{2,6},{3,7},{4,0},{5,1},{6,2},{7,3},{8,12},{9,13},{10,... | collective-permute-start | bytes 1769480 | tf_op jit(solution)/shard_map/ppermute | solution.py:1165
  524.1 21.9 %collective-permute-start.43 = (bf16[3,192,512]{2,1,0:T(8,128)(2,1)}, bf16[3,192,512]{2,1,0:T(8,128)(2,1)}, u32[]{:S(2)}, u32[]{:S(2)}) collective-permute-start(bf16[3,192,512]{2,1,0:T(8,128)(2,1)} %get-tuple-element.631), channel_id=1, source_target_pairs={{0,1},{1,0},{2,3},{3,2},{4,5},{5,4},{6,7},{7,6},{8,9},{9,8},{10,11... | collective-permute-start | bytes 1769480 | tf_op jit(solution)/shard_map/ppermute | solution.py:1165
  530.0 37.2 %collective-permute-start.41 = (bf16[1,384,1664]{2,1,0:T(8,128)(2,1)}, bf16[1,384,1664]{2,1,0:T(8,128)(2,1)}, u32[]{:S(2)}, u32[]{:S(2)}) collective-permute-start(bf16[1,384,1664]{2,1,0:T(8,128)(2,1)} %get-tuple-element.628), channel_id=1, source_target_pairs={{0,1},{1,0},{2,3},{3,2},{4,5},{5,4},{6,7},{7,6},{8,9},{9,8},{10,11... | collective-permute-start | bytes 3833864 | tf_op jit(solution)/shard_map/ppermute | solution.py:1165
  548.3 22.7 %collective-permute-start.45 = (bf16[2,3,48,512]{3,2,1,0:T(8,128)(2,1)S(1)}, bf16[2,3,48,512]{3,2,1,0:T(8,128)(2,1)S(1)}, u32[]{:S(2)}, u32[]{:S(2)}) collective-permute-start(bf16[2,3,48,512]{3,2,1,0:T(8,128)(2,1)S(1)} %get-tuple-element.645), channel_id=1, source_target_pairs={{0,8},{1,9},{2,10},{3,11},{4,12},{5,13},{6,14},{7,15},{8,0},{9,1},... | collective-permute-start | bytes 884744 | tf_op jit(solution)/shard_map/ppermute | solution.py:1165
  551.7 35.4 %collective-permute-start.46 = (bf16[2,3,48,512]{3,2,1,0:T(8,128)(2,1)S(1)}, bf16[2,3,48,512]{3,2,1,0:T(8,128)(2,1)S(1)}, u32[]{:S(2)}, u32[]{:S(2)}) collective-permute-start(bf16[2,3,48,512]{3,2,1,0:T(8,128)(2,1)S(1)} %get-tuple-element.646), channel_id=1, source_target_pairs={{0,16},{1,17},{2,18},{3,19},{4,20},{5,21},{6,22},{7,23},{8,24},{9,... | collective-permute-start | bytes 884744 | tf_op jit(solution)/shard_map/ppermute | solution.py:1165
  552.5 34.6 %collective-permute-start.47 = (bf16[2,3,48,512]{3,2,1,0:T(8,128)(2,1)S(1)}, bf16[2,3,48,512]{3,2,1,0:T(8,128)(2,1)S(1)}, u32[]{:S(2)}, u32[]{:S(2)}) collective-permute-start(bf16[2,3,48,512]{3,2,1,0:T(8,128)(2,1)S(1)} %get-tuple-element.647), channel_id=1, source_target_pairs={{0,24},{1,25},{2,26},{3,27},{4,28},{5,29},{6,30},{7,31},{8,16},{9,... | collective-permute-start | bytes 884744 | tf_op jit(solution)/shard_map/ppermute | solution.py:1165
  569.4 27.9 %collective-permute-start.44 = (bf16[1,192,1664]{2,1,0:T(8,128)(2,1)S(1)}, bf16[1,192,1664]{2,1,0:T(8,128)(2,1)S(1)}, u32[]{:S(2)}, u32[]{:S(2)}) collective-permute-start(bf16[1,192,1664]{2,1,0:T(8,128)(2,1)S(1)} %get-tuple-element.644), channel_id=1, source_target_pairs={{0,4},{1,5},{2,6},{3,7},{4,0},{5,1},{6,2},{7,3},{8,12},{9,13},{10,... | collective-permute-start | bytes 1916936 | tf_op jit(solution)/shard_map/ppermute | solution.py:1165
  598.0 20.4 %collective-permute-start.48 = (bf16[1,48,1664]{2,1,0:T(8,128)(2,1)S(1)}, bf16[1,48,1664]{2,1,0:T(8,128)(2,1)S(1)}, u32[]{:S(2)}, u32[]{:S(2)}) collective-permute-start(bf16[1,48,1664]{2,1,0:T(8,128)(2,1)S(1)} %get-tuple-element.657), channel_id=1, source_target_pairs={{0,8},{1,9},{2,10},{3,11},{4,12},{5,13},{6,14},{7,15},{8,0},{9,1},... | collective-permute-start | bytes 479240 | tf_op jit(solution)/shard_map/ppermute | solution.py:1165
  608.2 18.0 %collective-permute-start.49 = (bf16[1,48,1664]{2,1,0:T(8,128)(2,1)S(1)}, bf16[1,48,1664]{2,1,0:T(8,128)(2,1)S(1)}, u32[]{:S(2)}, u32[]{:S(2)}) collective-permute-start(bf16[1,48,1664]{2,1,0:T(8,128)(2,1)S(1)} %get-tuple-element.658), channel_id=1, source_target_pairs={{0,16},{1,17},{2,18},{3,19},{4,20},{5,21},{6,22},{7,23},{8,24},{9,... | collective-permute-start | bytes 479240 | tf_op jit(solution)/shard_map/ppermute | solution.py:1165
  634.9 26.4 %collective-permute-start.54 = (bf16[1,48,1664]{2,1,0:T(8,128)(2,1)}, bf16[1,48,1664]{2,1,0:T(8,128)(2,1)}, u32[]{:S(2)}, u32[]{:S(2)}) collective-permute-start(bf16[1,48,1664]{2,1,0:T(8,128)(2,1)} %sum_z.1.refs_0_), channel_id=1, source_target_pairs={{0,4},{1,5},{2,6},{3,7},{4,0},{5,1},{6,2},{7,3},{8,12},{9,13},{10,... | collective-permute-start | bytes 479240 | tf_op jit(solution)/shard_map/ppermute | solution.py:1165
  638.5 22.7 %collective-permute-start.55 = (bf16[1,48,1664]{2,1,0:T(8,128)(2,1)}, bf16[1,48,1664]{2,1,0:T(8,128)(2,1)}, u32[]{:S(2)}, u32[]{:S(2)}) collective-permute-start(bf16[1,48,1664]{2,1,0:T(8,128)(2,1)} %collective-permute-done.51.refs_1_), channel_id=1, source_target_pairs={{0,4},{1,5},{2,6},{3,7},{4,0},{5,1},{6,2},{7,3},{8,12},{9,13},{10,... | collective-permute-start | bytes 479240 | tf_op jit(solution)/shard_map/ppermute | solution.py:1165
  (88 other events, 1011.4 us)
Sparse Core Ops, SparseCore 0:
  336.8 47.2 reduce-scatter.1
  394.3 118.6 all-gather.4
  516.0 116.0 all-gather.6
  635.0 54.1 all-gather.8

commit v4 on v3

--- a/solution.py
+++ b/solution.py
@@ -129,7 +129,7 @@
     pair = pl.BlockSpec((length, PAIR), lambda p: (0, p))
     wide = jax.ShapeDtypeStruct((length, D), BF)
     weight = pl.BlockSpec((half, PAIR), lambda p: (0, p))
-    part = pl.BlockSpec((4, half // 2, PAIR), lambda p: (0, 0, p))
+    part = pl.BlockSpec((3, half // 2, PAIR), lambda p: (0, 0, p))
     return pl.pallas_call(
         attend_forward_body,
         cost_estimate=DEAR,
@@ -384,8 +384,8 @@
             rows,
             rows,
             resident((D // 2, D)),
-            pl.BlockSpec((None, D // 4, D), lambda i: (3, 0, 0), pipeline_mode=pl.Buffered(1)),
-            pl.BlockSpec((None, D // 4, D), lambda i: (3, 0, 0), pipeline_mode=pl.Buffered(1)),
+            resident((D // 4, D)),
+            resident((D // 4, D)),
             resident((1, D)),
             resident((8, D)),
             cols,
@@ -1206,7 +1206,7 @@
     tiny = jnp.concatenate([norm1_gain[None], norm2_gain[None], router.T], axis=0)
     tiny = jnp.pad(tiny, ((0, 8 - tiny.shape[0]), (0, 0)))
     tiny_got = over_x(tiny)
-    small_mine = over_x(later(jnp.stack([rows_c(w_query), rows_c(w_key), rows_c(w_value), rows_c(w_out)]), tiny_got))
+    small_mine = over_x(later(jnp.stack([rows_c(w_query), rows_c(w_key), rows_c(w_value)]), tiny_got))
     tiny_full = in_order(shard, tiny, tiny_got, 1)
     gain_one = tiny_full[0:1].astype(F32)
     gain_two = tiny_full[1:2].astype(F32)
@@ -1234,16 +1234,19 @@
     tables = rotary_tables(length)
     routes_t = jnp.pad(routes.T, ((0, 6), (0, 0)))
 
+    out_mine = over_x(rows_c(w_out))
     first_w = fetch(experts_w, ((0, 0), (1, 0)), 2, core * per_core)
     small_theirs = over_core(later(small_mine, held[0]))
+    out_theirs = over_core(out_mine)
     q, k, v, mixed, lse, wqkv = in_turn(
         attend_forward, where, pic_block, tokens, gain_one, (w_query, w_key, w_value), small_mine, small_theirs, tables,
+        need=(out_mine,),
     )
     first_w = [later(v, q) for v in first_w]
     first_w = (first_w[0], over_y(first_w[0]), first_w[1], over_z(first_w[1], 1))
     second_w = fetch(experts_w, ((0, 0), (1, 0)), 2, core * per_core + 1)
     resid, n2, n2p, comb, wout = in_turn(
-        middle, where, tokens, mixed, w_out, small_mine, small_theirs, gain_two, router_t8, routes_t,
+        middle, where, tokens, mixed, w_out, out_mine, out_theirs, gain_two, router_t8, routes_t,
     )
     toks = (n2p, over_core(n2p))
     shared_fetched = fetch(

time: 710 us -> 704 us (level)
  waiting for transfers between devices: 129 us -> 120 us
    ppermute x59 -> x61, waiting for transfers between devices: 111 us -> 103 us  [swap(): return lax.ppermute(value, ALL, perm)]
    ppermute x59 -> x61, starting transfers between devices: 90.5 us -> 94.8 us  [swap(): return lax.ppermute(value, ALL, perm)]
    unnamed x152 -> x142, local copies, waits for them, and re-layouts: 39.3 us -> 36.8 us
  transfers between devices with their start and end apart: 63 -> 65, of which waited for: 16 -> 17; matrix products, arithmetic and copies ran while one was open for 3% -> 3% of each run, Pallas kernels for 57% -> 58%
where the time goes in v4:
time: 704 us; the launch traced here: 699 us
  Pallas kernels  409 us (58%)
  waiting for transfers between devices  120 us (17%)
  starting transfers between devices  95 us (13%)
  local copies, waits for them, and re-layouts  48.2 us (7%)
  between operations  15.5 us (2%)
  other arithmetic  10.1 us (1%)
    pallas_call x4, Pallas kernels, ffn(): pl.pallas_call(functools.partial(ffn_body, routed, steps, chunk, before i...  209 us
    ppermute x61, waiting for transfers between devices, swap(): return lax.ppermute(value, ALL, perm)  103 us
    ppermute x61, starting transfers between devices, swap(): return lax.ppermute(value, ALL, perm)  94.8 us
    pallas_call x2, Pallas kernels, attend_backward(): pl.pallas_call(functools.partial(attend_backward_body, last), cost_estima...  64 us
    pallas_call x16, Pallas kernels, small_call(): pl.pallas_call(body, cost_estimate=cost, grid_spec=pltpu.PrefetchScalarGr...  44.5 us
    unnamed x142, local copies, waits for them, and re-layouts  36.8 us
    pallas_call x1, Pallas kernels, attend_forward(): pl.pallas_call(attend_forward_body, cost_estimate=DEAR, grid=(PAIRS,), in...  30.5 us
    pallas_call x3, Pallas kernels, place(): pl.pallas_call(body, cost_estimate=cost, grid_spec=pltpu.PrefetchScalarGr...  29.2 us
  transfers between devices with their start and end apart: 65, of which 17 were waited for; matrix products, arithmetic and copies ran while one was open for 3% of the time, Pallas kernels for 58%

profile of v4, /device:TPU:0, one launch (start us, length us, event | category | flops | bytes accessed | tf_op | source)
XLA Modules:
  0.0 698.5 jit_solution(951640020215178514)
XLA Ops:
  9.3 3.0 collective-permute-start
  17.4 4.1 pack.3
  23.5 13.7 %collective-permute-done.1.mine = bf16[3,192,768]{2,1,0:T(8,128)(2,1)S(1)} collective-permute-done((bf16[3,192,768]{2,1,0:T(8,128)(2,1)S(1)}, bf16[3,192,768]{2,1,0:T(8,128)(2,1)S(1)}, u32[]{:S(2)}, u32[]{:S(2)}) %collective-permute-start.1) | collective-permute-done | bytes 884768 | tf_op jit(solution)/shard_map/ppermute | solution.py:1165
  43.6 30.5 %attend_forward.1 = (bf16[1024,768]{1,0:T(8,128)(2,1)}, bf16[1024,768]{1,0:T(8,128)(2,1)}, bf16[1024,768]{1,0:T(8,128)(2,1)}, bf16[1024,768]{1,0:T(8,128)(2,1)},...) custom-call(s32[6]{0:T(128)S(1)} %copy-done.34, s32[1]{0:T(128)S(6)} %copy.98.pic, bf16[1024,768]{1,0:T(8,128)(2,1)} %tok.3, ...), custom_call_target="tpu_custom_call" | custom-call | flops 68719476736 | bytes 1 | tf_op jit(solution)/shard_map/attend_forward/pallas_call | solution.py:133
  76.3 16.4 %collective-permute-done.7.refs_6_.refs_10_ = bf16[2304,256]{1,0:T(8,128)(2,1)} collective-permute-done((bf16[2304,256]{1,0:T(8,128)(2,1)}, bf16[2304,256]{1,0:T(8,128)(2,1)}, u32[]{:S(2)}, u32[]{:S(2)}) %collective-permute-start.7) | collective-permute-done | bytes 1179680 | tf_op jit(solution)/shard_map/ppermute | solution.py:1165
  94.2 4.1 pack.4
  105.0 4.4 middle.1
  121.0 6.1 collective-permute-done.11.refs_6_.refs_8_
  127.1 4.1 pack.5
  133.9 77.8 %ffn_routed.3 = (bf16[2,1024,768]{2,1,0:T(8,128)(2,1)}, bf16[2,1024,768]{2,1,0:T(8,128)(2,1)}, f32[2,1024]{1,0:T(2,128)}, bf16[6,384,512]{2,1,0:T(8,128)(2,1)}, ...) custom-call(s32[6]{0:T(128)} %stack.56.w.where.shard, ...), custom_call_target="tpu_custom_call" | custom-call | flops 68719476736 | bytes 1 | tf_op jit(solution)/shard_map/ffn_routed/pallas_call | solution.py:722
  214.9 42.3 %ffn_routed.4 = (bf16[2,1024,768]{2,1,0:T(8,128)(2,1)}, bf16[2,1024,768]{2,1,0:T(8,128)(2,1)}, f32[2,1024]{1,0:T(2,128)}, bf16[3,384,512]{2,1,0:T(8,128)(2,1)}, ...) custom-call(s32[6]{0:T(128)} %stack.120.w.where, ...), custom_call_target="tpu_custom_call" | custom-call | flops 68719476736 | bytes 1 | tf_op jit(solution)/shard_map/ffn_routed/pallas_call | solution.py:722
  257.2 2.4 collective-permute-done.19.g_m.g_o
  263.0 6.6 pair_first.4
  271.2 2.5 add_convert_fusion
  276.4 42.1 %ffn_routed.5 = (bf16[2,1024,768]{2,1,0:T(8,128)(2,1)}, bf16[2,1024,768]{2,1,0:T(8,128)(2,1)}, f32[2,1024]{1,0:T(2,128)}, bf16[3,384,512]{2,1,0:T(8,128)(2,1)}, ...) custom-call(s32[6]{0:T(128)} %stack.120.w.where, ...), custom_call_target="tpu_custom_call" | custom-call | flops 68719476736 | bytes 1 | tf_op jit(solution)/shard_map/ffn_routed/pallas_call | solution.py:722
  325.1 4.7 pair_scatter.1
  331.4 3.9 pair_first.5
  339.9 46.9 %ffn_shared.1 = (bf16[2,1024,768]{2,1,0:T(8,128)(2,1)}, bf16[2,1024,768]{2,1,0:T(8,128)(2,1)}, bf16[3,384,512]{2,1,0:T(8,128)(2,1)}, bf16[3,384,512]{2,1,0:T(8,1...) custom-call(s32[6]{0:T(128)} %stack.56.w.where.shard, bf16[1024,768]{1,0:T(8,128)(2,1)} %copy-done.49, ...), custom_call_target="tpu_custom_call" | custom-call | flops 68719476736 | bytes 1 | tf_op jit(solution)/shard_map/ffn_shared/pallas_call | solution.py:722
  390.0 4.2 pair_first.6
  397.5 8.7 %join.1 = (bf16[1024,768]{1,0:T(8,128)(2,1)}, f32[1024,768]{1,0:T(8,128)S(1)}, bf16[1024,768]{1,0:T(8,128)(2,1)S(1)}, f32[1,768]{1,0:T(1,128)S(1)}) custom-call(s32[6]{0:T(128)S(1)} %copy-done.36, bf16[1024,768]{1,0:T(8,128)(2,1)S(1)} %copy-done.12, f32[1024,768]{1,0:T(8,128)S(1)} %copy-done.8, f32[1,768]{1,0:T(1,128)S(1)} %get-tuple-element.504.gain, ...), custom_call_target="tpu_custom_call" | custom-call | flops 1 | bytes 1 | tf_op jit(solution)/shard_map/join/pallas_call | solution.py:444
  406.3 2.7 pair_second.3
  410.7 2.6 collective-permute-start.35
  413.5 38.1 %attend_backward_1.1 = (bf16[384,1536]{1,0:T(8,128)(2,1)}, bf16[384,1536]{1,0:T(8,128)(2,1)}, bf16[512,768]{1,0:T(8,128)(2,1)}, f32[1024,768]{1,0:T(8,128)}) custom-call(s32[6]{0:T(128)} %stack.56.w.where.shard, s32[1]{0:T(128)S(6)} %copy.98.pic, bf16[1024,768]{1,0:T(8,128)(2,1)} %tok.3, f32[1,768]{1,0:T(1,128)} %copy-done.45, ...), custom_call_target="tpu_custom_call" | custom-call | flops 68719476736 | bytes 1 | tf_op jit(solution)/shard_map/attend_backward_1/pallas_call | solution.py:304
  455.5 2.7 collective-permute-start.41
  459.7 25.8 %attend_backward_2.1 = (bf16[384,768]{1,0:T(8,128)(2,1)}, bf16[384,768]{1,0:T(8,128)(2,1)}, bf16[256,768]{1,0:T(8,128)(2,1)}, f32[1024,768]{1,0:T(8,128)}, f32[1,768]{1,0:T(1,128)}) custom-call(s32[6]{0:T(128)} %stack.56.w.where.shard, s32[1]{0:T(128)S(6)} %copy.98.pic, bf16[1024,768]{1,0:T(8,128)(2,1)} %tok.3, f32[1,768]{1,0:T(1,128)} %copy-done.45, ...), custom_call_target="tpu_custom_call" | custom-call | flops 68719476736 | bytes 1 | tf_op jit(solution)/shard_map/attend_backward_2/pallas_call | solution.py:304
  489.4 2.6 attention_pack.1
  492.0 4.8 collective-permute-done.42.d
  502.0 4.3 pair_first.7
  508.1 3.6 attention_sum.1
  514.5 3.7 copy-done.46
  518.2 11.4 %place.3 = (f32[4,384,2048]{2,1,0:T(8,128)}, f32[4,384,2048]{2,1,0:T(8,128)}, f32[4,1024,768]{2,1,0:T(8,128)}) custom-call(s32[6]{0:T(128)S(1)} %copy-done.38, bf16[8,2,2,6,48,512]{5,4,3,2,1,0:T(8,128)(2,1)S(1)} %bitcast.60), custom_call_target="tpu_custom_call" | custom-call | flops 274877906944 | bytes 1 | tf_op jit(solution)/shard_map/place/pallas_call | solution.py:1113
  531.9 14.8 %collective-permute-start.47 = (bf16[2,3,48,512]{3,2,1,0:T(8,128)(2,1)S(1)}, bf16[2,3,48,512]{3,2,1,0:T(8,128)(2,1)S(1)}, u32[]{:S(2)}, u32[]{:S(2)}) collective-permute-start(bf16[2,3,48,512]{3,2,1,0:T(8,128)(2,1)S(1)} %get-tuple-element.645), channel_id=1, source_target_pairs={{0,8},{1,9},{2,10},{3,11},{4,12},{5,13},{6,14},{7,15},{8,0},{9,1},... | collective-permute-start | bytes 884744 | tf_op jit(solution)/shard_map/ppermute | solution.py:1165
  552.3 9.3 %collective-permute-done.47.b = bf16[2,3,48,512]{3,2,1,0:T(8,128)(2,1)S(1)} collective-permute-done((bf16[2,3,48,512]{3,2,1,0:T(8,128)(2,1)S(1)}, bf16[2,3,48,512]{3,2,1,0:T(8,128)(2,1)S(1)}, u32[]{:S(2)}, u32[]{:S(2)}) %collective-permute-start.47) | collective-permute-done | bytes 294944 | tf_op jit(solution)/shard_map/ppermute | solution.py:1165
  561.6 19.6 %collective-permute-done.48.c = bf16[2,3,48,512]{3,2,1,0:T(8,128)(2,1)S(1)} collective-permute-done((bf16[2,3,48,512]{3,2,1,0:T(8,128)(2,1)S(1)}, bf16[2,3,48,512]{3,2,1,0:T(8,128)(2,1)S(1)}, u32[]{:S(2)}, u32[]{:S(2)}) %collective-permute-start.48) | collective-permute-done | bytes 294944 | tf_op jit(solution)/shard_map/ppermute | solution.py:1165
  583.3 16.9 %collective-permute-start.50 = (bf16[1,48,1664]{2,1,0:T(8,128)(2,1)S(1)}, bf16[1,48,1664]{2,1,0:T(8,128)(2,1)S(1)}, u32[]{:S(2)}, u32[]{:S(2)}) collective-permute-start(bf16[1,48,1664]{2,1,0:T(8,128)(2,1)S(1)} %get-tuple-element.657), channel_id=1, source_target_pairs={{0,8},{1,9},{2,10},{3,11},{4,12},{5,13},{6,14},{7,15},{8,0},{9,1},... | collective-permute-start | bytes 479240 | tf_op jit(solution)/shard_map/ppermute | solution.py:1165
  600.2 2.4 collective-permute-start.52
  602.6 7.0 collective-permute-done.50.b
  609.6 9.7 %collective-permute-done.51.c = bf16[1,48,1664]{2,1,0:T(8,128)(2,1)S(1)} collective-permute-done((bf16[1,48,1664]{2,1,0:T(8,128)(2,1)S(1)}, bf16[1,48,1664]{2,1,0:T(8,128)(2,1)S(1)}, u32[]{:S(2)}, u32[]{:S(2)}) %collective-permute-start.51) | collective-permute-done | bytes 159776 | tf_op jit(solution)/shard_map/ppermute | solution.py:1165
  620.6 6.0 collective-permute-start.53
  630.0 3.3 collective-permute-done.53.refs_1_
  634.4 3.9 collective-permute-done.54.refs_2_
  640.4 3.7 copy-done.47
  644.1 11.4 %place.4 = (f32[4,384,2048]{2,1,0:T(8,128)}, f32[4,384,2048]{2,1,0:T(8,128)}, f32[4,1024,768]{2,1,0:T(8,128)}) custom-call(s32[6]{0:T(128)S(1)} %copy-done.38, bf16[8,2,2,6,48,512]{5,4,3,2,1,0:T(8,128)(2,1)S(1)} %bitcast.61, f32[4,384,2048]{2,1,0:T(8,128)} %get-tuple-element.668.refs_1_, ...), custom_call_target="tpu_custom_call", output_to_operand_aliasing={{0}: (2, {}), {1}: (3, {}), {2}: (4, {})} | custom-call | flops 274877906944 | bytes 1 | tf_op jit(solution)/shard_map/place/pallas_call | solution.py:1113
  655.5 2.9 assemble.1.m
  658.5 3.0 collective-permute-done.60.t
  661.4 3.1 attention_unpack.1
  666.2 16.9 %all-gather.9.cloned.1.call-done = bf16[32,3,48,512]{3,2,1,0:T(8,128)(2,1)} async-done(((bf16[2,3,48,512]{3,2,1,0:T(8,128)(2,1)}), bf16[32,3,48,512]{3,2,1,0:T(8,128)(2,1)}) %all-gather.9.cloned.1.call-update) | async-done | bytes 4718608 | tf_op jit(solution)/shard_map/all_gather | solution.py:1270
  685.4 6.4 place.5
  (306 shorter events, 111.9 us)
Async XLA Ops:
  7.2 380.0 %reduce-scatter.2.cloned.1.call-start = ((), (), s32[]{:S(2)}) async-start(), calls=%async_computation.1 | async-start | bytes 2949120 | tf_op jit(solution)/shard_map/reduce_scatter | solution.py:1315
  14.6 22.6 %collective-permute-start.1 = (bf16[3,192,768]{2,1,0:T(8,128)(2,1)S(1)}, bf16[3,192,768]{2,1,0:T(8,128)(2,1)S(1)}, u32[]{:S(2)}, u32[]{:S(2)}) collective-permute-start(bf16[3,192,768]{2,1,0:T(8,128)(2,1)S(1)} %pad_maximum_fusion), channel_id=1, source_target_pairs={{0,1},{1,0},{2,3},{3,2},{4,5},{5,4},{6,7},{7,6},{8,9},{9,8},{10,11... | collective-permute-start | bytes 2654216 | tf_op jit(solution)/shard_map/ppermute | solution.py:1165
  15.9 27.6 %collective-permute-start.3 = (bf16[192,768]{1,0:T(8,128)(2,1)S(1)}, bf16[192,768]{1,0:T(8,128)(2,1)S(1)}, u32[]{:S(2)}, u32[]{:S(2)}) collective-permute-start(bf16[192,768]{1,0:T(8,128)(2,1)S(1)} %constant_dynamic-slice_fusion), channel_id=1, source_target_pairs={{0,1},{1,0},{2,3},{3,2},{4,5},{5,4},{6,7},{7,6},{8,9},{9,8},{10,11... | collective-permute-start | bytes 884744 | tf_op jit(solution)/shard_map/ppermute | solution.py:1165
  21.5 53.3 %collective-permute-start.9 = (bf16[2304,256]{1,0:T(8,128)(2,1)}, bf16[2304,256]{1,0:T(8,128)(2,1)}, u32[]{:S(2)}, u32[]{:S(2)}) collective-permute-start(bf16[2304,256]{1,0:T(8,128)(2,1)} %get-tuple-element.390), channel_id=1, source_target_pairs={{0,1},{1,0},{2,3},{3,2},{4,5},{5,4},{6,7},{7,6},{8,9},{9,8},{10,11... | collective-permute-start | bytes 3538952 | tf_op jit(solution)/shard_map/ppermute | solution.py:1165
  22.8 70.0 %collective-permute-start.7 = (bf16[2304,256]{1,0:T(8,128)(2,1)}, bf16[2304,256]{1,0:T(8,128)(2,1)}, u32[]{:S(2)}, u32[]{:S(2)}) collective-permute-start(bf16[2304,256]{1,0:T(8,128)(2,1)} %get-tuple-element.356), channel_id=1, source_target_pairs={{0,1},{1,0},{2,3},{3,2},{4,5},{5,4},{6,7},{7,6},{8,9},{9,8},{10,11... | collective-permute-start | bytes 3538952 | tf_op jit(solution)/shard_map/ppermute | solution.py:1165
  74.8 44.8 %collective-permute-start.10 = (bf16[2304,256]{1,0:T(8,128)(2,1)}, bf16[2304,256]{1,0:T(8,128)(2,1)}, u32[]{:S(2)}, u32[]{:S(2)}) collective-permute-start(bf16[2304,256]{1,0:T(8,128)(2,1)} %collective-permute-done.9.refs_8_.refs_12_), channel_id=1, source_target_pairs={{0,8},{1,9},{2,10},{3,11},{4,12},{5,13},{6,14},{7,15},{8,0},{9,1},... | collective-permute-start | bytes 3538952 | tf_op jit(solution)/shard_map/ppermute | solution.py:1165
  92.7 28.3 %collective-permute-start.8 = (bf16[2304,256]{1,0:T(8,128)(2,1)}, bf16[2304,256]{1,0:T(8,128)(2,1)}, u32[]{:S(2)}, u32[]{:S(2)}) collective-permute-start(bf16[2304,256]{1,0:T(8,128)(2,1)} %collective-permute-done.7.refs_6_.refs_10_), channel_id=1, source_target_pairs={{0,4},{1,5},{2,6},{3,7},{4,0},{5,1},{6,2},{7,3},{8,12},{9,13},{10,... | collective-permute-start | bytes 3538952 | tf_op jit(solution)/shard_map/ppermute | solution.py:1165
  98.4 28.7 %collective-permute-start.11 = (bf16[2304,256]{1,0:T(8,128)(2,1)}, bf16[2304,256]{1,0:T(8,128)(2,1)}, u32[]{:S(2)}, u32[]{:S(2)}) collective-permute-start(bf16[2304,256]{1,0:T(8,128)(2,1)} %get-tuple-element.376), channel_id=1, source_target_pairs={{0,1},{1,0},{2,3},{3,2},{4,5},{5,4},{6,7},{7,6},{8,9},{9,8},{10,11... | collective-permute-start | bytes 3538952 | tf_op jit(solution)/shard_map/ppermute | solution.py:1165
  99.0 34.4 %collective-permute-start.6 = (bf16[1024,768]{1,0:T(8,128)(2,1)S(1)}, bf16[1024,768]{1,0:T(8,128)(2,1)}, u32[]{:S(2)}, u32[]{:S(2)}) collective-permute-start(bf16[1024,768]{1,0:T(8,128)(2,1)S(1)} %copy-done.11), channel_id=1, source_target_pairs={{0,2},{1,3},{2,0},{3,1},{4,6},{5,7},{6,4},{7,5},{8,10},{9,11},{10,... | collective-permute-start | bytes 4718600 | tf_op jit(solution)/shard_map/ppermute | solution.py:1165
  119.5 92.3 %collective-permute-start.17 = (bf16[2304,256]{1,0:T(8,128)(2,1)}, bf16[2304,256]{1,0:T(8,128)(2,1)}, u32[]{:S(2)}, u32[]{:S(2)}) collective-permute-start(bf16[2304,256]{1,0:T(8,128)(2,1)} %get-tuple-element.423), channel_id=1, source_target_pairs={{0,1},{1,0},{2,3},{3,2},{4,5},{5,4},{6,7},{7,6},{8,9},{9,8},{10,11... | collective-permute-start | bytes 3538952 | tf_op jit(solution)/shard_map/ppermute | solution.py:1165
  131.2 82.0 %collective-permute-start.15 = (bf16[2304,256]{1,0:T(8,128)(2,1)}, bf16[2304,256]{1,0:T(8,128)(2,1)}, u32[]{:S(2)}, u32[]{:S(2)}) collective-permute-start(bf16[2304,256]{1,0:T(8,128)(2,1)} %get-tuple-element.396), channel_id=1, source_target_pairs={{0,1},{1,0},{2,3},{3,2},{4,5},{5,4},{6,7},{7,6},{8,9},{9,8},{10,11... | collective-permute-start | bytes 3538952 | tf_op jit(solution)/shard_map/ppermute | solution.py:1165
  131.3 83.6 %collective-permute-start.16 = (bf16[2304,256]{1,0:T(8,128)(2,1)}, bf16[2304,256]{1,0:T(8,128)(2,1)}, u32[]{:S(2)}, u32[]{:S(2)}) collective-permute-start(bf16[2304,256]{1,0:T(8,128)(2,1)} %get-tuple-element.411), channel_id=1, source_target_pairs={{0,1},{1,0},{2,3},{3,2},{4,5},{5,4},{6,7},{7,6},{8,9},{9,8},{10,11... | collective-permute-start | bytes 3538952 | tf_op jit(solution)/shard_map/ppermute | solution.py:1165
  133.3 81.5 %collective-permute-start.14 = (bf16[2304,256]{1,0:T(8,128)(2,1)}, bf16[2304,256]{1,0:T(8,128)(2,1)}, u32[]{:S(2)}, u32[]{:S(2)}) collective-permute-start(bf16[2304,256]{1,0:T(8,128)(2,1)} %collective-permute-done.11.refs_6_.refs_8_), channel_id=1, source_target_pairs={{0,4},{1,5},{2,6},{3,7},{4,0},{5,1},{6,2},{7,3},{8,12},{9,13},{10,... | collective-permute-start | bytes 3538952 | tf_op jit(solution)/shard_map/ppermute | solution.py:1165
  211.7 47.9 %collective-permute-start.19 = (bf16[6,384,512]{2,1,0:T(8,128)(2,1)}, bf16[6,384,512]{2,1,0:T(8,128)(2,1)}, u32[]{:S(2)}, u32[]{:S(2)}) collective-permute-start(bf16[6,384,512]{2,1,0:T(8,128)(2,1)} %get-tuple-element.428), channel_id=1, source_target_pairs={{0,1},{1,0},{2,3},{3,2},{4,5},{5,4},{6,7},{7,6},{8,9},{9,8},{10,11... | collective-permute-start | bytes 7077896 | tf_op jit(solution)/shard_map/ppermute | solution.py:1165
  211.9 47.9 %collective-permute-start.20 = (bf16[2,6,192,512]{3,2,1,0:T(8,128)(2,1)}, bf16[2,6,192,512]{3,2,1,0:T(8,128)(2,1)}, u32[]{:S(2)}, u32[]{:S(2)}) collective-permute-start(bf16[2,6,192,512]{3,2,1,0:T(8,128)(2,1)} %get-tuple-element.430), channel_id=1, source_target_pairs={{0,4},{1,5},{2,6},{3,7},{4,0},{5,1},{6,2},{7,3},{8,12},{9,13},{10,... | collective-permute-start | bytes 7077896 | tf_op jit(solution)/shard_map/ppermute | solution.py:1165
  213.3 60.5 %collective-permute-start.18 = (bf16[2304,256]{1,0:T(8,128)(2,1)}, bf16[2304,256]{1,0:T(8,128)(2,1)}, u32[]{:S(2)}, u32[]{:S(2)}) collective-permute-start(bf16[2304,256]{1,0:T(8,128)(2,1)} %collective-permute-done.17.refs_6_.refs_8_), channel_id=1, source_target_pairs={{0,8},{1,9},{2,10},{3,11},{4,12},{5,13},{6,14},{7,15},{8,0},{9,1},... | collective-permute-start | bytes 3538952 | tf_op jit(solution)/shard_map/ppermute | solution.py:1165
  269.6 54.7 %collective-permute-start.24 = (bf16[6,192,512]{2,1,0:T(8,128)(2,1)}, bf16[6,192,512]{2,1,0:T(8,128)(2,1)}, u32[]{:S(2)}, u32[]{:S(2)}) collective-permute-start(bf16[6,192,512]{2,1,0:T(8,128)(2,1)} %get-tuple-element.437), channel_id=1, source_target_pairs={{0,4},{1,5},{2,6},{3,7},{4,0},{5,1},{6,2},{7,3},{8,12},{9,13},{10,... | collective-permute-start | bytes 3538952 | tf_op jit(solution)/shard_map/ppermute | solution.py:1165
  273.7 50.5 %collective-permute-start.25 = (bf16[6,192,512]{2,1,0:T(8,128)(2,1)}, bf16[6,192,512]{2,1,0:T(8,128)(2,1)}, u32[]{:S(2)}, u32[]{:S(2)}) collective-permute-start(bf16[6,192,512]{2,1,0:T(8,128)(2,1)} %get-tuple-element.462), channel_id=1, source_target_pairs={{0,1},{1,0},{2,3},{3,2},{4,5},{5,4},{6,7},{7,6},{8,9},{9,8},{10,11... | collective-permute-start | bytes 3538952 | tf_op jit(solution)/shard_map/ppermute | solution.py:1165
  275.5 54.4 %collective-permute-start.23 = (bf16[2,3,192,512]{3,2,1,0:T(8,128)(2,1)}, bf16[2,3,192,512]{3,2,1,0:T(8,128)(2,1)}, u32[]{:S(2)}, u32[]{:S(2)}) collective-permute-start(bf16[2,3,192,512]{3,2,1,0:T(8,128)(2,1)} %get-tuple-element.459), channel_id=1, source_target_pairs={{0,4},{1,5},{2,6},{3,7},{4,0},{5,1},{6,2},{7,3},{8,12},{9,13},{10,... | collective-permute-start | bytes 3538952 | tf_op jit(solution)/shard_map/ppermute | solution.py:1165
  276.0 53.9 %collective-permute-start.22 = (bf16[3,384,512]{2,1,0:T(8,128)(2,1)}, bf16[3,384,512]{2,1,0:T(8,128)(2,1)}, u32[]{:S(2)}, u32[]{:S(2)}) collective-permute-start(bf16[3,384,512]{2,1,0:T(8,128)(2,1)} %get-tuple-element.455), channel_id=1, source_target_pairs={{0,1},{1,0},{2,3},{3,2},{4,5},{5,4},{6,7},{7,6},{8,9},{9,8},{10,11... | collective-permute-start | bytes 3538952 | tf_op jit(solution)/shard_map/ppermute | solution.py:1165
  320.5 75.2 %collective-permute-start.26 = (bf16[2,1024,768]{2,1,0:T(8,128)(2,1)}, bf16[2,1024,768]{2,1,0:T(8,128)(2,1)}, u32[]{:S(2)}, u32[]{:S(2)}) collective-permute-start(bf16[2,1024,768]{2,1,0:T(8,128)(2,1)} %add_convert_fusion), channel_id=1, source_target_pairs={{0,2},{1,3},{2,0},{3,1},{4,6},{5,7},{6,4},{7,5},{8,10},{9,11},{10,... | collective-permute-start | bytes 9437192 | tf_op jit(solution)/shard_map/ppermute | solution.py:1165
  329.8 184.7 %all-gather.5.cloned.1.call-start = ((), (), s32[]{:S(2)}) async-start(), calls=%async_computation.2 | async-start | bytes 10027008 | tf_op jit(solution)/shard_map/all_gather | solution.py:1270
  336.2 70.1 %collective-permute-start.30 = (bf16[3,192,512]{2,1,0:T(8,128)(2,1)}, bf16[3,192,512]{2,1,0:T(8,128)(2,1)}, u32[]{:S(2)}, u32[]{:S(2)}) collective-permute-start(bf16[3,192,512]{2,1,0:T(8,128)(2,1)} %get-tuple-element.473), channel_id=1, source_target_pairs={{0,4},{1,5},{2,6},{3,7},{4,0},{5,1},{6,2},{7,3},{8,12},{9,13},{10,... | collective-permute-start | bytes 1769480 | tf_op jit(solution)/shard_map/ppermute | solution.py:1165
  337.7 49.1 %collective-permute-start.29 = (bf16[2,3,192,512]{3,2,1,0:T(8,128)(2,1)}, bf16[2,3,192,512]{3,2,1,0:T(8,128)(2,1)}, u32[]{:S(2)}, u32[]{:S(2)}) collective-permute-start(bf16[2,3,192,512]{3,2,1,0:T(8,128)(2,1)} %get-tuple-element.494), channel_id=1, source_target_pairs={{0,4},{1,5},{2,6},{3,7},{4,0},{5,1},{6,2},{7,3},{8,12},{9,13},{10,... | collective-permute-start | bytes 3538952 | tf_op jit(solution)/shard_map/ppermute | solution.py:1165
  338.2 49.0 %collective-permute-start.28 = (bf16[3,384,512]{2,1,0:T(8,128)(2,1)}, bf16[3,384,512]{2,1,0:T(8,128)(2,1)}, u32[]{:S(2)}, u32[]{:S(2)}) collective-permute-start(bf16[3,384,512]{2,1,0:T(8,128)(2,1)} %get-tuple-element.490), channel_id=1, source_target_pairs={{0,1},{1,0},{2,3},{3,2},{4,5},{5,4},{6,7},{7,6},{8,9},{9,8},{10,11... | collective-permute-start | bytes 3538952 | tf_op jit(solution)/shard_map/ppermute | solution.py:1165
  386.9 19.4 %collective-permute-start.31 = (bf16[3,192,512]{2,1,0:T(8,128)(2,1)}, bf16[3,192,512]{2,1,0:T(8,128)(2,1)S(1)}, u32[]{:S(2)}, u32[]{:S(2)}) collective-permute-start(bf16[3,192,512]{2,1,0:T(8,128)(2,1)} %copy-done.53), channel_id=1, source_target_pairs={{0,1},{1,0},{2,3},{3,2},{4,5},{5,4},{6,7},{7,6},{8,9},{9,8},{10,11... | collective-permute-start | bytes 1769480 | tf_op jit(solution)/shard_map/ppermute | solution.py:1165
  387.3 242.7 %all-gather.7.cloned.1.call-start = ((), (), s32[]{:S(2)}) async-start(), calls=%async_computation.3 | async-start | bytes 10027008 | tf_op jit(solution)/shard_map/all_gather | solution.py:1270
  394.2 58.2 %collective-permute-start.32 = (bf16[3,192,512]{2,1,0:T(8,128)(2,1)S(1)}, bf16[3,192,512]{2,1,0:T(8,128)(2,1)S(1)}, u32[]{:S(2)}, u32[]{:S(2)}) collective-permute-start(bf16[3,192,512]{2,1,0:T(8,128)(2,1)S(1)} %get-tuple-element.500), channel_id=1, source_target_pairs={{0,4},{1,5},{2,6},{3,7},{4,0},{5,1},{6,2},{7,3},{8,12},{9,13},{10,... | collective-permute-start | bytes 1769480 | tf_op jit(solution)/shard_map/ppermute | solution.py:1165
  395.8 56.6 %collective-permute-start.33 = (bf16[3,192,512]{2,1,0:T(8,128)(2,1)S(1)}, bf16[3,192,512]{2,1,0:T(8,128)(2,1)S(1)}, u32[]{:S(2)}, u32[]{:S(2)}) collective-permute-start(bf16[3,192,512]{2,1,0:T(8,128)(2,1)S(1)} %get-tuple-element.548), channel_id=1, source_target_pairs={{0,1},{1,0},{2,3},{3,2},{4,5},{5,4},{6,7},{7,6},{8,9},{9,8},{10,11... | collective-permute-start | bytes 1769480 | tf_op jit(solution)/shard_map/ppermute | solution.py:1165
  409.0 42.6 %collective-permute-start.34 = (bf16[2,3,48,512]{3,2,1,0:T(8,128)(2,1)S(1)}, bf16[2,3,48,512]{3,2,1,0:T(8,128)(2,1)S(1)}, u32[]{:S(2)}, u32[]{:S(2)}) collective-permute-start(bf16[2,3,48,512]{3,2,1,0:T(8,128)(2,1)S(1)} %get-tuple-element.549), channel_id=1, source_target_pairs={{0,8},{1,9},{2,10},{3,11},{4,12},{5,13},{6,14},{7,15},{8,0},{9,1},... | collective-permute-start | bytes 884744 | tf_op jit(solution)/shard_map/ppermute | solution.py:1165
  410.7 40.9 %collective-permute-start.35 = (bf16[2,3,48,512]{3,2,1,0:T(8,128)(2,1)S(1)}, bf16[2,3,48,512]{3,2,1,0:T(8,128)(2,1)S(1)}, u32[]{:S(2)}, u32[]{:S(2)}) collective-permute-start(bf16[2,3,48,512]{3,2,1,0:T(8,128)(2,1)S(1)} %get-tuple-element.550), channel_id=1, source_target_pairs={{0,16},{1,17},{2,18},{3,19},{4,20},{5,21},{6,22},{7,23},{8,24},{9,... | collective-permute-start | bytes 884744 | tf_op jit(solution)/shard_map/ppermute | solution.py:1165
  413.3 38.3 %collective-permute-start.36 = (bf16[2,3,48,512]{3,2,1,0:T(8,128)(2,1)S(1)}, bf16[2,3,48,512]{3,2,1,0:T(8,128)(2,1)S(1)}, u32[]{:S(2)}, u32[]{:S(2)}) collective-permute-start(bf16[2,3,48,512]{3,2,1,0:T(8,128)(2,1)S(1)} %get-tuple-element.551), channel_id=1, source_target_pairs={{0,24},{1,25},{2,26},{3,27},{4,28},{5,29},{6,30},{7,31},{8,16},{9,... | collective-permute-start | bytes 884744 | tf_op jit(solution)/shard_map/ppermute | solution.py:1165
  454.0 38.0 %collective-permute-start.40 = (bf16[2,3,48,512]{3,2,1,0:T(8,128)(2,1)}, bf16[2,3,48,512]{3,2,1,0:T(8,128)(2,1)S(1)}, u32[]{:S(2)}, u32[]{:S(2)}) collective-permute-start(bf16[2,3,48,512]{3,2,1,0:T(8,128)(2,1)} %get-tuple-element.610), channel_id=1, source_target_pairs={{0,8},{1,9},{2,10},{3,11},{4,12},{5,13},{6,14},{7,15},{8,0},{9,1},... | collective-permute-start | bytes 884744 | tf_op jit(solution)/shard_map/ppermute | solution.py:1165
  455.5 36.5 %collective-permute-start.41 = (bf16[2,3,48,512]{3,2,1,0:T(8,128)(2,1)}, bf16[2,3,48,512]{3,2,1,0:T(8,128)(2,1)S(1)}, u32[]{:S(2)}, u32[]{:S(2)}) collective-permute-start(bf16[2,3,48,512]{3,2,1,0:T(8,128)(2,1)} %get-tuple-element.611), channel_id=1, source_target_pairs={{0,16},{1,17},{2,18},{3,19},{4,20},{5,21},{6,22},{7,23},{8,24},{9,... | collective-permute-start | bytes 884744 | tf_op jit(solution)/shard_map/ppermute | solution.py:1165
  458.3 38.6 %collective-permute-start.42 = (bf16[2,3,48,512]{3,2,1,0:T(8,128)(2,1)}, bf16[2,3,48,512]{3,2,1,0:T(8,128)(2,1)}, u32[]{:S(2)}, u32[]{:S(2)}) collective-permute-start(bf16[2,3,48,512]{3,2,1,0:T(8,128)(2,1)} %get-tuple-element.612), channel_id=1, source_target_pairs={{0,24},{1,25},{2,26},{3,27},{4,28},{5,29},{6,30},{7,31},{8,16},{9,... | collective-permute-start | bytes 884744 | tf_op jit(solution)/shard_map/ppermute | solution.py:1165
  458.4 41.0 %collective-permute-start.39 = (bf16[2,3,192,512]{3,2,1,0:T(8,128)(2,1)}, bf16[2,3,192,512]{3,2,1,0:T(8,128)(2,1)}, u32[]{:S(2)}, u32[]{:S(2)}) collective-permute-start(bf16[2,3,192,512]{3,2,1,0:T(8,128)(2,1)} %get-tuple-element.609), channel_id=1, source_target_pairs={{0,4},{1,5},{2,6},{3,7},{4,0},{5,1},{6,2},{7,3},{8,12},{9,13},{10,... | collective-permute-start | bytes 3538952 | tf_op jit(solution)/shard_map/ppermute | solution.py:1165
  459.1 40.3 %collective-permute-start.38 = (bf16[3,384,512]{2,1,0:T(8,128)(2,1)}, bf16[3,384,512]{2,1,0:T(8,128)(2,1)}, u32[]{:S(2)}, u32[]{:S(2)}) collective-permute-start(bf16[3,384,512]{2,1,0:T(8,128)(2,1)} %get-tuple-element.605), channel_id=1, source_target_pairs={{0,1},{1,0},{2,3},{3,2},{4,5},{5,4},{6,7},{7,6},{8,9},{9,8},{10,11... | collective-permute-start | bytes 3538952 | tf_op jit(solution)/shard_map/ppermute | solution.py:1165
  499.4 183.7 %all-gather.9.cloned.1.call-start = ((), (), s32[]{:S(2)}) async-start(), calls=%async_computation.4 | async-start | bytes 5013504 | tf_op jit(solution)/shard_map/all_gather | solution.py:1270
  507.1 22.5 %collective-permute-start.44 = (bf16[3,192,512]{2,1,0:T(8,128)(2,1)}, bf16[3,192,512]{2,1,0:T(8,128)(2,1)}, u32[]{:S(2)}, u32[]{:S(2)}) collective-permute-start(bf16[3,192,512]{2,1,0:T(8,128)(2,1)} %get-tuple-element.623), channel_id=1, source_target_pairs={{0,4},{1,5},{2,6},{3,7},{4,0},{5,1},{6,2},{7,3},{8,12},{9,13},{10,... | collective-permute-start | bytes 1769480 | tf_op jit(solution)/shard_map/ppermute | solution.py:1165
  507.7 21.9 %collective-permute-start.45 = (bf16[3,192,512]{2,1,0:T(8,128)(2,1)}, bf16[3,192,512]{2,1,0:T(8,128)(2,1)}, u32[]{:S(2)}, u32[]{:S(2)}) collective-permute-start(bf16[3,192,512]{2,1,0:T(8,128)(2,1)} %get-tuple-element.631), channel_id=1, source_target_pairs={{0,1},{1,0},{2,3},{3,2},{4,5},{5,4},{6,7},{7,6},{8,9},{9,8},{10,11... | collective-permute-start | bytes 1769480 | tf_op jit(solution)/shard_map/ppermute | solution.py:1165
  512.7 36.3 %collective-permute-start.43 = (bf16[1,384,1664]{2,1,0:T(8,128)(2,1)}, bf16[1,384,1664]{2,1,0:T(8,128)(2,1)}, u32[]{:S(2)}, u32[]{:S(2)}) collective-permute-start(bf16[1,384,1664]{2,1,0:T(8,128)(2,1)} %get-tuple-element.628), channel_id=1, source_target_pairs={{0,1},{1,0},{2,3},{3,2},{4,5},{5,4},{6,7},{7,6},{8,9},{9,8},{10,11... | collective-permute-start | bytes 3833864 | tf_op jit(solution)/shard_map/ppermute | solution.py:1165
  531.9 29.7 %collective-permute-start.47 = (bf16[2,3,48,512]{3,2,1,0:T(8,128)(2,1)S(1)}, bf16[2,3,48,512]{3,2,1,0:T(8,128)(2,1)S(1)}, u32[]{:S(2)}, u32[]{:S(2)}) collective-permute-start(bf16[2,3,48,512]{3,2,1,0:T(8,128)(2,1)S(1)} %get-tuple-element.645), channel_id=1, source_target_pairs={{0,8},{1,9},{2,10},{3,11},{4,12},{5,13},{6,14},{7,15},{8,0},{9,1},... | collective-permute-start | bytes 884744 | tf_op jit(solution)/shard_map/ppermute | solution.py:1165
  546.6 34.6 %collective-permute-start.48 = (bf16[2,3,48,512]{3,2,1,0:T(8,128)(2,1)S(1)}, bf16[2,3,48,512]{3,2,1,0:T(8,128)(2,1)S(1)}, u32[]{:S(2)}, u32[]{:S(2)}) collective-permute-start(bf16[2,3,48,512]{3,2,1,0:T(8,128)(2,1)S(1)} %get-tuple-element.646), channel_id=1, source_target_pairs={{0,16},{1,17},{2,18},{3,19},{4,20},{5,21},{6,22},{7,23},{8,24},{9,... | collective-permute-start | bytes 884744 | tf_op jit(solution)/shard_map/ppermute | solution.py:1165
  546.9 34.3 %collective-permute-start.49 = (bf16[2,3,48,512]{3,2,1,0:T(8,128)(2,1)S(1)}, bf16[2,3,48,512]{3,2,1,0:T(8,128)(2,1)S(1)}, u32[]{:S(2)}, u32[]{:S(2)}) collective-permute-start(bf16[2,3,48,512]{3,2,1,0:T(8,128)(2,1)S(1)} %get-tuple-element.647), channel_id=1, source_target_pairs={{0,24},{1,25},{2,26},{3,27},{4,28},{5,29},{6,30},{7,31},{8,16},{9,... | collective-permute-start | bytes 884744 | tf_op jit(solution)/shard_map/ppermute | solution.py:1165
  551.2 31.4 %collective-permute-start.46 = (bf16[1,192,1664]{2,1,0:T(8,128)(2,1)S(1)}, bf16[1,192,1664]{2,1,0:T(8,128)(2,1)S(1)}, u32[]{:S(2)}, u32[]{:S(2)}) collective-permute-start(bf16[1,192,1664]{2,1,0:T(8,128)(2,1)S(1)} %get-tuple-element.644), channel_id=1, source_target_pairs={{0,4},{1,5},{2,6},{3,7},{4,0},{5,1},{6,2},{7,3},{8,12},{9,13},{10,... | collective-permute-start | bytes 1916936 | tf_op jit(solution)/shard_map/ppermute | solution.py:1165
  583.3 26.3 %collective-permute-start.50 = (bf16[1,48,1664]{2,1,0:T(8,128)(2,1)S(1)}, bf16[1,48,1664]{2,1,0:T(8,128)(2,1)S(1)}, u32[]{:S(2)}, u32[]{:S(2)}) collective-permute-start(bf16[1,48,1664]{2,1,0:T(8,128)(2,1)S(1)} %get-tuple-element.657), channel_id=1, source_target_pairs={{0,8},{1,9},{2,10},{3,11},{4,12},{5,13},{6,14},{7,15},{8,0},{9,1},... | collective-permute-start | bytes 479240 | tf_op jit(solution)/shard_map/ppermute | solution.py:1165
  629.0 26.5 %collective-permute-start.56 = (bf16[1,48,1664]{2,1,0:T(8,128)(2,1)}, bf16[1,48,1664]{2,1,0:T(8,128)(2,1)}, u32[]{:S(2)}, u32[]{:S(2)}) collective-permute-start(bf16[1,48,1664]{2,1,0:T(8,128)(2,1)} %sum_z.1.refs_0_), channel_id=1, source_target_pairs={{0,4},{1,5},{2,6},{3,7},{4,0},{5,1},{6,2},{7,3},{8,12},{9,13},{10,... | collective-permute-start | bytes 479240 | tf_op jit(solution)/shard_map/ppermute | solution.py:1165
  633.2 22.2 %collective-permute-start.57 = (bf16[1,48,1664]{2,1,0:T(8,128)(2,1)}, bf16[1,48,1664]{2,1,0:T(8,128)(2,1)}, u32[]{:S(2)}, u32[]{:S(2)}) collective-permute-start(bf16[1,48,1664]{2,1,0:T(8,128)(2,1)} %collective-permute-done.53.refs_1_), channel_id=1, source_target_pairs={{0,4},{1,5},{2,6},{3,7},{4,0},{5,1},{6,2},{7,3},{8,12},{9,13},{10,... | collective-permute-start | bytes 479240 | tf_op jit(solution)/shard_map/ppermute | solution.py:1165
  (85 other events, 928.9 us)
Sparse Core Ops, SparseCore 0:
  329.9 49.4 reduce-scatter.1
  387.4 125.8 all-gather.4
  516.1 110.5 all-gather.6
  629.4 53.5 all-gather.8
